TPU v7x, 32 devices: a whole 2x2x4 slice. The times are simulated.
32 devices in a mesh: model: 4 (over z), dp: 8 (over y, x, core).
Axes of the slice: x: 2, y: 2, z: 4, core: 2. Of those that a mesh axis runs over, the one named last changes fastest.
Arguments:
- weight: float32 [16, 768, 3072], P(None, 'dp', 'model')
- grad_parts: float32 [16, 6144, 3072], P(None, 'dp', 'model')
- row_stat: float32 [16, 768], P(None, 'dp')
- col_stat: float32 [16, 3072], P(None, 'model')
- norm_scale: float32 [16, 768], P(None, 'dp')
- norm_grads: float32 [16, 6144], P(None, 'dp')
- norm_stat: float32 [16, 768], P(None, 'dp')
- learn_rate: float32 [], replicated
Outputs:
- output 1: float32 [16, 768, 3072], P(None, 'dp', 'model')
- output 2: float32 [16, 768], P(None, 'dp')
- output 3: float32 [16, 3072], P(None, 'model')
- output 4: float32 [16, 768], P(None, 'dp')
- output 5: float32 [16, 768], P(None, 'dp')
All inputs are finite; a program needn't handle non-finite values.
Results may differ from a plain program's by a relative error of at most 0.001.
Values sent between devices are 32-bit elements.
A program may use at most 1 GiB of HBM per device.

v0:
```python
import jax
import jax.numpy as jnp
from jax import lax
from jax.sharding import PartitionSpec as P

STEP_COUNT = 4
DECAY_POWER = 0.8
EPS_FLOOR = 1e-30
SCALE_FLOOR = 1e-3
CLIP_LIMIT = 1.0


def solution(mesh):
    replicas = mesh.shape['dp']
    shards = mesh.shape['model']
    decay_rate = 1.0 - STEP_COUNT ** -DECAY_POWER

    def local_step(weight, grad_parts, row_stat, col_stat, norm_scale, norm_grads, norm_stat, learn_rate):
        rows_local = weight.shape[1]
        cols_local = weight.shape[2]
        rows_total = rows_local * replicas
        cols_total = cols_local * shards
        grad_block = lax.psum_scatter(grad_parts, 'dp', scatter_dimension=1, tiled=True)
        norm_grad = lax.psum_scatter(norm_grads, 'dp', scatter_dimension=1, tiled=True)
        grad_sq = grad_block * grad_block + EPS_FLOOR
        row_sums = lax.psum(jnp.sum(grad_sq, axis=2), 'model')
        col_sums = lax.psum(jnp.sum(grad_sq, axis=1), 'dp')
        row_new = decay_rate * row_stat + (1.0 - decay_rate) * (row_sums / cols_total)
        col_new = decay_rate * col_stat + (1.0 - decay_rate) * (col_sums / rows_total)
        row_mean = lax.psum(jnp.sum(row_new, axis=1, keepdims=True), 'dp') / rows_total
        update = grad_block * lax.rsqrt(row_new / row_mean)[:, :, None] * lax.rsqrt(col_new)[:, None, :]
        upd_sq = lax.psum(jnp.sum(update * update, axis=(1, 2)), ('model', 'dp'))
        upd_rms = jnp.sqrt(upd_sq / (rows_total * cols_total))[:, None, None]
        update = update / jnp.maximum(1.0, upd_rms / CLIP_LIMIT)
        weight_sq = lax.psum(jnp.sum(weight * weight, axis=(1, 2)), ('model', 'dp'))
        weight_rms = jnp.sqrt(weight_sq / (rows_total * cols_total))[:, None, None]
        weight_new = weight - learn_rate * jnp.maximum(SCALE_FLOOR, weight_rms) * update
        norm_stat_new = decay_rate * norm_stat + (1.0 - decay_rate) * (norm_grad * norm_grad + EPS_FLOOR)
        norm_update = norm_grad * lax.rsqrt(norm_stat_new)
        norm_upd_sq = lax.psum(jnp.sum(norm_update * norm_update, axis=1, keepdims=True), 'dp')
        norm_update = norm_update / jnp.maximum(1.0, jnp.sqrt(norm_upd_sq / rows_total) / CLIP_LIMIT)
        scale_sq = lax.psum(jnp.sum(norm_scale * norm_scale, axis=1, keepdims=True), 'dp')
        scale_rms = jnp.sqrt(scale_sq / rows_total)
        norm_new = norm_scale - learn_rate * jnp.maximum(SCALE_FLOOR, scale_rms) * norm_update
        return weight_new, row_new, col_new, norm_new, norm_stat_new

    mat_spec = P(None, 'dp', 'model')
    row_spec = P(None, 'dp')
    col_spec = P(None, 'model')
    return jax.shard_map(local_step, mesh=mesh, in_specs=(mat_spec, mat_spec, row_spec, col_spec, row_spec, row_spec, row_spec, P()), out_specs=(mat_spec, row_spec, col_spec, row_spec, row_spec), check_vma=False)
```

profile of v0, /device:TPU:0, one launch (start us, length us, event | category | flops | bytes accessed | tf_op | source)
XLA Modules:
  0.0 369.0 jit_solution(3212700236783009764)
XLA Ops:
  7.2 0.0 reduce-scatter.7.cloned.1.call-start
  7.2 1.7 copy.13
  8.9 0.0 reduce-scatter.7.cloned.1.call-update
  8.9 0.0 copy-start.3
  9.0 0.0 reduce-scatter.5.cloned.1.call-start
  9.0 0.7 reduce-scatter.5.cloned.1.call-update
  9.7 0.0 copy-done.3
  9.7 0.0 copy-start.4
  9.7 0.1 multiply_reduce_fusion.3
  9.9 0.0 copy-start.5
  9.9 0.0 copy-start
  9.9 2.8 multiply_reduce_fusion.1
  12.7 35.5 %reduce-scatter.7.cloned.1.call-done = f32[96,16]{1,0:T(8,128)} async-done(((f32[768,16]{1,0:T(8,128)}), f32[96,16]{1,0:T(8,128)}) %reduce-scatter.7.cloned.1.call-update) | async-done | bytes 6160
  48.2 0.9 copy.14
  49.1 0.0 copy-done.4
  49.1 0.1 multiply_reduce_fusion.2
  49.2 0.0 copy-start.2
  49.2 227.3 %reduce-scatter.5.cloned.1.call-done = f32[16,96,768]{2,1,0:T(8,128)} async-done(((f32[16,768,768]{2,1,0:T(8,128)}), f32[16,96,768]{2,1,0:T(8,128)}) %reduce-scatter.5.cloned.1.call-update) | async-done | bytes 4718608 | tf_op jit(solution)/shard_map/reduce_scatter | solution.py:23
  276.5 3.1 fusion.1
  279.6 11.8 %psum.50 = f32[16,96]{1,0:T(8,128)S(1)} all-reduce(f32[16,96]{1,0:T(8,128)S(1)} %get-tuple-element.5), channel_id=1, replica_groups=mesh['model'=4,'dp'=8] {'model'}, use_global_device_ids=true, to_apply=%region_4.0 | all-reduce | flops 1536 | bytes 12288 | tf_op jit(solution)/shard_map/psum | solution.py:26
  291.5 0.0 copy-done.5
  291.5 0.1 fusion.3
  291.6 22.7 %all-reduce.1 = (f32[16,768]{1,0:T(8,128)S(1)}, f32[16,1]{0,1:T(1,128)S(1)}, f32[16,1]{0,1:T(1,128)S(1)}, f32[16,1]{0,1:T(1,128)S(1)}) all-reduce(f32[16,768]{1,0:T(8,128)S(1)} %get-tuple-element.6, f32[16,1]{0,1:T(1,128)S(1)} %bitcast.15, f32[16,1]{0,1:T(1,128)S(1)} %bitcast.14, ...), channel_id=1, replica_groups=mesh['model'=4,'dp'=8] {'dp'}, use_global_device_ids=true, to_apply=%region_8.0 | all-reduce | flops 12336 | bytes 98688 | tf_op jit(solution)/shard_map/psum | solution.py:27
  314.3 0.1 divide_rsqrt_fusion
  314.4 0.0 copy-done
  314.4 0.6 fusion.2
  315.1 3.2 multiply_reduce_fusion
  318.9 36.9 %all-reduce = (f32[16]{0:T(128)S(1)}, f32[16]{0:T(128)S(1)}) all-reduce(f32[16]{0:T(128)S(1)} %multiply_reduce_fusion, f32[16]{0:T(128)S(1)} %multiply_reduce_fusion.1), channel_id=1, replica_groups=mesh['model'=4,'dp'=8] {'model','dp'}, use_global_device_ids=true, to_apply=%region_10.0 | all-reduce | flops 32 | bytes 256 | tf_op jit(solution)/shard_map/psum | solution.py:32
  355.8 0.0 copy-done.2
  355.8 0.7 multiply_subtract_fusion.1
  356.5 5.7 %multiply_subtract_fusion = f32[16,96,768]{2,1,0:T(8,128)} fusion(f32[16,96,768]{2,1,0:T(8,128)} %param.8, f32[16,96,768]{2,1,0:T(8,128)} %reduce-scatter.5.cloned.1.call-done, f32[16]{0:T(128)S(1)} %get-tuple-element.21, f32[16,768]{1,0:T(8,128)S(1)} %get-tuple-element.13, f32[16,96]{1,0:T(8,128)S(1)} %divide_rsqrt_fusion, f32[16]{0:T(128)S(1)} %get-tuple-element.22), kind=kLoop, calls=%fused_computation | loop fusion | flops 5898240 | bytes 14211200 | tf_op jit(solution)/shard_map/sub | solution.py:37
  362.2 0.0 copy-done.1
  (4 shorter events, 0.0 us)
Async XLA Ops:
  7.2 41.1 %reduce-scatter.7.cloned.1.call-start = ((), (), s32[]{:S(2)}) async-start(), calls=%async_computation.3 | async-start | bytes 442368
  8.9 0.8 copy-start.3
  9.0 267.5 %reduce-scatter.5.cloned.1.call-start = ((), (), s32[]{:S(2)}) async-start(), calls=%async_computation.2 | async-start | bytes 42467328 | tf_op jit(solution)/shard_map/reduce_scatter | solution.py:23
  9.7 39.3 %copy-start.4 = (f32[16,96]{1,0:T(8,128)S(1)}, f32[16,96]{1,0:T(8,128)}, u32[]{:S(2)}) copy-start(f32[16,96]{1,0:T(8,128)} %param.14) | copy-start | bytes 18436
  9.9 281.6 %copy-start.5 = (f32[16,96]{1,0:T(8,128)S(1)}, f32[16,96]{1,0:T(8,128)}, u32[]{:S(2)}) copy-start(f32[16,96]{1,0:T(8,128)} %param.10) | copy-start | bytes 18436
  9.9 304.6 %copy-start = (f32[16,768]{1,0:T(8,128)S(1)}, f32[16,768]{1,0:T(8,128)}, u32[]{:S(2)}) copy-start(f32[16,768]{1,0:T(8,128)} %param.11) | copy-start | bytes 147460
  49.2 306.6 %copy-start.2 = (f32[16,96]{1,0:T(8,128)}, f32[16,96]{1,0:T(8,128)S(1)}, u32[]{:S(2)}) copy-start(f32[16,96]{1,0:T(8,128)S(1)} %get-tuple-element.16) | copy-start | bytes 18436
  291.6 70.6 %copy-start.1 = (f32[16,96]{1,0:T(8,128)}, f32[16,96]{1,0:T(8,128)S(1)}, u32[]{:S(2)}) copy-start(f32[16,96]{1,0:T(8,128)S(1)} %get-tuple-element.18) | copy-start | bytes 18436
Sparse Core Ops, SparseCore 0:
  11.6 36.5 reduce-scatter.6
  51.8 224.6 reduce-scatter.4
where the time goes:
time: 370 us; the launch traced here: 369 us
  waiting for transfers between devices  264 us (71%)
  blocking collectives  71.4 us (19%)
  other arithmetic  16.6 us (4%)
  between operations  14.8 us (4%)
    reduce_scatter x1, waiting for transfers between devices, local_step(): lax.psum_scatter(grad_parts, 'dp', scatter_dimension=1, tiled=True)  227 us
    psum x1, blocking collectives, local_step(): upd_sq = lax.psum(jnp.sum(update * update, axis=(1, 2)), ('model', 'dp'))  36.9 us
    unnamed x3, waiting for transfers between devices  36.2 us
    psum x1, blocking collectives, local_step(): col_sums = lax.psum(jnp.sum(grad_sq, axis=1), 'dp')  22.7 us
    psum x1, blocking collectives, local_step(): row_sums = lax.psum(jnp.sum(grad_sq, axis=2), 'model')  11.8 us
  transfers between devices with their start and end apart: 2, of which 2 were waited for; matrix products, arithmetic and copies ran while one was open for 1% of the time, Pallas kernels for 0%

commit v1 on v0

v1 whole, which is shorter than its diff:
```python
import functools

import jax
import jax.numpy as jnp
from jax import lax
from jax.experimental import pallas as pl
from jax.experimental.pallas import tpu as pltpu
from jax.sharding import PartitionSpec as P

STEP_COUNT = 4
DECAY_POWER = 0.8
EPS_FLOOR = 1e-30
SCALE_FLOOR = 1e-3
CLIP_LIMIT = 1.0
DECAY = 1.0 - STEP_COUNT ** -DECAY_POWER
MESH = pl.DeviceIdType.MESH
LANES = 128
AHEAD = 2


def step_kernel(w_hbm, g_hbm, r_hbm, c_hbm, n_hbm, ng_hbm, v_hbm, lr_ref,
                wo_hbm, ro_hbm, co_hbm, no_hbm, vo_hbm,
                own, peer, in1x, in1y, in2, w_buf,
                r_buf, c_buf, n_buf, ng_buf, v_buf, r_pad,
                r_all, c_all, s_all, t_all, h_all, h_out, k_all,
                load_sem, pair_send, pair_recv,
                x1_send, x1_recv, y1_send, y1_recv, x2_send, x2_recv, y2_send, y2_recv,
                r_send, r_recv, c_send, c_recv, s_send, s_recv, t_send, t_recv,
                w_in_sem, w_out_sem, small_sem, out_sem, h_send, h_recv, k_send, k_recv):
    layers, _, rows, cols = own.shape
    half = rows // 2
    zs, ds = r_all.shape[1], c_all.shape[1]
    rows_total, cols_total = rows * ds, cols * zs
    z = lax.axis_index('model')
    d = lax.axis_index('dp')
    core = d % 2
    dx = d + 2 - 4 * ((d // 2) % 2)
    dy = d + 4 - 8 * (d // 4)
    dxy = dx + dy - d
    dc = d + 1 - 2 * core
    blocks = (dx, dxy, dy, d)

    def remote(src, dst, send, recv, **where):
        return pltpu.make_async_remote_copy(src_ref=src, dst_ref=dst, send_sem=send, recv_sem=recv,
                                            device_id=where, device_id_type=MESH)

    def drain(ref, sem):
        pltpu.make_async_copy(ref, ref, sem).wait()

    def load_own(l):
        for k in range(4):
            pltpu.make_async_copy(g_hbm.at[l, blocks[k]], own.at[l, k], load_sem.at[l]).start()

    def send_pair(l):
        for k in range(4):
            remote(g_hbm.at[l, blocks[k] + dc - d], peer.at[l, k], pair_send.at[l], pair_recv.at[l], dp=dc).start()

    def x1(l):
        return remote(own.at[l, 0:2, 0:half], in1x.at[l], x1_send.at[l], x1_recv.at[l], dp=dx)

    def y1(l):
        return remote(own.at[l, 1:3, half:rows], in1y.at[l], y1_send.at[l], y1_recv.at[l], dp=dy)

    def y2(l):
        return remote(own.at[l, 2, 0:half], in2.at[l, 0], y2_send.at[l], y2_recv.at[l], dp=dy)

    def x2(l):
        return remote(own.at[l, 0, half:rows], in2.at[l, 1], x2_send.at[l], x2_recv.at[l], dp=dx)

    def spread_z(buf, l, send, recv):
        for j in range(1, zs):
            remote(buf.at[l, z], buf.at[l, z], send.at[l], recv.at[l], model=(z + j) % zs).start()

    def spread_d(buf, l, send, recv):
        for j in range(1, ds):
            remote(buf.at[l, d], buf.at[l, d], send.at[l], recv.at[l], dp=(d + j) % ds).start()

    def total(buf, l):
        acc = buf[l, 0]
        for j in range(1, buf.shape[1]):
            acc = acc + buf[l, j]
        return acc

    def column(row):
        return jnp.transpose(jnp.broadcast_to(row, (LANES, LANES)))[0:rows]

    def fold(values):
        acc = values[:, 0:LANES]
        for t in range(1, cols // LANES):
            acc = acc + values[:, t * LANES:(t + 1) * LANES]
        return acc

    small = ((r_hbm, r_buf), (c_hbm, c_buf), (n_hbm, n_buf), (ng_hbm, ng_buf), (v_hbm, v_buf))
    for i, (src, dst) in enumerate(small):
        pltpu.make_async_copy(src, dst, small_sem.at[i]).start()
    for l in range(AHEAD):
        load_own(l)

    barrier = pltpu.get_barrier_semaphore()
    for j in range(1, zs):
        pl.semaphore_signal(barrier, inc=1, device_id={'model': (z + j) % zs}, device_id_type=MESH)
    for j in range(1, ds):
        pl.semaphore_signal(barrier, inc=1, device_id={'dp': (d + j) % ds}, device_id_type=MESH)
    pl.semaphore_wait(barrier, zs + ds - 2)
    for l in range(AHEAD):
        send_pair(l)

    def norm_send():
        for i, (src, dst) in enumerate(small):
            pltpu.make_async_copy(src, dst, small_sem.at[i]).wait()
        r_pad[...] = jnp.zeros_like(r_pad)
        r_pad[:, 0:rows] = r_buf[...]
        h_out[...] = jnp.zeros_like(h_out)
        for k in range(ds):
            h_out[k, :, 0:rows] = ng_buf[:, k * rows:(k + 1) * rows]
        h_all[d] = h_out[d]
        for j in range(1, ds):
            other = (d + j) % ds
            remote(h_out.at[other], h_all.at[d], h_send, h_recv, dp=other).start()

    def norm_grad():
        acc = h_all[0]
        for k in range(1, ds):
            acc = acc + h_all[k]
        return acc[:, 0:rows]

    def layer_sums(values):
        padded = jnp.concatenate([values, jnp.zeros((layers, LANES - rows), jnp.float32)], axis=1)
        return jnp.sum(jnp.transpose(padded), axis=0, keepdims=True)

    def norm_stats():
        drain(h_all.at[0:ds - 1], h_recv)
        h = norm_grad()
        v_new = DECAY * v_buf[...] + (1.0 - DECAY) * (h * h + EPS_FLOOR)
        v_buf[...] = v_new
        zv = h * lax.rsqrt(v_new)
        nv = n_buf[...]
        k_all[d, :, 0:layers] = layer_sums(zv * zv)
        k_all[d, :, LANES:LANES + layers] = layer_sums(nv * nv)
        for j in range(1, ds):
            remote(k_all.at[d], k_all.at[d], k_send, k_recv, dp=(d + j) % ds).start()
        pltpu.make_async_copy(v_buf, vo_hbm, out_sem.at[0]).start()

    def norm_update():
        drain(k_all.at[0:ds - 1], k_recv)
        acc = k_all[0]
        for k in range(1, ds):
            acc = acc + k_all[k]
        z_sq, n_sq = acc[:, 0:layers], acc[:, LANES:LANES + layers]
        clip = jnp.maximum(1.0, jnp.sqrt(z_sq / rows_total) / CLIP_LIMIT)
        scale = lr_ref[0, 0] * jnp.maximum(SCALE_FLOOR, jnp.sqrt(n_sq / rows_total))
        clip = jnp.transpose(jnp.broadcast_to(clip, (LANES, layers)))[:, 0:rows]
        scale = jnp.transpose(jnp.broadcast_to(scale, (LANES, layers)))[:, 0:rows]
        zv = norm_grad() * lax.rsqrt(v_buf[...])
        n_buf[...] = n_buf[...] - scale * (zv / clip)

    def stage_combine(l):
        drain(own.at[l], load_sem.at[l])
        drain(peer.at[l], pair_recv.at[l])
        own[l] = own[l] + peer[l]
        x1(l).start()
        y1(l).start()

    def stage_forward(l):
        x1(l).wait_recv()
        own[l, 2, 0:half] = own[l, 2, 0:half] + in1x[l, 1]
        y1(l).wait_recv()
        own[l, 0, half:rows] = own[l, 0, half:rows] + in1y[l, 0]
        own[l, 3, 0:half] = own[l, 3, 0:half] + in1x[l, 0]
        y2(l).start()
        own[l, 3, half:rows] = own[l, 3, half:rows] + in1y[l, 1]
        x2(l).start()

    def stage_stats(l):
        y2(l).wait_recv()
        x2(l).wait_recv()
        g = own[l, 3] + in2[l].reshape(rows, cols)
        own[l, 3] = g
        q = g * g + EPS_FLOOR
        c_all[l, d] = jnp.sum(q, axis=0, keepdims=True)
        p = fold(q)
        p = jnp.concatenate([p, jnp.zeros((LANES - rows, LANES), jnp.float32)], axis=0)
        r_all[l, z] = jnp.sum(jnp.transpose(p), axis=0, keepdims=True)
        spread_d(c_all, l, c_send, c_recv)
        spread_z(r_all, l, r_send, r_recv)

    def stage_moments(l):
        drain(r_all.at[l, 0:zs - 1], r_recv.at[l])
        drain(c_all.at[l, 0:ds - 1], c_recv.at[l])
        drain(w_buf.at[l], w_in_sem.at[l])
        r_new = DECAY * r_pad[pl.ds(l, 1)] + (1.0 - DECAY) * (total(r_all, l) / cols_total)
        c_new = DECAY * c_buf[pl.ds(l, 1)] + (1.0 - DECAY) * (total(c_all, l) / rows_total)
        r_pad[pl.ds(l, 1)] = r_new
        r_buf[pl.ds(l, 1)] = r_new[:, 0:rows]
        c_buf[pl.ds(l, 1)] = c_new
        a = column(lax.rsqrt(r_new))
        b = lax.rsqrt(c_new)
        acc = jnp.zeros((1, LANES), jnp.float32)
        w_acc = jnp.zeros((1, LANES), jnp.float32)
        for t in range(cols // LANES):
            sl = slice(t * LANES, (t + 1) * LANES)
            u = own[l, 3, :, sl] * a * b[:, sl]
            acc = acc + jnp.sum(u * u, axis=0, keepdims=True)
            w = w_buf[l, :, sl]
            w_acc = w_acc + jnp.sum(w * w, axis=0, keepdims=True)
        s_all[l, z, :, 0:LANES] = acc
        s_all[l, z, :, LANES:2 * LANES] = w_acc
        spread_z(s_all, l, s_send, s_recv)

    def stage_gather(l):
        drain(s_all.at[l, 0:zs - 1], s_recv.at[l])
        t_all[l, d, :, 0:2 * LANES] = total(s_all, l)
        t_all[l, d, :, 2 * LANES:3 * LANES] = r_pad[pl.ds(l, 1)]
        spread_d(t_all, l, t_send, t_recv)

    def stage_update(l):
        drain(t_all.at[l, 0:ds - 1], t_recv.at[l])
        sums = total(t_all, l)
        count = rows_total * cols_total
        u_sum = jnp.sum(sums[:, 0:LANES], axis=1, keepdims=True)
        w_sum = jnp.sum(sums[:, LANES:2 * LANES], axis=1, keepdims=True)
        r_mean = jnp.sum(sums[:, 2 * LANES:3 * LANES], axis=1, keepdims=True) / rows_total
        u_rms = jnp.sqrt(u_sum / count * r_mean)
        clip = jnp.maximum(1.0, u_rms / CLIP_LIMIT)
        scale = lr_ref[0, 0] * jnp.maximum(SCALE_FLOOR, jnp.sqrt(w_sum / count))
        a = column(lax.rsqrt(r_pad[pl.ds(l, 1)] / r_mean))
        b = lax.rsqrt(c_buf[pl.ds(l, 1)]) / clip
        for t in range(cols // LANES):
            sl = slice(t * LANES, (t + 1) * LANES)
            u = own[l, 3, :, sl] * a * b[:, sl]
            w_buf[l, :, sl] = w_buf[l, :, sl] - scale * u

    def write(l):
        return pltpu.make_async_copy(w_buf.at[l], wo_hbm.at[l], w_out_sem.at[l])

    def body(i, carry):
        @pl.when(i + AHEAD < layers)
        def _():
            load_own(i + AHEAD)
            send_pair(i + AHEAD)

        @pl.when(i < layers)
        def _():
            pltpu.make_async_copy(w_hbm.at[i], w_buf.at[i], w_in_sem.at[i]).start()
            stage_combine(i)

        @pl.when((i >= 1) & (i < layers + 1))
        def _():
            stage_forward(i - 1)

        @pl.when(i == 1)
        def _():
            norm_send()

        @pl.when((i >= 2) & (i < layers + 2))
        def _():
            stage_stats(i - 2)

        @pl.when(i == 3)
        def _():
            norm_stats()

        @pl.when((i >= 3) & (i < layers + 3))
        def _():
            stage_moments(i - 3)

        @pl.when((i >= 4) & (i < layers + 4))
        def _():
            stage_gather(i - 4)

        @pl.when(i == 5)
        def _():
            norm_update()

        @pl.when((i >= 5) & (i < layers + 5))
        def _():
            stage_update(i - 5)

        @pl.when((i >= 6) & (i < layers + 6))
        def _():
            write(i - 6).start()

        @pl.when(i == layers + 3)
        def _():
            pltpu.make_async_copy(r_buf, ro_hbm, out_sem.at[1]).start()
            pltpu.make_async_copy(c_buf, co_hbm, out_sem.at[2]).start()
            pltpu.make_async_copy(n_buf, no_hbm, out_sem.at[3]).start()

        return carry

    lax.fori_loop(0, layers + 6, body, 0)

    def finish(l, carry):
        drain(peer.at[l], pair_send.at[l])
        x1(l).wait_send()
        y1(l).wait_send()
        x2(l).wait_send()
        y2(l).wait_send()
        drain(r_all.at[l, 0:zs - 1], r_send.at[l])
        drain(c_all.at[l, 0:ds - 1], c_send.at[l])
        drain(s_all.at[l, 0:zs - 1], s_send.at[l])
        drain(t_all.at[l, 0:ds - 1], t_send.at[l])
        write(l).wait()
        return carry

    lax.fori_loop(0, layers, finish, 0)
    drain(h_all.at[0:ds - 1], h_send)
    drain(k_all.at[0:ds - 1], k_send)
    for i, (src, dst) in enumerate(((v_buf, vo_hbm), (r_buf, ro_hbm), (c_buf, co_hbm), (n_buf, no_hbm))):
        pltpu.make_async_copy(src, dst, out_sem.at[i]).wait()


def solution(mesh):
    ds = mesh.shape['dp']
    zs = mesh.shape['model']

    def local_step(weight, grad_parts, row_stat, col_stat, norm_scale, norm_grads, norm_stat, learn_rate):
        layers, rows, cols = weight.shape
        half = rows // 2
        f32 = jnp.float32
        grads = grad_parts.reshape(layers, ds, rows, cols)
        any_spec = pl.BlockSpec(memory_space=pltpu.MemorySpace.HBM)
        dma = pltpu.SemaphoreType.DMA
        per_layer = [dma((layers,))] * 21
        return pl.pallas_call(
            step_kernel,
            out_shape=[jax.ShapeDtypeStruct(a.shape, f32) for a in (weight, row_stat, col_stat, norm_scale, norm_stat)],
            in_specs=[any_spec] * 7 + [pl.BlockSpec(memory_space=pltpu.SMEM)],
            out_specs=[any_spec] * 5,
            scratch_shapes=[
                pltpu.VMEM((layers, 4, rows, cols), f32),
                pltpu.VMEM((layers, 4, rows, cols), f32),
                pltpu.VMEM((layers, 2, half, cols), f32),
                pltpu.VMEM((layers, 2, half, cols), f32),
                pltpu.VMEM((layers, 2, half, cols), f32),
                pltpu.VMEM((layers, rows, cols), f32),
                pltpu.VMEM(row_stat.shape, f32),
                pltpu.VMEM(col_stat.shape, f32),
                pltpu.VMEM(norm_scale.shape, f32),
                pltpu.VMEM(norm_grads.shape, f32),
                pltpu.VMEM(norm_stat.shape, f32),
                pltpu.VMEM((layers, LANES), f32),
                pltpu.VMEM((layers, zs, 1, LANES), f32),
                pltpu.VMEM((layers, ds, 1, cols), f32),
                pltpu.VMEM((layers, zs, 1, 2 * LANES), f32),
                pltpu.VMEM((layers, ds, 1, 3 * LANES), f32),
                pltpu.VMEM((ds, layers, LANES), f32),
                pltpu.VMEM((ds, layers, LANES), f32),
                pltpu.VMEM((ds, 1, 2 * LANES), f32),
                *per_layer[:19],
                dma((layers,)), dma((layers,)), dma((5,)), dma((4,)),
                dma, dma, dma, dma,
            ],
            compiler_params=pltpu.CompilerParams(collective_id=0, has_side_effects=True, vmem_limit_bytes=67043328),
            name='adafactor_step',
        )(weight, grads, row_stat, col_stat, norm_scale, norm_grads, norm_stat, learn_rate.reshape(1, 1))

    mat_spec = P(None, 'dp', 'model')
    row_spec = P(None, 'dp')
    col_spec = P(None, 'model')
    return jax.shard_map(local_step, mesh=mesh, in_specs=(mat_spec, mat_spec, row_spec, col_spec, row_spec, row_spec, row_spec, P()), out_specs=(mat_spec, row_spec, col_spec, row_spec, row_spec), check_vma=False)
```

time: 370 us -> 191 us (0.52)
  waiting for transfers between devices: 264 us -> 0 us
  Pallas kernels: 0 us -> 182 us
  blocking collectives: 71.4 us -> 0 us
  other arithmetic: 16.6 us -> 0 us
  between operations: 14.8 us -> 1.32 us
  local copies, waits for them, and re-layouts: 2.6 us -> 7.4 us
    reduce_scatter x1 -> x0, waiting for transfers between devices: 227 us -> none  [local_step(): lax.psum_scatter(grad_parts, 'dp', scatter_dimension=1, tiled=True)]
    pallas_call x0 -> x1, Pallas kernels: none -> 182 us  [local_step(): pl.pallas_call(step_kernel, out_shape=[jax.ShapeDtypeStruct(a.shape, f32)...]
    psum x3 -> x0, blocking collectives: 71.4 us -> none  [the longest x1 36.9 us: local_step(): upd_sq = lax.psum(jnp.sum(update * update, axis=(1, 2)), ('model', 'dp'))]
    unnamed x3 -> x0, waiting for transfers between devices: 36.2 us -> none
    reduce_sum x6 -> x0, other arithmetic: 9.46 us -> none  [the longest x1 3.18 us: local_step(): upd_sq = lax.psum(jnp.sum(update * update, axis=(1, 2)), ('model', 'dp'))]
    sub x2 -> x0, other arithmetic: 6.39 us -> none  [the longest x1 5.71 us: local_step(): weight - learn_rate * jnp.maximum(SCALE_FLOOR, weight_rms) * update]
    unnamed x14 -> x13, local copies, waits for them, and re-layouts: 2.6 us -> 7.4 us
  transfers between devices with their start and end apart: 2 -> 0, of which waited for: 2 -> 0; matrix products, arithmetic and copies ran while one was open for 1% -> 0% of each run, Pallas kernels for 0% -> 0%
where the time goes in v1:
time: 191 us
  Pallas kernels  182 us (95%)
  local copies, waits for them, and re-layouts  7.4 us (4%)
    pallas_call x1, Pallas kernels, local_step(): pl.pallas_call(step_kernel, out_shape=[jax.ShapeDtypeStruct(a.shape, f32)...  182 us
    unnamed x13, local copies, waits for them, and re-layouts  7.4 us

profile of v1, /device:TPU:0, one launch (start us, length us, event | category | flops | bytes accessed | tf_op | source)
XLA Modules:
  0.0 191.0 jit_solution(692501198154327086)
XLA Ops:
  1.3 182.2 %adafactor_step.1 = (f32[16,96,768]{2,1,0:T(8,128)}, f32[16,96]{1,0:T(8,128)}, f32[16,768]{1,0:T(8,128)}, f32[16,96]{1,0:T(8,128)}, f32[16,96]{1,0:T(8,128)}) custom-call(f32[16,96,768]{2,1,0:T(8,128)} %w_hbm.1, f32[16,8,96,768]{3,2,1,0:T(8,128)} %bitcast.3, f32[16,96]{1,0:T(8,128)} %r_hbm.1, f32[16,768]{1,0:T(8,128)} %c_hbm.1, f32[16,96]{1,0:T(8,128)} %n_hbm.1, ...), custom_call_target="tpu_custom_call" | custom-call | tf_op jit(solution)/shard_map/adafactor_step/pallas_call | solution.py:325
  183.5 0.0 copy-start.3
  183.5 0.0 copy-start
  183.6 0.0 copy-start.2
  183.6 0.0 copy-start.1
  183.6 5.0 %copy.19 = f32[16,96,768]{2,1,0:T(8,128)} copy(f32[16,96,768]{2,1,0:T(8,128)} %get-tuple-element.10) | data formatting | bytes 9437184
  188.5 0.0 copy-done.3
  188.5 0.6 copy.20
  189.1 0.0 copy-done
  189.1 0.6 copy.21
  189.8 0.0 copy-done.2
  189.8 0.6 copy.22
  190.4 0.0 copy-done.1
  190.4 0.6 copy.23
Async XLA Ops:
  183.5 5.0 %copy-start.3 = (f32[16,96]{1,0:T(8,128)S(1)}, f32[16,96]{1,0:T(8,128)}, u32[]{:S(2)}) copy-start(f32[16,96]{1,0:T(8,128)} %get-tuple-element.11) | copy-start | bytes 18436
  183.5 5.6 %copy-start = (f32[16,768]{1,0:T(8,128)S(1)}, f32[16,768]{1,0:T(8,128)}, u32[]{:S(2)}) copy-start(f32[16,768]{1,0:T(8,128)} %get-tuple-element.12) | copy-start | bytes 147460
  183.6 6.2 %copy-start.2 = (f32[16,96]{1,0:T(8,128)S(1)}, f32[16,96]{1,0:T(8,128)}, u32[]{:S(2)}) copy-start(f32[16,96]{1,0:T(8,128)} %get-tuple-element.13) | copy-start | bytes 18436
  183.6 6.8 %copy-start.1 = (f32[16,96]{1,0:T(8,128)S(1)}, f32[16,96]{1,0:T(8,128)}, u32[]{:S(2)}) copy-start(f32[16,96]{1,0:T(8,128)} %get-tuple-element.14) | copy-start | bytes 18436

commit v2 on v1

--- a/solution.py
+++ b/solution.py
@@ -19,14 +19,13 @@
 
 
 def step_kernel(w_hbm, g_hbm, r_hbm, c_hbm, n_hbm, ng_hbm, v_hbm, lr_ref,
-                wo_hbm, ro_hbm, co_hbm, no_hbm, vo_hbm,
-                own, peer, in1x, in1y, in2, w_buf,
-                r_buf, c_buf, n_buf, ng_buf, v_buf, r_pad,
+                w_buf, r_buf, c_buf, n_buf, v_buf,
+                own, peer, in1x, in1y, in2, ng_buf, r_pad,
                 r_all, c_all, s_all, t_all, h_all, h_out, k_all,
                 load_sem, pair_send, pair_recv,
                 x1_send, x1_recv, y1_send, y1_recv, x2_send, x2_recv, y2_send, y2_recv,
                 r_send, r_recv, c_send, c_recv, s_send, s_recv, t_send, t_recv,
-                w_in_sem, w_out_sem, small_sem, out_sem, h_send, h_recv, k_send, k_recv):
+                w_in_sem, small_sem, h_send, h_recv, k_send, k_recv):
     layers, _, rows, cols = own.shape
     half = rows // 2
     zs, ds = r_all.shape[1], c_all.shape[1]
@@ -139,7 +138,6 @@
         k_all[d, :, LANES:LANES + layers] = layer_sums(nv * nv)
         for j in range(1, ds):
             remote(k_all.at[d], k_all.at[d], k_send, k_recv, dp=(d + j) % ds).start()
-        pltpu.make_async_copy(v_buf, vo_hbm, out_sem.at[0]).start()
 
     def norm_update():
         drain(k_all.at[0:ds - 1], k_recv)
@@ -230,9 +228,6 @@
             u = own[l, 3, :, sl] * a * b[:, sl]
             w_buf[l, :, sl] = w_buf[l, :, sl] - scale * u
 
-    def write(l):
-        return pltpu.make_async_copy(w_buf.at[l], wo_hbm.at[l], w_out_sem.at[l])
-
     def body(i, carry):
         @pl.when(i + AHEAD < layers)
         def _():
@@ -276,19 +271,9 @@
         def _():
             stage_update(i - 5)
 
-        @pl.when((i >= 6) & (i < layers + 6))
-        def _():
-            write(i - 6).start()
-
-        @pl.when(i == layers + 3)
-        def _():
-            pltpu.make_async_copy(r_buf, ro_hbm, out_sem.at[1]).start()
-            pltpu.make_async_copy(c_buf, co_hbm, out_sem.at[2]).start()
-            pltpu.make_async_copy(n_buf, no_hbm, out_sem.at[3]).start()
-
         return carry
 
-    lax.fori_loop(0, layers + 6, body, 0)
+    lax.fori_loop(0, layers + 5, body, 0)
 
     def finish(l, carry):
         drain(peer.at[l], pair_send.at[l])
@@ -300,14 +285,33 @@
         drain(c_all.at[l, 0:ds - 1], c_send.at[l])
         drain(s_all.at[l, 0:zs - 1], s_send.at[l])
         drain(t_all.at[l, 0:ds - 1], t_send.at[l])
-        write(l).wait()
         return carry
 
     lax.fori_loop(0, layers, finish, 0)
     drain(h_all.at[0:ds - 1], h_send)
     drain(k_all.at[0:ds - 1], k_send)
-    for i, (src, dst) in enumerate(((v_buf, vo_hbm), (r_buf, ro_hbm), (c_buf, co_hbm), (n_buf, no_hbm))):
-        pltpu.make_async_copy(src, dst, out_sem.at[i]).wait()
+
+
+def write_kernel(*refs):
+    count = len(refs) // 2
+    pairs = list(zip(refs[:count], refs[count:2 * count]))
+    sem = refs[-1]
+    for i, (src, dst) in enumerate(pairs):
+        pltpu.make_async_copy(src, dst, sem.at[i]).start()
+    for i, (src, dst) in enumerate(pairs):
+        pltpu.make_async_copy(src, dst, sem.at[i]).wait()
+
+
+def write_out(arrays):
+    return pl.pallas_call(
+        write_kernel,
+        out_shape=[jax.ShapeDtypeStruct(a.shape, a.dtype) for a in arrays],
+        in_specs=[pl.BlockSpec(memory_space=pltpu.MemorySpace.VMEM)] * len(arrays),
+        out_specs=[pl.BlockSpec(memory_space=pltpu.MemorySpace.HBM)] * len(arrays),
+        scratch_shapes=[pltpu.SemaphoreType.DMA((len(arrays),))],
+        compiler_params=pltpu.CompilerParams(vmem_limit_bytes=1 << 20),
+        name='write_out',
+    )(*arrays)
 
 
 def solution(mesh):
@@ -322,23 +326,18 @@
         any_spec = pl.BlockSpec(memory_space=pltpu.MemorySpace.HBM)
         dma = pltpu.SemaphoreType.DMA
         per_layer = [dma((layers,))] * 21
-        return pl.pallas_call(
+        outs = pl.pallas_call(
             step_kernel,
-            out_shape=[jax.ShapeDtypeStruct(a.shape, f32) for a in (weight, row_stat, col_stat, norm_scale, norm_stat)],
+            out_shape=[pltpu.VMEM(a.shape, f32) for a in (weight, row_stat, col_stat, norm_scale, norm_stat)],
             in_specs=[any_spec] * 7 + [pl.BlockSpec(memory_space=pltpu.SMEM)],
-            out_specs=[any_spec] * 5,
+            out_specs=[pl.BlockSpec(memory_space=pltpu.MemorySpace.VMEM)] * 5,
             scratch_shapes=[
                 pltpu.VMEM((layers, 4, rows, cols), f32),
                 pltpu.VMEM((layers, 4, rows, cols), f32),
                 pltpu.VMEM((layers, 2, half, cols), f32),
                 pltpu.VMEM((layers, 2, half, cols), f32),
                 pltpu.VMEM((layers, 2, half, cols), f32),
-                pltpu.VMEM((layers, rows, cols), f32),
-                pltpu.VMEM(row_stat.shape, f32),
-                pltpu.VMEM(col_stat.shape, f32),
-                pltpu.VMEM(norm_scale.shape, f32),
                 pltpu.VMEM(norm_grads.shape, f32),
-                pltpu.VMEM(norm_stat.shape, f32),
                 pltpu.VMEM((layers, LANES), f32),
                 pltpu.VMEM((layers, zs, 1, LANES), f32),
                 pltpu.VMEM((layers, ds, 1, cols), f32),
@@ -348,12 +347,13 @@
                 pltpu.VMEM((ds, layers, LANES), f32),
                 pltpu.VMEM((ds, 1, 2 * LANES), f32),
                 *per_layer[:19],
-                dma((layers,)), dma((layers,)), dma((5,)), dma((4,)),
+                dma((layers,)), dma((5,)),
                 dma, dma, dma, dma,
             ],
-            compiler_params=pltpu.CompilerParams(collective_id=0, has_side_effects=True, vmem_limit_bytes=67043328),
+            compiler_params=pltpu.CompilerParams(collective_id=0, has_side_effects=True, vmem_limit_bytes=54 * 1000 * 1000),
             name='adafactor_step',
         )(weight, grads, row_stat, col_stat, norm_scale, norm_grads, norm_stat, learn_rate.reshape(1, 1))
+        return write_out(outs)
 
     mat_spec = P(None, 'dp', 'model')
     row_spec = P(None, 'dp')

time: 191 us -> 185 us (0.969)
  local copies, waits for them, and re-layouts: 7.4 us -> 0 us
  Pallas kernels: 182 us -> 184 us
    unnamed x13 -> x0, local copies, waits for them, and re-layouts: 7.4 us -> none
    pallas_call x1 -> x2, Pallas kernels: 182 us -> 184 us  [the longest x1 181 us: local_step(): pl.pallas_call(step_kernel, out_shape=[pltpu.VMEM(a.shape, f32) for a in...]
where the time goes in v2:
time: 185 us
  Pallas kernels  184 us (99%)
    pallas_call x1, Pallas kernels, local_step(): pl.pallas_call(step_kernel, out_shape=[pltpu.VMEM(a.shape, f32) for a in...  181 us

profile of v2, /device:TPU:0, one launch (start us, length us, event | category | flops | bytes accessed | tf_op | source)
XLA Modules:
  0.0 185.0 jit_solution(12767187694373410725)
XLA Ops:
  1.3 181.4 %adafactor_step.1 = (f32[16,96,768]{2,1,0:T(8,128)S(1)}, f32[16,96]{1,0:T(8,128)S(1)}, f32[16,768]{1,0:T(8,128)S(1)}, f32[16,96]{1,0:T(8,128)S(1)}, f32[16,96]{1,0:T(8,128)S(1)}) custom-call(f32[16,96,768]{2,1,0:T(8,128)} %w_hbm.1, f32[16,8,96,768]{3,2,1,0:T(8,128)} %bitcast.3, f32[16,96]{1,0:T(8,128)} %r_hbm.1, f32[16,768]{1,0:T(8,128)} %c_hbm.1, ...), custom_call_target="tpu_custom_call" | custom-call | tf_op jit(solution)/shard_map/adafactor_step/pallas_call | solution.py:329
  182.7 2.2 %write_out.1 = (f32[16,96,768]{2,1,0:T(8,128)}, f32[16,96]{1,0:T(8,128)}, f32[16,768]{1,0:T(8,128)}, f32[16,96]{1,0:T(8,128)}, f32[16,96]{1,0:T(8,128)}) custom-call(f32[16,96,768]{2,1,0:T(8,128)S(1)} %get-tuple-element.10.refs_0_, f32[16,96]{1,0:T(8,128)S(1)} %get-tuple-element.11.refs_1_, f32[16,768]{1,0:T(8,128)S(1)} %get-tuple-element.12.refs_2_, ...), custom_call_target="tpu_custom_call" | custom-call | tf_op jit(solution)/shard_map/write_out/pallas_call | solution.py:306

commit v3 on v2

v3 whole, which is shorter than its diff:
```python
import functools

import jax
import jax.numpy as jnp
from jax import lax
from jax.experimental import pallas as pl
from jax.experimental.pallas import tpu as pltpu
from jax.sharding import PartitionSpec as P

STEP_COUNT = 4
DECAY_POWER = 0.8
EPS_FLOOR = 1e-30
SCALE_FLOOR = 1e-3
CLIP_LIMIT = 1.0
DECAY = 1.0 - STEP_COUNT ** -DECAY_POWER
MESH = pl.DeviceIdType.MESH
LANES = 128
AHEAD = 2


def step_kernel(w_hbm, g_hbm, r_hbm, c_hbm, n_hbm, ng_hbm, v_hbm, lr_ref,
                w_buf, r_buf, c_buf, n_buf, v_buf,
                own, peer, in1x, in1y, in2, ng_buf, r_pad,
                r_all, c_pair, c_all, c_last, s_all, t_all, h_out, h_pair, h_all, k_all,
                load_sem, pair_send, pair_x, pair_y, pair_rest,
                x1_send, x1_recv, y1_send, y1_recv, x2_send, x2_recv, y2_send, y2_recv,
                r_send, r_recv, cp_send, cp_recv, c_send, c_recv, s_send, s_recv, t_send, t_recv, w_sem,
                small_sem, h_send, h_recv, k_send, k_recv):
    layers, _, rows, cols = own.shape
    half = rows // 2
    last = layers - 1
    zs, ds = r_all.shape[1], c_last.shape[0]
    chips = ds // 2
    rows_total, cols_total = rows * ds, cols * zs
    z = lax.axis_index('model')
    d = lax.axis_index('dp')
    core = d % 2
    chip = d // 2
    dx = d + 2 - 4 * (chip % 2)
    dy = d + 4 - 8 * (d // 4)
    dxy = dx + dy - d
    dc = d + 1 - 2 * core
    blocks = (dx, dxy, dy, d)
    column_peers = []
    for j in range(1, 2 * zs):
        other = (2 * z + core + j) % (2 * zs)
        column_peers.append({'model': other // 2, 'dp': d - core + other % 2})
    z_peers = [{'model': (z + j) % zs} for j in range(1, zs)]
    d_peers = [{'dp': (d + j) % ds} for j in range(1, ds)]
    plane_peers = [{'dp': e} for e in (dx, dy, dxy)]

    def remote(src, dst, send, recv, where):
        return pltpu.make_async_remote_copy(src_ref=src, dst_ref=dst, send_sem=send, recv_sem=recv,
                                            device_id=where, device_id_type=MESH)

    def spread(ref, send, recv, peers):
        for where in peers:
            remote(ref, ref, send, recv, where).start()

    def drain(ref, sem):
        pltpu.make_async_copy(ref, ref, sem).wait()

    def load_own(l):
        for k in range(4):
            pltpu.make_async_copy(g_hbm.at[l, blocks[k]], own.at[l, k], load_sem.at[l]).start()

    def send_pair(l, source):
        pieces = ((0, 0, pair_x), (1, 0, pair_x), (1, half, pair_y), (2, half, pair_y),
                  (0, half, pair_rest), (2, 0, pair_rest), (3, 0, pair_rest), (3, half, pair_rest))
        for k, row, recv in pieces:
            part = pl.ds(row, half)
            remote(source(k).at[part], peer.at[l, k, part], pair_send.at[l], recv.at[l], {'dp': dc}).start()

    def from_hbm(l):
        return lambda k: g_hbm.at[l, blocks[k] + dc - d]

    def x1(l):
        return remote(own.at[l, 0:2, 0:half], in1x.at[l], x1_send.at[l], x1_recv.at[l], {'dp': dx})

    def y1(l):
        return remote(own.at[l, 1:3, half:rows], in1y.at[l], y1_send.at[l], y1_recv.at[l], {'dp': dy})

    def y2(l):
        return remote(own.at[l, 2, 0:half], in2.at[l, 0], y2_send.at[l], y2_recv.at[l], {'dp': dy})

    def x2(l):
        return remote(own.at[l, 0, half:rows], in2.at[l, 1], x2_send.at[l], x2_recv.at[l], {'dp': dx})

    def total(buf):
        acc = buf[0]
        for j in range(1, buf.shape[0]):
            acc = acc + buf[j]
        return acc

    def column(row):
        return jnp.transpose(jnp.broadcast_to(row, (LANES, LANES)))[0:rows]

    def fold(values):
        acc = values[:, 0:LANES]
        for t in range(1, cols // LANES):
            acc = acc + values[:, t * LANES:(t + 1) * LANES]
        return acc

    small = ((r_hbm, r_buf), (c_hbm, c_buf), (n_hbm, n_buf), (ng_hbm, ng_buf), (v_hbm, v_buf))
    for k in range(4):
        pltpu.make_async_copy(g_hbm.at[0, blocks[k] + dc - d], own.at[last, k], load_sem.at[last]).start()
    for l in range(AHEAD):
        load_own(l)
    for i, (src, dst) in enumerate(small):
        pltpu.make_async_copy(src, dst, small_sem.at[i]).start()

    barrier = pltpu.get_barrier_semaphore()
    everyone = d_peers + column_peers
    for where in everyone:
        pl.semaphore_signal(barrier, inc=1, device_id=where, device_id_type=MESH)
    pl.semaphore_wait(barrier, len(everyone))
    drain(own.at[last], load_sem.at[last])
    send_pair(0, lambda k: own.at[last, k])
    for l in range(1, AHEAD):
        send_pair(l, from_hbm(l))

    def norm_split():
        for i, (src, dst) in enumerate(small):
            pltpu.make_async_copy(src, dst, small_sem.at[i]).wait()
        r_pad[...] = jnp.zeros_like(r_pad)
        r_pad[:, 0:rows] = r_buf[...]
        h_out[...] = jnp.zeros_like(h_out)
        k_all[...] = jnp.zeros_like(k_all)
        for k in range(ds):
            h_out[k // 2, k % 2, :, 0:rows] = ng_buf[:, k * rows:(k + 1) * rows]
        remote(h_out.at[:, 1 - core], h_pair, h_send.at[0], h_recv.at[0], {'dp': dc}).start()

    def norm_send():
        remote(h_out.at[:, 1 - core], h_pair, h_send.at[0], h_recv.at[0], {'dp': dc}).wait()
        for k in range(chips):
            h_pair[k] = h_pair[k] + h_out[k, core]
        h_all[chip] = h_pair[chip]
        for e in (dx, dy, dxy):
            remote(h_pair.at[e // 2], h_all.at[chip], h_send.at[1], h_recv.at[1], {'dp': e}).start()

    def layer_sums(values):
        padded = jnp.concatenate([values, jnp.zeros((layers, LANES - rows), jnp.float32)], axis=1)
        return jnp.sum(jnp.transpose(padded), axis=0, keepdims=True)

    def norm_stats():
        drain(h_all.at[0:chips - 1], h_recv.at[1])
        h = total(h_all)[:, 0:rows]
        v_new = DECAY * v_buf[...] + (1.0 - DECAY) * (h * h + EPS_FLOOR)
        v_buf[...] = v_new
        zv = h * lax.rsqrt(v_new)
        nv = n_buf[...]
        k_all[d, :, 0:layers] = layer_sums(zv * zv)
        k_all[d, :, LANES:LANES + layers] = layer_sums(nv * nv)
        spread(k_all.at[d], k_send, k_recv, d_peers)

    def norm_update():
        drain(k_all.at[0:ds - 1], k_recv)
        acc = total(k_all)
        z_sq, n_sq = acc[:, 0:layers], acc[:, LANES:LANES + layers]
        clip = jnp.maximum(1.0, jnp.sqrt(z_sq / rows_total) / CLIP_LIMIT)
        scale = lr_ref[0, 0] * jnp.maximum(SCALE_FLOOR, jnp.sqrt(n_sq / rows_total))
        clip = jnp.transpose(jnp.broadcast_to(clip, (LANES, layers)))[:, 0:rows]
        scale = jnp.transpose(jnp.broadcast_to(scale, (LANES, layers)))[:, 0:rows]
        zv = total(h_all)[:, 0:rows] * lax.rsqrt(v_buf[...])
        n_buf[...] = n_buf[...] - scale * (zv / clip)

    def stage_combine(l):
        drain(own.at[l], load_sem.at[l])
        drain(in1x.at[l], pair_x.at[l])
        own[l, 0:2, 0:half] = own[l, 0:2, 0:half] + peer[l, 0:2, 0:half]
        x1(l).start()
        drain(in1y.at[l], pair_y.at[l])
        own[l, 1:3, half:rows] = own[l, 1:3, half:rows] + peer[l, 1:3, half:rows]
        y1(l).start()
        drain(peer.at[l, 0:2], pair_rest.at[l])
        own[l, 0, half:rows] = own[l, 0, half:rows] + peer[l, 0, half:rows]
        own[l, 2, 0:half] = own[l, 2, 0:half] + peer[l, 2, 0:half]
        own[l, 3] = own[l, 3] + peer[l, 3]

    def stage_forward(l):
        x1(l).wait_recv()
        own[l, 2, 0:half] = own[l, 2, 0:half] + in1x[l, 1]
        y1(l).wait_recv()
        own[l, 0, half:rows] = own[l, 0, half:rows] + in1y[l, 0]
        y2(l).start()
        own[l, 3, 0:half] = own[l, 3, 0:half] + in1x[l, 0]
        x2(l).start()
        own[l, 3, half:rows] = own[l, 3, half:rows] + in1y[l, 1]

    def stage_stats(l):
        y2(l).wait_recv()
        x2(l).wait_recv()
        g = own[l, 3] + in2[l].reshape(rows, cols)
        own[l, 3] = g
        q = g * g + EPS_FLOOR
        col = jnp.sum(q, axis=0, keepdims=True)
        c_pair[l, core] = col
        c_last[d] = col
        p = jnp.concatenate([fold(q), jnp.zeros((LANES - rows, LANES), jnp.float32)], axis=0)
        r_all[l, z] = jnp.sum(jnp.transpose(p), axis=0, keepdims=True)

        @pl.when(l < last)
        def _():
            spread(c_pair.at[l, core], cp_send.at[l], cp_recv.at[l], [{'dp': dc}])

        @pl.when(l == last)
        def _():
            spread(c_last.at[d], c_send.at[l], c_recv.at[l], d_peers)

        spread(r_all.at[l, z], r_send.at[l], r_recv.at[l], z_peers)

    def stage_columns(l):
        remote(c_pair.at[l, core], c_pair.at[l, core], cp_send.at[l], cp_recv.at[l], {'dp': dc}).wait()
        c_all[l, chip] = c_pair[l, 0] + c_pair[l, 1]
        spread(c_all.at[l, chip], c_send.at[l], c_recv.at[l], plane_peers)

    def stage_moments(l):
        @pl.when(l < last)
        def _():
            drain(c_all.at[l, 0:chips - 1], c_recv.at[l])

        @pl.when(l == last)
        def _():
            drain(c_last.at[0:ds - 1], c_recv.at[l])
            for k in range(chips):
                c_all[l, k] = c_last[2 * k] + c_last[2 * k + 1]

        if zs > 1:
            drain(r_all.at[l, 0:zs - 1], r_recv.at[l])
        drain(w_buf.at[l], w_sem.at[l])
        r_new = DECAY * r_pad[pl.ds(l, 1)] + (1.0 - DECAY) * (total(r_all.at[l]) / cols_total)
        c_new = DECAY * c_buf[pl.ds(l, 1)] + (1.0 - DECAY) * (total(c_all.at[l]) / rows_total)
        r_pad[pl.ds(l, 1)] = r_new
        r_buf[pl.ds(l, 1)] = r_new[:, 0:rows]
        c_buf[pl.ds(l, 1)] = c_new
        a = column(lax.rsqrt(r_new))
        b = lax.rsqrt(c_new)
        acc = jnp.zeros((1, LANES), jnp.float32)
        w_acc = jnp.zeros((1, LANES), jnp.float32)
        for t in range(cols // LANES):
            sl = slice(t * LANES, (t + 1) * LANES)
            u = own[l, 3, :, sl] * a * b[:, sl]
            acc = acc + jnp.sum(u * u, axis=0, keepdims=True)
            w = w_buf[l, :, sl]
            w_acc = w_acc + jnp.sum(w * w, axis=0, keepdims=True)
        lane = lax.broadcasted_iota(jnp.int32, (1, LANES), 1)
        row = jnp.where(lane == 0, jnp.sum(acc, axis=1, keepdims=True), 0.0)
        row = jnp.where(lane == 1, jnp.sum(w_acc, axis=1, keepdims=True), row)
        row = jnp.where(lane == 2, jnp.sum(r_new, axis=1, keepdims=True), row)
        s_all[l, 2 * z + core] = row
        spread(s_all.at[l, 2 * z + core], s_send.at[l], s_recv.at[l], column_peers)

    def stage_gather(l):
        drain(s_all.at[l, 0:2 * zs - 1], s_recv.at[l])
        t_all[l, chip] = total(s_all.at[l])
        spread(t_all.at[l, chip], t_send.at[l], t_recv.at[l], plane_peers)

    def stage_update(l):
        drain(t_all.at[l, 0:chips - 1], t_recv.at[l])
        sums = total(t_all.at[l])
        count = rows_total * cols_total
        r_mean = sums[:, 2:3] / (rows_total * zs)
        u_rms = jnp.sqrt(sums[:, 0:1] / count * r_mean)
        clip = jnp.maximum(1.0, u_rms / CLIP_LIMIT)
        scale = lr_ref[0, 0] * jnp.maximum(SCALE_FLOOR, jnp.sqrt(sums[:, 1:2] / count))
        a = column(lax.rsqrt(r_pad[pl.ds(l, 1)] / r_mean))
        b = lax.rsqrt(c_buf[pl.ds(l, 1)]) / clip
        for t in range(cols // LANES):
            sl = slice(t * LANES, (t + 1) * LANES)
            u = own[l, 3, :, sl] * a * b[:, sl]
            w_buf[l, :, sl] = w_buf[l, :, sl] - scale * u

    def drain_bulk(l):
        drain(peer.at[l], pair_send.at[l])
        x1(l).wait_send()
        y1(l).wait_send()
        x2(l).wait_send()
        y2(l).wait_send()

    def drain_sums(l):
        if zs > 1:
            drain(r_all.at[l, 0:zs - 1], r_send.at[l])

        @pl.when(l < last)
        def _():
            drain(c_all.at[l, 0:chips - 1], c_send.at[l])

        @pl.when(l == last)
        def _():
            drain(c_last.at[0:ds - 1], c_send.at[l])

        drain(s_all.at[l, 0:2 * zs - 1], s_send.at[l])
        drain(t_all.at[l, 0:chips - 1], t_send.at[l])

    def at(i, lag, stage):
        @pl.when((i >= lag) & (i < layers + lag))
        def _():
            stage(i - lag)

    def once(i, when, stage):
        @pl.when(i == when)
        def _():
            stage()

    def body(i, carry):
        @pl.when(i + AHEAD < layers)
        def _():
            load_own(i + AHEAD)
            send_pair(i + AHEAD, from_hbm(i + AHEAD))

        @pl.when(i < layers)
        def _():
            stage_combine(i)
            pltpu.make_async_copy(w_hbm.at[i], w_buf.at[i], w_sem.at[i]).start()

        at(i, 1, stage_forward)
        once(i, 1, norm_split)
        once(i, 2, norm_send)

        @pl.when((i >= 3) & (i < last + 3))
        def _():
            stage_columns(i - 3)

        at(i, 4, stage_moments)
        at(i, 5, stage_gather)
        at(i, 6, stage_update)
        at(i, 4, drain_bulk)
        at(i, 7, drain_sums)
        once(i, 4, norm_stats)
        once(i, 6, norm_update)
        at(i, 2, stage_stats)
        return carry

    lax.fori_loop(0, layers + 6, body, 0)
    for l in range(last, layers):
        drain_sums(l)
    drain(h_all.at[0:chips - 1], h_send.at[1])
    drain(k_all.at[0:ds - 1], k_send)


def write_kernel(*refs):
    count = len(refs) // 2
    pairs = list(zip(refs[:count], refs[count:2 * count]))
    sem = refs[-1]
    for i, (src, dst) in enumerate(pairs):
        pltpu.make_async_copy(src, dst, sem.at[i]).start()
    for i, (src, dst) in enumerate(pairs):
        pltpu.make_async_copy(src, dst, sem.at[i]).wait()


def write_out(arrays):
    return pl.pallas_call(
        write_kernel,
        out_shape=[jax.ShapeDtypeStruct(a.shape, a.dtype) for a in arrays],
        in_specs=[pl.BlockSpec(memory_space=pltpu.MemorySpace.VMEM)] * len(arrays),
        out_specs=[pl.BlockSpec(memory_space=pltpu.MemorySpace.HBM)] * len(arrays),
        scratch_shapes=[pltpu.SemaphoreType.DMA((len(arrays),))],
        compiler_params=pltpu.CompilerParams(vmem_limit_bytes=1 << 20),
        name='write_out',
    )(*arrays)


def solution(mesh):
    ds = mesh.shape['dp']
    zs = mesh.shape['model']

    def local_step(weight, grad_parts, row_stat, col_stat, norm_scale, norm_grads, norm_stat, learn_rate):
        layers, rows, cols = weight.shape
        half = rows // 2
        f32 = jnp.float32
        grads = grad_parts.reshape(layers, ds, rows, cols)
        any_spec = pl.BlockSpec(memory_space=pltpu.MemorySpace.HBM)
        dma = pltpu.SemaphoreType.DMA
        outs = pl.pallas_call(
            step_kernel,
            out_shape=[pltpu.VMEM(a.shape, f32) for a in (weight, row_stat, col_stat, norm_scale, norm_stat)],
            in_specs=[any_spec] * 7 + [pl.BlockSpec(memory_space=pltpu.SMEM)],
            out_specs=[pl.BlockSpec(memory_space=pltpu.MemorySpace.VMEM)] * 5,
            scratch_shapes=[
                pltpu.VMEM((layers, 4, rows, cols), f32),
                pltpu.VMEM((layers, 4, rows, cols), f32),
                pltpu.VMEM((layers, 2, half, cols), f32),
                pltpu.VMEM((layers, 2, half, cols), f32),
                pltpu.VMEM((layers, 2, half, cols), f32),
                pltpu.VMEM(norm_grads.shape, f32),
                pltpu.VMEM((layers, LANES), f32),
                pltpu.VMEM((layers, zs, 1, LANES), f32),
                pltpu.VMEM((layers, 2, 1, cols), f32),
                pltpu.VMEM((layers, ds // 2, 1, cols), f32),
                pltpu.VMEM((ds, 1, cols), f32),
                pltpu.VMEM((layers, 2 * zs, 1, LANES), f32),
                pltpu.VMEM((layers, ds // 2, 1, LANES), f32),
                pltpu.VMEM((ds // 2, 2, layers, LANES), f32),
                pltpu.VMEM((ds // 2, layers, LANES), f32),
                pltpu.VMEM((ds // 2, layers, LANES), f32),
                pltpu.VMEM((ds, 1, 2 * LANES), f32),
                *[dma((layers,))] * 24,
                dma((5,)), dma((2,)), dma((2,)), dma, dma,
            ],
            compiler_params=pltpu.CompilerParams(collective_id=0, has_side_effects=True, vmem_limit_bytes=54 * 1000 * 1000),
            name='adafactor_step',
        )(weight, grads, row_stat, col_stat, norm_scale, norm_grads, norm_stat, learn_rate.reshape(1, 1))
        return write_out(outs)

    mat_spec = P(None, 'dp', 'model')
    row_spec = P(None, 'dp')
    col_spec = P(None, 'model')
    return jax.shard_map(local_step, mesh=mesh, in_specs=(mat_spec, mat_spec, row_spec, col_spec, row_spec, row_spec, row_spec, P()), out_specs=(mat_spec, row_spec, col_spec, row_spec, row_spec), check_vma=False)
```

time: 185 us -> 183 us (0.989)
  Pallas kernels: 184 us -> 182 us
    pallas_call x1, Pallas kernels: 181 us -> 179 us  [local_step(): pl.pallas_call(step_kernel, out_shape=[pltpu.VMEM(a.shape, f32) for a in...]
where the time goes in v3:
time: 183 us
  Pallas kernels  182 us (99%)
    pallas_call x1, Pallas kernels, local_step(): pl.pallas_call(step_kernel, out_shape=[pltpu.VMEM(a.shape, f32) for a in...  179 us

profile of v3, /device:TPU:0, one launch (start us, length us, event | category | flops | bytes accessed | tf_op | source)
XLA Modules:
  0.0 183.0 jit_solution(6562655328058867678)
XLA Ops:
  1.3 179.5 %adafactor_step.1 = (f32[16,96,768]{2,1,0:T(8,128)S(1)}, f32[16,96]{1,0:T(8,128)S(1)}, f32[16,768]{1,0:T(8,128)S(1)}, f32[16,96]{1,0:T(8,128)S(1)}, f32[16,96]{1,0:T(8,128)S(1)}) custom-call(f32[16,96,768]{2,1,0:T(8,128)} %w_hbm.1, f32[16,8,96,768]{3,2,1,0:T(8,128)} %bitcast.3, f32[16,96]{1,0:T(8,128)} %r_hbm.1, f32[16,768]{1,0:T(8,128)} %c_hbm.1, ...), custom_call_target="tpu_custom_call" | custom-call | tf_op jit(solution)/shard_map/adafactor_step/pallas_call | solution.py:374
  180.8 2.2 %write_out.1 = (f32[16,96,768]{2,1,0:T(8,128)}, f32[16,96]{1,0:T(8,128)}, f32[16,768]{1,0:T(8,128)}, f32[16,96]{1,0:T(8,128)}, f32[16,96]{1,0:T(8,128)}) custom-call(f32[16,96,768]{2,1,0:T(8,128)S(1)} %get-tuple-element.10.refs_0_, f32[16,96]{1,0:T(8,128)S(1)} %get-tuple-element.11.refs_1_, f32[16,768]{1,0:T(8,128)S(1)} %get-tuple-element.12.refs_2_, ...), custom_call_target="tpu_custom_call" | custom-call | tf_op jit(solution)/shard_map/write_out/pallas_call | solution.py:352

commit v4 on v3

--- a/solution.py
+++ b/solution.py
@@ -23,9 +23,9 @@
                 own, peer, in1x, in1y, in2, ng_buf, r_pad,
                 r_all, c_pair, c_all, c_last, s_all, t_all, h_out, h_pair, h_all, k_all,
                 load_sem, pair_send, pair_x, pair_y, pair_rest,
-                x1_send, x1_recv, y1_send, y1_recv, x2_send, x2_recv, y2_send, y2_recv,
+                one_send, x1_recv, y1_recv, two_send, x2_recv, y2_recv,
                 r_send, r_recv, cp_send, cp_recv, c_send, c_recv, s_send, s_recv, t_send, t_recv, w_sem,
-                small_sem, h_send, h_recv, k_send, k_recv):
+                small_sem, h_send, h_recv, k_send, k_recv, last_send, last_recv):
     layers, _, rows, cols = own.shape
     half = rows // 2
     last = layers - 1
@@ -34,20 +34,19 @@
     rows_total, cols_total = rows * ds, cols * zs
     z = lax.axis_index('model')
     d = lax.axis_index('dp')
-    core = d % 2
-    chip = d // 2
-    dx = d + 2 - 4 * (chip % 2)
-    dy = d + 4 - 8 * (d // 4)
+    chip, core = lax.div(d, 2), lax.rem(d, 2)
+    dx = d + 2 - 4 * lax.rem(chip, 2)
+    dy = d + 4 - 8 * lax.div(d, 4)
     dxy = dx + dy - d
     dc = d + 1 - 2 * core
     blocks = (dx, dxy, dy, d)
-    column_peers = []
-    for j in range(1, 2 * zs):
-        other = (2 * z + core + j) % (2 * zs)
-        column_peers.append({'model': other // 2, 'dp': d - core + other % 2})
-    z_peers = [{'model': (z + j) % zs} for j in range(1, zs)]
-    d_peers = [{'dp': (d + j) % ds} for j in range(1, ds)]
+    z_peers = [{'model': lax.rem(z + j, zs)} for j in range(1, zs)]
+    d_peers = [{'dp': e} for e in (dc, dx, dx + dc - d, dy, dy + dc - d, dxy, dxy + dc - d)]
+    column_peers = [{'dp': dc}] + [{'model': p['model'], 'dp': e} for p in z_peers for e in (d, dc)]
     plane_peers = [{'dp': e} for e in (dx, dy, dxy)]
+
+    def ring(sem, l):
+        return sem.at[lax.rem(l, sem.shape[0])]
 
     def remote(src, dst, send, recv, where):
         return pltpu.make_async_remote_copy(src_ref=src, dst_ref=dst, send_sem=send, recv_sem=recv,
@@ -62,29 +61,29 @@
 
     def load_own(l):
         for k in range(4):
-            pltpu.make_async_copy(g_hbm.at[l, blocks[k]], own.at[l, k], load_sem.at[l]).start()
+            pltpu.make_async_copy(g_hbm.at[l, blocks[k]], own.at[l, k], ring(load_sem, l)).start()
 
     def send_pair(l, source):
         pieces = ((0, 0, pair_x), (1, 0, pair_x), (1, half, pair_y), (2, half, pair_y),
                   (0, half, pair_rest), (2, 0, pair_rest), (3, 0, pair_rest), (3, half, pair_rest))
         for k, row, recv in pieces:
             part = pl.ds(row, half)
-            remote(source(k).at[part], peer.at[l, k, part], pair_send.at[l], recv.at[l], {'dp': dc}).start()
+            remote(source(k).at[part], peer.at[l, k, part], ring(pair_send, l), ring(recv, l), {'dp': dc}).start()
 
     def from_hbm(l):
         return lambda k: g_hbm.at[l, blocks[k] + dc - d]
 
     def x1(l):
-        return remote(own.at[l, 0:2, 0:half], in1x.at[l], x1_send.at[l], x1_recv.at[l], {'dp': dx})
+        return remote(own.at[l, 0:2, 0:half], in1x.at[l], ring(one_send, l), ring(x1_recv, l), {'dp': dx})
 
     def y1(l):
-        return remote(own.at[l, 1:3, half:rows], in1y.at[l], y1_send.at[l], y1_recv.at[l], {'dp': dy})
+        return remote(own.at[l, 1:3, half:rows], in1y.at[l], ring(one_send, l), ring(y1_recv, l), {'dp': dy})
 
     def y2(l):
-        return remote(own.at[l, 2, 0:half], in2.at[l, 0], y2_send.at[l], y2_recv.at[l], {'dp': dy})
+        return remote(own.at[l, 2, 0:half], in2.at[l, 0], ring(two_send, l), ring(y2_recv, l), {'dp': dy})
 
     def x2(l):
-        return remote(own.at[l, 0, half:rows], in2.at[l, 1], x2_send.at[l], x2_recv.at[l], {'dp': dx})
+        return remote(own.at[l, 0, half:rows], in2.at[l, 1], ring(two_send, l), ring(x2_recv, l), {'dp': dx})
 
     def total(buf):
         acc = buf[0]
@@ -103,7 +102,7 @@
 
     small = ((r_hbm, r_buf), (c_hbm, c_buf), (n_hbm, n_buf), (ng_hbm, ng_buf), (v_hbm, v_buf))
     for k in range(4):
-        pltpu.make_async_copy(g_hbm.at[0, blocks[k] + dc - d], own.at[last, k], load_sem.at[last]).start()
+        pltpu.make_async_copy(g_hbm.at[0, blocks[k] + dc - d], own.at[last, k], load_sem.at[AHEAD]).start()
     for l in range(AHEAD):
         load_own(l)
     for i, (src, dst) in enumerate(small):
@@ -114,7 +113,7 @@
     for where in everyone:
         pl.semaphore_signal(barrier, inc=1, device_id=where, device_id_type=MESH)
     pl.semaphore_wait(barrier, len(everyone))
-    drain(own.at[last], load_sem.at[last])
+    drain(own.at[last], load_sem.at[AHEAD])
     send_pair(0, lambda k: own.at[last, k])
     for l in range(1, AHEAD):
         send_pair(l, from_hbm(l))
@@ -136,7 +135,7 @@
             h_pair[k] = h_pair[k] + h_out[k, core]
         h_all[chip] = h_pair[chip]
         for e in (dx, dy, dxy):
-            remote(h_pair.at[e // 2], h_all.at[chip], h_send.at[1], h_recv.at[1], {'dp': e}).start()
+            remote(h_pair.at[lax.div(e, 2)], h_all.at[chip], h_send.at[1], h_recv.at[1], {'dp': e}).start()
 
     def layer_sums(values):
         padded = jnp.concatenate([values, jnp.zeros((layers, LANES - rows), jnp.float32)], axis=1)
@@ -165,17 +164,18 @@
         n_buf[...] = n_buf[...] - scale * (zv / clip)
 
     def stage_combine(l):
-        drain(own.at[l], load_sem.at[l])
-        drain(in1x.at[l], pair_x.at[l])
+        drain(own.at[l], ring(load_sem, l))
+        drain(in1x.at[l], ring(pair_x, l))
         own[l, 0:2, 0:half] = own[l, 0:2, 0:half] + peer[l, 0:2, 0:half]
         x1(l).start()
-        drain(in1y.at[l], pair_y.at[l])
+        drain(in1y.at[l], ring(pair_y, l))
         own[l, 1:3, half:rows] = own[l, 1:3, half:rows] + peer[l, 1:3, half:rows]
         y1(l).start()
-        drain(peer.at[l, 0:2], pair_rest.at[l])
+        drain(peer.at[l, 0:2], ring(pair_rest, l))
         own[l, 0, half:rows] = own[l, 0, half:rows] + peer[l, 0, half:rows]
         own[l, 2, 0:half] = own[l, 2, 0:half] + peer[l, 2, 0:half]
         own[l, 3] = own[l, 3] + peer[l, 3]
+        drain(peer.at[l], ring(pair_send, l))
 
     def stage_forward(l):
         x1(l).wait_recv()
@@ -188,6 +188,7 @@
         own[l, 3, half:rows] = own[l, 3, half:rows] + in1y[l, 1]
 
     def stage_stats(l):
+        pltpu.make_async_copy(w_hbm.at[l], w_buf.at[l], ring(w_sem, l)).start()
         y2(l).wait_recv()
         x2(l).wait_recv()
         g = own[l, 3] + in2[l].reshape(rows, cols)
@@ -201,33 +202,35 @@
 
         @pl.when(l < last)
         def _():
-            spread(c_pair.at[l, core], cp_send.at[l], cp_recv.at[l], [{'dp': dc}])
+            spread(c_pair.at[l, core], ring(cp_send, l), ring(cp_recv, l), [{'dp': dc}])
 
         @pl.when(l == last)
         def _():
-            spread(c_last.at[d], c_send.at[l], c_recv.at[l], d_peers)
-
-        spread(r_all.at[l, z], r_send.at[l], r_recv.at[l], z_peers)
+            spread(c_last.at[d], last_send, last_recv, d_peers)
+
+        spread(r_all.at[l, z], ring(r_send, l), ring(r_recv, l), z_peers)
 
     def stage_columns(l):
-        remote(c_pair.at[l, core], c_pair.at[l, core], cp_send.at[l], cp_recv.at[l], {'dp': dc}).wait()
+        remote(c_pair.at[l, core], c_pair.at[l, core], ring(cp_send, l), ring(cp_recv, l), {'dp': dc}).wait()
         c_all[l, chip] = c_pair[l, 0] + c_pair[l, 1]
-        spread(c_all.at[l, chip], c_send.at[l], c_recv.at[l], plane_peers)
+        spread(c_all.at[l, chip], ring(c_send, l), ring(c_recv, l), plane_peers)
 
     def stage_moments(l):
         @pl.when(l < last)
         def _():
-            drain(c_all.at[l, 0:chips - 1], c_recv.at[l])
+            drain(c_all.at[l, 0:chips - 1], ring(c_recv, l))
+            drain(c_all.at[l, 0:chips - 1], ring(c_send, l))
 
         @pl.when(l == last)
         def _():
-            drain(c_last.at[0:ds - 1], c_recv.at[l])
+            drain(c_last.at[0:ds - 1], last_recv)
             for k in range(chips):
                 c_all[l, k] = c_last[2 * k] + c_last[2 * k + 1]
 
         if zs > 1:
-            drain(r_all.at[l, 0:zs - 1], r_recv.at[l])
-        drain(w_buf.at[l], w_sem.at[l])
+            drain(r_all.at[l, 0:zs - 1], ring(r_recv, l))
+            drain(r_all.at[l, 0:zs - 1], ring(r_send, l))
+        drain(w_buf.at[l], ring(w_sem, l))
         r_new = DECAY * r_pad[pl.ds(l, 1)] + (1.0 - DECAY) * (total(r_all.at[l]) / cols_total)
         c_new = DECAY * c_buf[pl.ds(l, 1)] + (1.0 - DECAY) * (total(c_all.at[l]) / rows_total)
         r_pad[pl.ds(l, 1)] = r_new
@@ -248,15 +251,17 @@
         row = jnp.where(lane == 1, jnp.sum(w_acc, axis=1, keepdims=True), row)
         row = jnp.where(lane == 2, jnp.sum(r_new, axis=1, keepdims=True), row)
         s_all[l, 2 * z + core] = row
-        spread(s_all.at[l, 2 * z + core], s_send.at[l], s_recv.at[l], column_peers)
+        spread(s_all.at[l, 2 * z + core], ring(s_send, l), ring(s_recv, l), column_peers)
 
     def stage_gather(l):
-        drain(s_all.at[l, 0:2 * zs - 1], s_recv.at[l])
+        drain(s_all.at[l, 0:2 * zs - 1], ring(s_recv, l))
+        drain(s_all.at[l, 0:2 * zs - 1], ring(s_send, l))
         t_all[l, chip] = total(s_all.at[l])
-        spread(t_all.at[l, chip], t_send.at[l], t_recv.at[l], plane_peers)
+        spread(t_all.at[l, chip], ring(t_send, l), ring(t_recv, l), plane_peers)
 
     def stage_update(l):
-        drain(t_all.at[l, 0:chips - 1], t_recv.at[l])
+        drain(t_all.at[l, 0:chips - 1], ring(t_recv, l))
+        drain(t_all.at[l, 0:chips - 1], ring(t_send, l))
         sums = total(t_all.at[l])
         count = rows_total * cols_total
         r_mean = sums[:, 2:3] / (rows_total * zs)
@@ -271,26 +276,8 @@
             w_buf[l, :, sl] = w_buf[l, :, sl] - scale * u
 
     def drain_bulk(l):
-        drain(peer.at[l], pair_send.at[l])
-        x1(l).wait_send()
-        y1(l).wait_send()
-        x2(l).wait_send()
-        y2(l).wait_send()
-
-    def drain_sums(l):
-        if zs > 1:
-            drain(r_all.at[l, 0:zs - 1], r_send.at[l])
-
-        @pl.when(l < last)
-        def _():
-            drain(c_all.at[l, 0:chips - 1], c_send.at[l])
-
-        @pl.when(l == last)
-        def _():
-            drain(c_last.at[0:ds - 1], c_send.at[l])
-
-        drain(s_all.at[l, 0:2 * zs - 1], s_send.at[l])
-        drain(t_all.at[l, 0:chips - 1], t_send.at[l])
+        drain(in1x.at[0:2], ring(one_send, l))
+        drain(in2.at[l], ring(two_send, l))
 
     def at(i, lag, stage):
         @pl.when((i >= lag) & (i < layers + lag))
@@ -311,7 +298,6 @@
         @pl.when(i < layers)
         def _():
             stage_combine(i)
-            pltpu.make_async_copy(w_hbm.at[i], w_buf.at[i], w_sem.at[i]).start()
 
         at(i, 1, stage_forward)
         once(i, 1, norm_split)
@@ -325,15 +311,13 @@
         at(i, 5, stage_gather)
         at(i, 6, stage_update)
         at(i, 4, drain_bulk)
-        at(i, 7, drain_sums)
         once(i, 4, norm_stats)
         once(i, 6, norm_update)
         at(i, 2, stage_stats)
         return carry
 
     lax.fori_loop(0, layers + 6, body, 0)
-    for l in range(last, layers):
-        drain_sums(l)
+    drain(c_last.at[0:ds - 1], last_send)
     drain(h_all.at[0:chips - 1], h_send.at[1])
     drain(k_all.at[0:ds - 1], k_send)
 
@@ -394,8 +378,8 @@
                 pltpu.VMEM((ds // 2, layers, LANES), f32),
                 pltpu.VMEM((ds // 2, layers, LANES), f32),
                 pltpu.VMEM((ds, 1, 2 * LANES), f32),
-                *[dma((layers,))] * 24,
-                dma((5,)), dma((2,)), dma((2,)), dma, dma,
+                *[dma((n,)) for n in (4, 4, 8, 8, 8, 4, 4, 4, 4, 4, 4, 2, 4, 2, 2, 2, 4, 2, 4, 2, 4, 4)],
+                dma((5,)), dma((2,)), dma((2,)), dma, dma, dma, dma,
             ],
             compiler_params=pltpu.CompilerParams(collective_id=0, has_side_effects=True, vmem_limit_bytes=54 * 1000 * 1000),
             name='adafactor_step',

time: 183 us -> 180 us (0.984)
  Pallas kernels: 182 us -> 179 us
    pallas_call x1, Pallas kernels: 179 us -> 177 us  [local_step(): pl.pallas_call(step_kernel, out_shape=[pltpu.VMEM(a.shape, f32) for a in...]
where the time goes in v4:
time: 180 us
  Pallas kernels  179 us (99%)
    pallas_call x1, Pallas kernels, local_step(): pl.pallas_call(step_kernel, out_shape=[pltpu.VMEM(a.shape, f32) for a in...  177 us

profile of v4, /device:TPU:0, one launch (start us, length us, event | category | flops | bytes accessed | tf_op | source)
XLA Modules:
  0.0 180.3 jit_solution(10432870088104025542)
XLA Ops:
  1.3 176.8 %adafactor_step.1 = (f32[16,96,768]{2,1,0:T(8,128)S(1)}, f32[16,96]{1,0:T(8,128)S(1)}, f32[16,768]{1,0:T(8,128)S(1)}, f32[16,96]{1,0:T(8,128)S(1)}, f32[16,96]{1,0:T(8,128)S(1)}) custom-call(f32[16,96,768]{2,1,0:T(8,128)} %w_hbm.1, f32[16,8,96,768]{3,2,1,0:T(8,128)} %bitcast.3, f32[16,96]{1,0:T(8,128)} %r_hbm.1, f32[16,768]{1,0:T(8,128)} %c_hbm.1, ...), custom_call_target="tpu_custom_call" | custom-call | tf_op jit(solution)/shard_map/adafactor_step/pallas_call | solution.py:358
  178.1 2.2 %write_out.1 = (f32[16,96,768]{2,1,0:T(8,128)}, f32[16,96]{1,0:T(8,128)}, f32[16,768]{1,0:T(8,128)}, f32[16,96]{1,0:T(8,128)}, f32[16,96]{1,0:T(8,128)}) custom-call(f32[16,96,768]{2,1,0:T(8,128)S(1)} %get-tuple-element.10.refs_0_, f32[16,96]{1,0:T(8,128)S(1)} %get-tuple-element.11.refs_1_, f32[16,768]{1,0:T(8,128)S(1)} %get-tuple-element.12.refs_2_, ...), custom_call_target="tpu_custom_call" | custom-call | tf_op jit(solution)/shard_map/write_out/pallas_call | solution.py:336

commit v5 on v4

--- a/solution.py
+++ b/solution.py
@@ -16,20 +16,22 @@
 MESH = pl.DeviceIdType.MESH
 LANES = 128
 AHEAD = 2
+DIRECT = 2
 
 
 def step_kernel(w_hbm, g_hbm, r_hbm, c_hbm, n_hbm, ng_hbm, v_hbm, lr_ref,
                 w_buf, r_buf, c_buf, n_buf, v_buf,
                 own, peer, in1x, in1y, in2, ng_buf, r_pad,
-                r_all, c_pair, c_all, c_last, s_all, t_all, h_out, h_pair, h_all, k_all,
-                load_sem, pair_send, pair_x, pair_y, pair_rest,
-                one_send, x1_recv, y1_recv, two_send, x2_recv, y2_recv,
-                r_send, r_recv, cp_send, cp_recv, c_send, c_recv, s_send, s_recv, t_send, t_recv, w_sem,
-                small_sem, h_send, h_recv, k_send, k_recv, last_send, last_recv):
+                r_all, c_mine, c_pair, c_all, c_full, c_last, s_all, t_all, t_last, h_out, h_pair, h_all, k_all,
+                load_sem, stage_sem, first_recv, pair_send, pair_recv, one_send, one_recv, two_send, two_recv,
+                r_send, r_recv, cp_send, cp_recv, c_send, c_recv, cf_send, cf_recv,
+                s_send, s_recv, t_send, t_recv, w_sem,
+                cl_send, cl_recv, tl_send, tl_recv, small_sem, h_send, h_recv, k_send, k_recv):
     layers, _, rows, cols = own.shape
     half = rows // 2
-    last = layers - 1
-    zs, ds = r_all.shape[1], c_last.shape[0]
+    direct, ds = c_last.shape[0], c_last.shape[1]
+    late = layers - direct
+    zs = r_all.shape[1]
     chips = ds // 2
     rows_total, cols_total = rows * ds, cols * zs
     z = lax.axis_index('model')
@@ -44,6 +46,7 @@
     d_peers = [{'dp': e} for e in (dc, dx, dx + dc - d, dy, dy + dc - d, dxy, dxy + dc - d)]
     column_peers = [{'dp': dc}] + [{'model': p['model'], 'dp': e} for p in z_peers for e in (d, dc)]
     plane_peers = [{'dp': e} for e in (dx, dy, dxy)]
+    others = [{'model': p['model'], **q} for q in d_peers[::-1] for p in z_peers] + d_peers[::-1] + z_peers
 
     def ring(sem, l):
         return sem.at[lax.rem(l, sem.shape[0])]
@@ -63,33 +66,34 @@
         for k in range(4):
             pltpu.make_async_copy(g_hbm.at[l, blocks[k]], own.at[l, k], ring(load_sem, l)).start()
 
-    def send_pair(l, source):
-        pieces = ((0, 0, pair_x), (1, 0, pair_x), (1, half, pair_y), (2, half, pair_y),
-                  (0, half, pair_rest), (2, 0, pair_rest), (3, 0, pair_rest), (3, half, pair_rest))
-        for k, row, recv in pieces:
-            part = pl.ds(row, half)
-            remote(source(k).at[part], peer.at[l, k, part], ring(pair_send, l), ring(recv, l), {'dp': dc}).start()
-
-    def from_hbm(l):
-        return lambda k: g_hbm.at[l, blocks[k] + dc - d]
+    def pair_copy(l, k, row, source, recv):
+        part = pl.ds(row, half)
+        return remote(source.at[part], peer.at[l, k, part], ring(pair_send, l), recv, {'dp': dc})
+
+    def from_hbm(l, k):
+        return g_hbm.at[l, blocks[k] + dc - d]
+
+    def send_pair(l):
+        for k in range(4):
+            remote(from_hbm(l, k), peer.at[l, k], ring(pair_send, l), ring(pair_recv, l), {'dp': dc}).start()
 
     def x1(l):
-        return remote(own.at[l, 0:2, 0:half], in1x.at[l], ring(one_send, l), ring(x1_recv, l), {'dp': dx})
+        return remote(own.at[l, 0:2, 0:half], in1x.at[l], ring(one_send, l), ring(one_recv, l), {'dp': dx})
 
     def y1(l):
-        return remote(own.at[l, 1:3, half:rows], in1y.at[l], ring(one_send, l), ring(y1_recv, l), {'dp': dy})
+        return remote(own.at[l, 1:3, half:rows], in1y.at[l], ring(one_send, l), ring(one_recv, l), {'dp': dy})
 
     def y2(l):
-        return remote(own.at[l, 2, 0:half], in2.at[l, 0], ring(two_send, l), ring(y2_recv, l), {'dp': dy})
+        return remote(own.at[l, 2, 0:half], in2.at[l, 0], ring(two_send, l), ring(two_recv, l), {'dp': dy})
 
     def x2(l):
-        return remote(own.at[l, 0, half:rows], in2.at[l, 1], ring(two_send, l), ring(x2_recv, l), {'dp': dx})
+        return remote(own.at[l, 0, half:rows], in2.at[l, 1], ring(two_send, l), ring(two_recv, l), {'dp': dx})
 
     def total(buf):
-        acc = buf[0]
-        for j in range(1, buf.shape[0]):
-            acc = acc + buf[j]
-        return acc
+        parts = [buf[j] for j in range(buf.shape[0])]
+        while len(parts) > 1:
+            parts = [a + b for a, b in zip(parts[::2], parts[1::2])]
+        return parts[0]
 
     def column(row):
         return jnp.transpose(jnp.broadcast_to(row, (LANES, LANES)))[0:rows]
@@ -101,22 +105,31 @@
         return acc
 
     small = ((r_hbm, r_buf), (c_hbm, c_buf), (n_hbm, n_buf), (ng_hbm, ng_buf), (v_hbm, v_buf))
-    for k in range(4):
-        pltpu.make_async_copy(g_hbm.at[0, blocks[k] + dc - d], own.at[last, k], load_sem.at[AHEAD]).start()
+    groups = (((0, 0), (1, 0)), ((1, half), (2, half)))
+    for i, group in enumerate(groups):
+        for k, row in group:
+            part = pl.ds(row, half)
+            pltpu.make_async_copy(from_hbm(0, k).at[part], own.at[layers - 1, i, pl.ds((k - i) * half, half)], stage_sem.at[i]).start()
     for l in range(AHEAD):
         load_own(l)
     for i, (src, dst) in enumerate(small):
         pltpu.make_async_copy(src, dst, small_sem.at[i]).start()
 
     barrier = pltpu.get_barrier_semaphore()
-    everyone = d_peers + column_peers
-    for where in everyone:
+    known = d_peers + column_peers[1:]
+    for where in known:
         pl.semaphore_signal(barrier, inc=1, device_id=where, device_id_type=MESH)
-    pl.semaphore_wait(barrier, len(everyone))
-    drain(own.at[last], load_sem.at[AHEAD])
-    send_pair(0, lambda k: own.at[last, k])
+    pl.semaphore_wait(barrier, len(known))
+    for i, group in enumerate(groups):
+        drain(own.at[layers - 1, i], stage_sem.at[i])
+        for k, row in group:
+            part = pl.ds(row, half)
+            remote(own.at[layers - 1, i, pl.ds((k - i) * half, half)], peer.at[0, k, part],
+                   pair_send.at[0], first_recv.at[i], {'dp': dc}).start()
+    for k, row in ((0, half), (2, 0), (3, 0), (3, half)):
+        pair_copy(0, k, row, from_hbm(0, k), first_recv.at[2]).start()
     for l in range(1, AHEAD):
-        send_pair(l, from_hbm(l))
+        send_pair(l)
 
     def norm_split():
         for i, (src, dst) in enumerate(small):
@@ -163,24 +176,40 @@
         zv = total(h_all)[:, 0:rows] * lax.rsqrt(v_buf[...])
         n_buf[...] = n_buf[...] - scale * (zv / clip)
 
+    def combine(l, k, part):
+        own[l, k, part] = own[l, k, part] + peer[l, k, part]
+
+    first, second = slice(0, half), slice(half, rows)
+
+    def stage_first():
+        drain(own.at[0], load_sem.at[0])
+        drain(in1x.at[0], first_recv.at[0])
+        combine(0, slice(0, 2), first)
+        x1(0).start()
+        drain(in1y.at[0], first_recv.at[1])
+        combine(0, slice(1, 3), second)
+        y1(0).start()
+        drain(peer.at[0, 0:2], first_recv.at[2])
+        combine(0, 0, second)
+        combine(0, 2, first)
+        combine(0, 3, slice(0, rows))
+        drain(peer.at[0], pair_send.at[0])
+
     def stage_combine(l):
         drain(own.at[l], ring(load_sem, l))
-        drain(in1x.at[l], ring(pair_x, l))
-        own[l, 0:2, 0:half] = own[l, 0:2, 0:half] + peer[l, 0:2, 0:half]
+        drain(peer.at[l], ring(pair_recv, l))
+        combine(l, slice(0, 2), first)
         x1(l).start()
-        drain(in1y.at[l], ring(pair_y, l))
-        own[l, 1:3, half:rows] = own[l, 1:3, half:rows] + peer[l, 1:3, half:rows]
+        combine(l, slice(1, 3), second)
         y1(l).start()
-        drain(peer.at[l, 0:2], ring(pair_rest, l))
-        own[l, 0, half:rows] = own[l, 0, half:rows] + peer[l, 0, half:rows]
-        own[l, 2, 0:half] = own[l, 2, 0:half] + peer[l, 2, 0:half]
-        own[l, 3] = own[l, 3] + peer[l, 3]
+        combine(l, 0, second)
+        combine(l, 2, first)
+        combine(l, 3, slice(0, rows))
         drain(peer.at[l], ring(pair_send, l))
 
     def stage_forward(l):
-        x1(l).wait_recv()
+        drain(in1x.at[0:2], ring(one_recv, l))
         own[l, 2, 0:half] = own[l, 2, 0:half] + in1x[l, 1]
-        y1(l).wait_recv()
         own[l, 0, half:rows] = own[l, 0, half:rows] + in1y[l, 0]
         y2(l).start()
         own[l, 3, 0:half] = own[l, 3, 0:half] + in1x[l, 0]
@@ -189,50 +218,73 @@
 
     def stage_stats(l):
         pltpu.make_async_copy(w_hbm.at[l], w_buf.at[l], ring(w_sem, l)).start()
-        y2(l).wait_recv()
-        x2(l).wait_recv()
+        drain(in2.at[l], ring(two_recv, l))
         g = own[l, 3] + in2[l].reshape(rows, cols)
         own[l, 3] = g
         q = g * g + EPS_FLOOR
         col = jnp.sum(q, axis=0, keepdims=True)
-        c_pair[l, core] = col
-        c_last[d] = col
+
+        @pl.when(l < late)
+        def _():
+            c_mine[l, 0] = col[:, 0:cols // 2]
+            c_mine[l, 1] = col[:, cols // 2:cols]
+
+        @pl.when(l >= late)
+        def _():
+            c_last[l - late, d] = col
+
         p = jnp.concatenate([fold(q), jnp.zeros((LANES - rows, LANES), jnp.float32)], axis=0)
         r_all[l, z] = jnp.sum(jnp.transpose(p), axis=0, keepdims=True)
 
-        @pl.when(l < last)
-        def _():
-            spread(c_pair.at[l, core], ring(cp_send, l), ring(cp_recv, l), [{'dp': dc}])
-
-        @pl.when(l == last)
-        def _():
-            spread(c_last.at[d], last_send, last_recv, d_peers)
+        @pl.when(l < late)
+        def _():
+            pair_columns(l).start()
+
+        @pl.when(l >= late)
+        def _():
+            e = l - late
+            spread(c_last.at[e, d], cl_send.at[e], cl_recv.at[e], d_peers)
 
         spread(r_all.at[l, z], ring(r_send, l), ring(r_recv, l), z_peers)
 
+    def pair_columns(l):
+        return remote(c_mine.at[l, 1 - core], c_pair.at[l], ring(cp_send, l), ring(cp_recv, l), {'dp': dc})
+
+    def full_columns(l):
+        return remote(c_full.at[l, core], c_full.at[l, core], ring(cf_send, l), ring(cf_recv, l), {'dp': dc})
+
     def stage_columns(l):
-        remote(c_pair.at[l, core], c_pair.at[l, core], ring(cp_send, l), ring(cp_recv, l), {'dp': dc}).wait()
-        c_all[l, chip] = c_pair[l, 0] + c_pair[l, 1]
+        pair_columns(l).wait()
+        c_all[l, chip] = c_mine[l, core] + c_pair[l]
         spread(c_all.at[l, chip], ring(c_send, l), ring(c_recv, l), plane_peers)
 
+    def stage_share(l):
+        drain(c_all.at[l, 0:chips - 1], ring(c_recv, l))
+        drain(c_all.at[l, 0:chips - 1], ring(c_send, l))
+        c_full[l, core] = total(c_all.at[l])
+        full_columns(l).start()
+
     def stage_moments(l):
-        @pl.when(l < last)
-        def _():
-            drain(c_all.at[l, 0:chips - 1], ring(c_recv, l))
-            drain(c_all.at[l, 0:chips - 1], ring(c_send, l))
-
-        @pl.when(l == last)
-        def _():
-            drain(c_last.at[0:ds - 1], last_recv)
-            for k in range(chips):
-                c_all[l, k] = c_last[2 * k] + c_last[2 * k + 1]
+        @pl.when(l < late)
+        def _():
+            full_columns(l).wait()
+
+        @pl.when(l >= late)
+        def _():
+            e = l - late
+            drain(c_last.at[e, 0:ds - 1], cl_recv.at[e])
+            drain(c_last.at[e, 0:ds - 1], cl_send.at[e])
+            col = total(c_last.at[e])
+            c_full[l, 0] = col[:, 0:cols // 2]
+            c_full[l, 1] = col[:, cols // 2:cols]
 
         if zs > 1:
             drain(r_all.at[l, 0:zs - 1], ring(r_recv, l))
             drain(r_all.at[l, 0:zs - 1], ring(r_send, l))
         drain(w_buf.at[l], ring(w_sem, l))
+        col = jnp.concatenate([c_full[l, 0], c_full[l, 1]], axis=1)
         r_new = DECAY * r_pad[pl.ds(l, 1)] + (1.0 - DECAY) * (total(r_all.at[l]) / cols_total)
-        c_new = DECAY * c_buf[pl.ds(l, 1)] + (1.0 - DECAY) * (total(c_all.at[l]) / rows_total)
+        c_new = DECAY * c_buf[pl.ds(l, 1)] + (1.0 - DECAY) * (col / rows_total)
         r_pad[pl.ds(l, 1)] = r_new
         r_buf[pl.ds(l, 1)] = r_new[:, 0:rows]
         c_buf[pl.ds(l, 1)] = c_new
@@ -250,8 +302,18 @@
         row = jnp.where(lane == 0, jnp.sum(acc, axis=1, keepdims=True), 0.0)
         row = jnp.where(lane == 1, jnp.sum(w_acc, axis=1, keepdims=True), row)
         row = jnp.where(lane == 2, jnp.sum(r_new, axis=1, keepdims=True), row)
-        s_all[l, 2 * z + core] = row
-        spread(s_all.at[l, 2 * z + core], ring(s_send, l), ring(s_recv, l), column_peers)
+
+        @pl.when(l < late)
+        def _():
+            s_all[l, 2 * z + core] = row
+            spread(s_all.at[l, 2 * z + core], ring(s_send, l), ring(s_recv, l), column_peers)
+
+        @pl.when(l >= late)
+        def _():
+            e = l - late
+            me = ds * z + d
+            t_last[e, me] = row
+            spread(t_last.at[e, me], tl_send.at[e], tl_recv.at[e], others)
 
     def stage_gather(l):
         drain(s_all.at[l, 0:2 * zs - 1], ring(s_recv, l))
@@ -262,7 +324,14 @@
     def stage_update(l):
         drain(t_all.at[l, 0:chips - 1], ring(t_recv, l))
         drain(t_all.at[l, 0:chips - 1], ring(t_send, l))
-        sums = total(t_all.at[l])
+        apply(l, total(t_all.at[l]))
+
+    def stage_final(e):
+        drain(t_last.at[e, 0:ds * zs - 1], tl_recv.at[e])
+        drain(t_last.at[e, 0:ds * zs - 1], tl_send.at[e])
+        apply(e + late, total(t_last.at[e]))
+
+    def apply(l, sums):
         count = rows_total * cols_total
         r_mean = sums[:, 2:3] / (rows_total * zs)
         u_rms = jnp.sqrt(sums[:, 0:1] / count * r_mean)
@@ -279,8 +348,8 @@
         drain(in1x.at[0:2], ring(one_send, l))
         drain(in2.at[l], ring(two_send, l))
 
-    def at(i, lag, stage):
-        @pl.when((i >= lag) & (i < layers + lag))
+    def at(i, lag, stage, begin=0, end=layers):
+        @pl.when((i >= begin + lag) & (i < end + lag))
         def _():
             stage(i - lag)
 
@@ -289,35 +358,31 @@
         def _():
             stage()
 
+    def prefetch(l):
+        load_own(l)
+        send_pair(l)
+
     def body(i, carry):
-        @pl.when(i + AHEAD < layers)
-        def _():
-            load_own(i + AHEAD)
-            send_pair(i + AHEAD, from_hbm(i + AHEAD))
-
-        @pl.when(i < layers)
-        def _():
-            stage_combine(i)
-
+        at(i, -AHEAD, prefetch)
+        at(i, 0, stage_combine, 1)
+        once(i, 0, stage_first)
         at(i, 1, stage_forward)
         once(i, 1, norm_split)
         once(i, 2, norm_send)
-
-        @pl.when((i >= 3) & (i < last + 3))
-        def _():
-            stage_columns(i - 3)
-
-        at(i, 4, stage_moments)
-        at(i, 5, stage_gather)
-        at(i, 6, stage_update)
+        at(i, 3, stage_columns, 0, late)
+        at(i, 4, stage_share, 0, late)
+        at(i, 5, stage_moments)
+        at(i, 7, stage_gather, 0, late)
+        at(i, 8, stage_update, 0, late)
         at(i, 4, drain_bulk)
         once(i, 4, norm_stats)
         once(i, 6, norm_update)
         at(i, 2, stage_stats)
         return carry
 
-    lax.fori_loop(0, layers + 6, body, 0)
-    drain(c_last.at[0:ds - 1], last_send)
+    lax.fori_loop(0, late + 8, body, 0)
+    for e in range(direct):
+        stage_final(e)
     drain(h_all.at[0:chips - 1], h_send.at[1])
     drain(k_all.at[0:ds - 1], k_send)
 
@@ -369,17 +434,20 @@
                 pltpu.VMEM(norm_grads.shape, f32),
                 pltpu.VMEM((layers, LANES), f32),
                 pltpu.VMEM((layers, zs, 1, LANES), f32),
-                pltpu.VMEM((layers, 2, 1, cols), f32),
-                pltpu.VMEM((layers, ds // 2, 1, cols), f32),
-                pltpu.VMEM((ds, 1, cols), f32),
+                pltpu.VMEM((layers, 2, 1, cols // 2), f32),
+                pltpu.VMEM((layers, 1, cols // 2), f32),
+                pltpu.VMEM((layers, ds // 2, 1, cols // 2), f32),
+                pltpu.VMEM((layers, 2, 1, cols // 2), f32),
+                pltpu.VMEM((DIRECT, ds, 1, cols), f32),
                 pltpu.VMEM((layers, 2 * zs, 1, LANES), f32),
                 pltpu.VMEM((layers, ds // 2, 1, LANES), f32),
+                pltpu.VMEM((DIRECT, ds * zs, 1, LANES), f32),
                 pltpu.VMEM((ds // 2, 2, layers, LANES), f32),
                 pltpu.VMEM((ds // 2, layers, LANES), f32),
                 pltpu.VMEM((ds // 2, layers, LANES), f32),
                 pltpu.VMEM((ds, 1, 2 * LANES), f32),
-                *[dma((n,)) for n in (4, 4, 8, 8, 8, 4, 4, 4, 4, 4, 4, 2, 4, 2, 2, 2, 4, 2, 4, 2, 4, 4)],
-                dma((5,)), dma((2,)), dma((2,)), dma, dma, dma, dma,
+                *[dma((n,)) for n in (3, 2, 3, 3, 4, 4, 4, 4, 4, 3, 6, 2, 2, 2, 4, 2, 4, 3, 6, 2, 4, 3)],
+                *[dma((DIRECT,))] * 4, dma((5,)), dma((2,)), dma((2,)), dma, dma,
             ],
             compiler_params=pltpu.CompilerParams(collective_id=0, has_side_effects=True, vmem_limit_bytes=54 * 1000 * 1000),
             name='adafactor_step',

time: 180 us -> 177 us (0.983)
  Pallas kernels: 179 us -> 176 us
    pallas_call x1, Pallas kernels: 177 us -> 174 us  [local_step(): pl.pallas_call(step_kernel, out_shape=[pltpu.VMEM(a.shape, f32) for a in...]
where the time goes in v5:
time: 177 us
  Pallas kernels  176 us (99%)
    pallas_call x1, Pallas kernels, local_step(): pl.pallas_call(step_kernel, out_shape=[pltpu.VMEM(a.shape, f32) for a in...  174 us

profile of v5, /device:TPU:0, one launch (start us, length us, event | category | flops | bytes accessed | tf_op | source)
XLA Modules:
  0.0 177.1 jit_solution(12974770571413455247)
XLA Ops:
  1.3 173.5 %adafactor_step.1 = (f32[16,96,768]{2,1,0:T(8,128)S(1)}, f32[16,96]{1,0:T(8,128)S(1)}, f32[16,768]{1,0:T(8,128)S(1)}, f32[16,96]{1,0:T(8,128)S(1)}, f32[16,96]{1,0:T(8,128)S(1)}) custom-call(f32[16,96,768]{2,1,0:T(8,128)} %w_hbm.1, f32[16,8,96,768]{3,2,1,0:T(8,128)} %bitcast.3, f32[16,96]{1,0:T(8,128)} %r_hbm.1, f32[16,768]{1,0:T(8,128)} %c_hbm.1, ...), custom_call_target="tpu_custom_call" | custom-call | tf_op jit(solution)/shard_map/adafactor_step/pallas_call | solution.py:423
  174.8 2.2 %write_out.1 = (f32[16,96,768]{2,1,0:T(8,128)}, f32[16,96]{1,0:T(8,128)}, f32[16,768]{1,0:T(8,128)}, f32[16,96]{1,0:T(8,128)}, f32[16,96]{1,0:T(8,128)}) custom-call(f32[16,96,768]{2,1,0:T(8,128)S(1)} %get-tuple-element.10.refs_0_, f32[16,96]{1,0:T(8,128)S(1)} %get-tuple-element.11.refs_1_, f32[16,768]{1,0:T(8,128)S(1)} %get-tuple-element.12.refs_2_, ...), custom_call_target="tpu_custom_call" | custom-call | tf_op jit(solution)/shard_map/write_out/pallas_call | solution.py:401

commit v6 on v5

--- a/solution.py
+++ b/solution.py
@@ -19,9 +19,9 @@
 DIRECT = 2
 
 
-def step_kernel(w_hbm, g_hbm, r_hbm, c_hbm, n_hbm, ng_hbm, v_hbm, lr_ref,
-                w_buf, r_buf, c_buf, n_buf, v_buf,
-                own, peer, in1x, in1y, in2, ng_buf, r_pad,
+def step_kernel(w_hbm, g_hbm, r_hbm, c_hbm, n_hbm, ng_hbm, v_hbm,
+                w_buf, d_buf, r_buf, c_buf, n_buf, dn_buf, v_buf,
+                own, peer, in1x, in1y, in2, ng_buf, r_pad, w_sq,
                 r_all, c_mine, c_pair, c_all, c_full, c_last, s_all, t_all, t_last, h_out, h_pair, h_all, k_all,
                 load_sem, stage_sem, first_recv, pair_send, pair_recv, one_send, one_recv, two_send, two_recv,
                 r_send, r_recv, cp_send, cp_recv, c_send, c_recv, cf_send, cf_recv,
@@ -29,8 +29,8 @@
                 cl_send, cl_recv, tl_send, tl_recv, small_sem, h_send, h_recv, k_send, k_recv):
     layers, _, rows, cols = own.shape
     half = rows // 2
-    direct, ds = c_last.shape[0], c_last.shape[1]
-    late = layers - direct
+    last, ds = layers - 1, c_last.shape[0]
+    late = layers - DIRECT
     zs = r_all.shape[1]
     chips = ds // 2
     rows_total, cols_total = rows * ds, cols * zs
@@ -63,8 +63,9 @@
         pltpu.make_async_copy(ref, ref, sem).wait()
 
     def load_own(l):
-        for k in range(4):
+        for k in range(3):
             pltpu.make_async_copy(g_hbm.at[l, blocks[k]], own.at[l, k], ring(load_sem, l)).start()
+        pltpu.make_async_copy(g_hbm.at[l, d], d_buf.at[l], ring(load_sem, l)).start()
 
     def pair_copy(l, k, row, source, recv):
         part = pl.ds(row, half)
@@ -110,8 +111,7 @@
         for k, row in group:
             part = pl.ds(row, half)
             pltpu.make_async_copy(from_hbm(0, k).at[part], own.at[layers - 1, i, pl.ds((k - i) * half, half)], stage_sem.at[i]).start()
-    for l in range(AHEAD):
-        load_own(l)
+    load_own(0)
     for i, (src, dst) in enumerate(small):
         pltpu.make_async_copy(src, dst, small_sem.at[i]).start()
 
@@ -130,6 +130,7 @@
         pair_copy(0, k, row, from_hbm(0, k), first_recv.at[2]).start()
     for l in range(1, AHEAD):
         send_pair(l)
+        load_own(l)
 
     def norm_split():
         for i, (src, dst) in enumerate(small):
@@ -170,11 +171,11 @@
         acc = total(k_all)
         z_sq, n_sq = acc[:, 0:layers], acc[:, LANES:LANES + layers]
         clip = jnp.maximum(1.0, jnp.sqrt(z_sq / rows_total) / CLIP_LIMIT)
-        scale = lr_ref[0, 0] * jnp.maximum(SCALE_FLOOR, jnp.sqrt(n_sq / rows_total))
+        scale = jnp.maximum(SCALE_FLOOR, jnp.sqrt(n_sq / rows_total))
         clip = jnp.transpose(jnp.broadcast_to(clip, (LANES, layers)))[:, 0:rows]
         scale = jnp.transpose(jnp.broadcast_to(scale, (LANES, layers)))[:, 0:rows]
         zv = total(h_all)[:, 0:rows] * lax.rsqrt(v_buf[...])
-        n_buf[...] = n_buf[...] - scale * (zv / clip)
+        dn_buf[...] = scale * (zv / clip)
 
     def combine(l, k, part):
         own[l, k, part] = own[l, k, part] + peer[l, k, part]
@@ -182,7 +183,7 @@
     first, second = slice(0, half), slice(half, rows)
 
     def stage_first():
-        drain(own.at[0], load_sem.at[0])
+        drain(peer.at[0], load_sem.at[0])
         drain(in1x.at[0], first_recv.at[0])
         combine(0, slice(0, 2), first)
         x1(0).start()
@@ -192,11 +193,11 @@
         drain(peer.at[0, 0:2], first_recv.at[2])
         combine(0, 0, second)
         combine(0, 2, first)
-        combine(0, 3, slice(0, rows))
+        d_buf[0] = d_buf[0] + peer[0, 3]
         drain(peer.at[0], pair_send.at[0])
 
     def stage_combine(l):
-        drain(own.at[l], ring(load_sem, l))
+        drain(peer.at[l], ring(load_sem, l))
         drain(peer.at[l], ring(pair_recv, l))
         combine(l, slice(0, 2), first)
         x1(l).start()
@@ -204,46 +205,48 @@
         y1(l).start()
         combine(l, 0, second)
         combine(l, 2, first)
-        combine(l, 3, slice(0, rows))
+        d_buf[l] = d_buf[l] + peer[l, 3]
         drain(peer.at[l], ring(pair_send, l))
 
     def stage_forward(l):
+        pltpu.make_async_copy(w_hbm.at[l], w_buf.at[l], ring(w_sem, l)).start()
         drain(in1x.at[0:2], ring(one_recv, l))
         own[l, 2, 0:half] = own[l, 2, 0:half] + in1x[l, 1]
         own[l, 0, half:rows] = own[l, 0, half:rows] + in1y[l, 0]
         y2(l).start()
-        own[l, 3, 0:half] = own[l, 3, 0:half] + in1x[l, 0]
+        d_buf[l, 0:half] = d_buf[l, 0:half] + in1x[l, 0]
         x2(l).start()
-        own[l, 3, half:rows] = own[l, 3, half:rows] + in1y[l, 1]
+        d_buf[l, half:rows] = d_buf[l, half:rows] + in1y[l, 1]
 
     def stage_stats(l):
-        pltpu.make_async_copy(w_hbm.at[l], w_buf.at[l], ring(w_sem, l)).start()
+        drain(w_buf.at[l], ring(w_sem, l))
+        w = w_buf[l]
+        w_sq[pl.ds(l, 1)] = fold(jnp.sum(w * w, axis=0, keepdims=True))
         drain(in2.at[l], ring(two_recv, l))
-        g = own[l, 3] + in2[l].reshape(rows, cols)
-        own[l, 3] = g
+        g = d_buf[l] + in2[l].reshape(rows, cols)
+        d_buf[l] = g
         q = g * g + EPS_FLOOR
         col = jnp.sum(q, axis=0, keepdims=True)
 
-        @pl.when(l < late)
+        @pl.when(l < last)
         def _():
             c_mine[l, 0] = col[:, 0:cols // 2]
             c_mine[l, 1] = col[:, cols // 2:cols]
 
-        @pl.when(l >= late)
-        def _():
-            c_last[l - late, d] = col
+        @pl.when(l == last)
+        def _():
+            c_last[d] = col
 
         p = jnp.concatenate([fold(q), jnp.zeros((LANES - rows, LANES), jnp.float32)], axis=0)
         r_all[l, z] = jnp.sum(jnp.transpose(p), axis=0, keepdims=True)
 
-        @pl.when(l < late)
+        @pl.when(l < last)
         def _():
             pair_columns(l).start()
 
-        @pl.when(l >= late)
-        def _():
-            e = l - late
-            spread(c_last.at[e, d], cl_send.at[e], cl_recv.at[e], d_peers)
+        @pl.when(l == last)
+        def _():
+            spread(c_last.at[d], cl_send, cl_recv, d_peers)
 
         spread(r_all.at[l, z], ring(r_send, l), ring(r_recv, l), z_peers)
 
@@ -265,23 +268,21 @@
         full_columns(l).start()
 
     def stage_moments(l):
-        @pl.when(l < late)
+        @pl.when(l < last)
         def _():
             full_columns(l).wait()
 
-        @pl.when(l >= late)
-        def _():
-            e = l - late
-            drain(c_last.at[e, 0:ds - 1], cl_recv.at[e])
-            drain(c_last.at[e, 0:ds - 1], cl_send.at[e])
-            col = total(c_last.at[e])
+        @pl.when(l == last)
+        def _():
+            drain(c_last.at[0:ds - 1], cl_recv)
+            drain(c_last.at[0:ds - 1], cl_send)
+            col = total(c_last)
             c_full[l, 0] = col[:, 0:cols // 2]
             c_full[l, 1] = col[:, cols // 2:cols]
 
         if zs > 1:
             drain(r_all.at[l, 0:zs - 1], ring(r_recv, l))
             drain(r_all.at[l, 0:zs - 1], ring(r_send, l))
-        drain(w_buf.at[l], ring(w_sem, l))
         col = jnp.concatenate([c_full[l, 0], c_full[l, 1]], axis=1)
         r_new = DECAY * r_pad[pl.ds(l, 1)] + (1.0 - DECAY) * (total(r_all.at[l]) / cols_total)
         c_new = DECAY * c_buf[pl.ds(l, 1)] + (1.0 - DECAY) * (col / rows_total)
@@ -291,16 +292,13 @@
         a = column(lax.rsqrt(r_new))
         b = lax.rsqrt(c_new)
         acc = jnp.zeros((1, LANES), jnp.float32)
-        w_acc = jnp.zeros((1, LANES), jnp.float32)
         for t in range(cols // LANES):
             sl = slice(t * LANES, (t + 1) * LANES)
-            u = own[l, 3, :, sl] * a * b[:, sl]
+            u = d_buf[l, :, sl] * a * b[:, sl]
             acc = acc + jnp.sum(u * u, axis=0, keepdims=True)
-            w = w_buf[l, :, sl]
-            w_acc = w_acc + jnp.sum(w * w, axis=0, keepdims=True)
         lane = lax.broadcasted_iota(jnp.int32, (1, LANES), 1)
         row = jnp.where(lane == 0, jnp.sum(acc, axis=1, keepdims=True), 0.0)
-        row = jnp.where(lane == 1, jnp.sum(w_acc, axis=1, keepdims=True), row)
+        row = jnp.where(lane == 1, jnp.sum(w_sq[pl.ds(l, 1)], axis=1, keepdims=True), row)
         row = jnp.where(lane == 2, jnp.sum(r_new, axis=1, keepdims=True), row)
 
         @pl.when(l < late)
@@ -336,13 +334,12 @@
         r_mean = sums[:, 2:3] / (rows_total * zs)
         u_rms = jnp.sqrt(sums[:, 0:1] / count * r_mean)
         clip = jnp.maximum(1.0, u_rms / CLIP_LIMIT)
-        scale = lr_ref[0, 0] * jnp.maximum(SCALE_FLOOR, jnp.sqrt(sums[:, 1:2] / count))
+        scale = jnp.maximum(SCALE_FLOOR, jnp.sqrt(sums[:, 1:2] / count))
         a = column(lax.rsqrt(r_pad[pl.ds(l, 1)] / r_mean))
-        b = lax.rsqrt(c_buf[pl.ds(l, 1)]) / clip
+        b = lax.rsqrt(c_buf[pl.ds(l, 1)])
         for t in range(cols // LANES):
             sl = slice(t * LANES, (t + 1) * LANES)
-            u = own[l, 3, :, sl] * a * b[:, sl]
-            w_buf[l, :, sl] = w_buf[l, :, sl] - scale * u
+            d_buf[l, :, sl] = d_buf[l, :, sl] * a * (b[:, sl] / clip) * scale
 
     def drain_bulk(l):
         drain(in1x.at[0:2], ring(one_send, l))
@@ -369,8 +366,8 @@
         at(i, 1, stage_forward)
         once(i, 1, norm_split)
         once(i, 2, norm_send)
-        at(i, 3, stage_columns, 0, late)
-        at(i, 4, stage_share, 0, late)
+        at(i, 3, stage_columns, 0, last)
+        at(i, 4, stage_share, 0, last)
         at(i, 5, stage_moments)
         at(i, 7, stage_gather, 0, late)
         at(i, 8, stage_update, 0, late)
@@ -381,32 +378,41 @@
         return carry
 
     lax.fori_loop(0, late + 8, body, 0)
-    for e in range(direct):
+    for e in range(DIRECT):
         stage_final(e)
     drain(h_all.at[0:chips - 1], h_send.at[1])
     drain(k_all.at[0:ds - 1], k_send)
 
 
-def write_kernel(*refs):
-    count = len(refs) // 2
-    pairs = list(zip(refs[:count], refs[count:2 * count]))
-    sem = refs[-1]
-    for i, (src, dst) in enumerate(pairs):
-        pltpu.make_async_copy(src, dst, sem.at[i]).start()
-    for i, (src, dst) in enumerate(pairs):
-        pltpu.make_async_copy(src, dst, sem.at[i]).wait()
-
-
-def write_out(arrays):
+def write_kernel(lr_ref, w, d, r, c, n, dn, v, wo, ro, co, no, vo, w_new, n_new, sem):
+    layers = w.shape[0]
+    rate = lr_ref[...]
+    pairs = ((r, ro), (c, co), (v, vo), (n_new, no))
+    for i in range(3):
+        pltpu.make_async_copy(*pairs[i], sem.at[i]).start()
+    n_new[...] = n[...] - rate * dn[...]
+    for l in range(layers + 1):
+        if l < layers:
+            w_new[l] = w[l] - rate * d[l]
+        if l == 1:
+            pltpu.make_async_copy(*pairs[3], sem.at[3]).start()
+        if l >= 1:
+            pltpu.make_async_copy(w_new.at[l - 1], wo.at[l - 1], sem.at[4]).start()
+    for i, pair in enumerate(pairs):
+        pltpu.make_async_copy(*pair, sem.at[i]).wait()
+    pltpu.make_async_copy(w_new, wo, sem.at[4]).wait()
+
+
+def write_out(rate, w, d, r, c, n, dn, v):
     return pl.pallas_call(
         write_kernel,
-        out_shape=[jax.ShapeDtypeStruct(a.shape, a.dtype) for a in arrays],
-        in_specs=[pl.BlockSpec(memory_space=pltpu.MemorySpace.VMEM)] * len(arrays),
-        out_specs=[pl.BlockSpec(memory_space=pltpu.MemorySpace.HBM)] * len(arrays),
-        scratch_shapes=[pltpu.SemaphoreType.DMA((len(arrays),))],
-        compiler_params=pltpu.CompilerParams(vmem_limit_bytes=1 << 20),
+        out_shape=[jax.ShapeDtypeStruct(a.shape, a.dtype) for a in (w, r, c, n, v)],
+        in_specs=[pl.BlockSpec(memory_space=pltpu.MemorySpace.SMEM)] + [pl.BlockSpec(memory_space=pltpu.MemorySpace.VMEM)] * 7,
+        out_specs=[pl.BlockSpec(memory_space=pltpu.MemorySpace.HBM)] * 5,
+        scratch_shapes=[pltpu.VMEM(w.shape, w.dtype), pltpu.VMEM(n.shape, n.dtype), pltpu.SemaphoreType.DMA((5,))],
+        compiler_params=pltpu.CompilerParams(vmem_limit_bytes=8 << 20),
         name='write_out',
-    )(*arrays)
+    )(rate, w, d, r, c, n, dn, v)
 
 
 def solution(mesh):
@@ -422,23 +428,24 @@
         dma = pltpu.SemaphoreType.DMA
         outs = pl.pallas_call(
             step_kernel,
-            out_shape=[pltpu.VMEM(a.shape, f32) for a in (weight, row_stat, col_stat, norm_scale, norm_stat)],
-            in_specs=[any_spec] * 7 + [pl.BlockSpec(memory_space=pltpu.SMEM)],
-            out_specs=[pl.BlockSpec(memory_space=pltpu.MemorySpace.VMEM)] * 5,
+            out_shape=[pltpu.VMEM(a.shape, f32) for a in (weight, weight, row_stat, col_stat, norm_scale, norm_scale, norm_stat)],
+            in_specs=[any_spec] * 7,
+            out_specs=[pl.BlockSpec(memory_space=pltpu.MemorySpace.VMEM)] * 7,
             scratch_shapes=[
-                pltpu.VMEM((layers, 4, rows, cols), f32),
+                pltpu.VMEM((layers, 3, rows, cols), f32),
                 pltpu.VMEM((layers, 4, rows, cols), f32),
                 pltpu.VMEM((layers, 2, half, cols), f32),
                 pltpu.VMEM((layers, 2, half, cols), f32),
                 pltpu.VMEM((layers, 2, half, cols), f32),
                 pltpu.VMEM(norm_grads.shape, f32),
                 pltpu.VMEM((layers, LANES), f32),
+                pltpu.VMEM((layers, LANES), f32),
                 pltpu.VMEM((layers, zs, 1, LANES), f32),
                 pltpu.VMEM((layers, 2, 1, cols // 2), f32),
                 pltpu.VMEM((layers, 1, cols // 2), f32),
                 pltpu.VMEM((layers, ds // 2, 1, cols // 2), f32),
                 pltpu.VMEM((layers, 2, 1, cols // 2), f32),
-                pltpu.VMEM((DIRECT, ds, 1, cols), f32),
+                pltpu.VMEM((ds, 1, cols), f32),
                 pltpu.VMEM((layers, 2 * zs, 1, LANES), f32),
                 pltpu.VMEM((layers, ds // 2, 1, LANES), f32),
                 pltpu.VMEM((DIRECT, ds * zs, 1, LANES), f32),
@@ -446,13 +453,13 @@
                 pltpu.VMEM((ds // 2, layers, LANES), f32),
                 pltpu.VMEM((ds // 2, layers, LANES), f32),
                 pltpu.VMEM((ds, 1, 2 * LANES), f32),
-                *[dma((n,)) for n in (3, 2, 3, 3, 4, 4, 4, 4, 4, 3, 6, 2, 2, 2, 4, 2, 4, 3, 6, 2, 4, 3)],
-                *[dma((DIRECT,))] * 4, dma((5,)), dma((2,)), dma((2,)), dma, dma,
+                *[dma((n,)) for n in (3, 2, 3, 3, 4, 4, 4, 4, 4, 3, 6, 2, 2, 2, 4, 2, 4, 3, 6, 2, 4, 2)],
+                dma, dma, dma((DIRECT,)), dma((DIRECT,)), dma((5,)), dma((2,)), dma((2,)), dma, dma,
             ],
-            compiler_params=pltpu.CompilerParams(collective_id=0, has_side_effects=True, vmem_limit_bytes=54 * 1000 * 1000),
+            compiler_params=pltpu.CompilerParams(collective_id=0, has_side_effects=True, vmem_limit_bytes=50 * 1000 * 1000),
             name='adafactor_step',
-        )(weight, grads, row_stat, col_stat, norm_scale, norm_grads, norm_stat, learn_rate.reshape(1, 1))
-        return write_out(outs)
+        )(weight, grads, row_stat, col_stat, norm_scale, norm_grads, norm_stat)
+        return write_out(learn_rate, *outs)
 
     mat_spec = P(None, 'dp', 'model')
     row_spec = P(None, 'dp')

time: 177 us -> 178 us (level)
  no operation moved by 1% of the time
where the time goes in v6:
time: 178 us
  Pallas kernels  176 us (99%)
    pallas_call x1, Pallas kernels, local_step(): pl.pallas_call(step_kernel, out_shape=[pltpu.VMEM(a.shape, f32) for a in...  174 us

profile of v6, /device:TPU:0, one launch (start us, length us, event | category | flops | bytes accessed | tf_op | source)
XLA Modules:
  0.0 177.6 jit_solution(14006485717511090507)
XLA Ops:
  1.3 174.0 %adafactor_step.1 = (f32[16,96,768]{2,1,0:T(8,128)S(1)}, f32[16,96,768]{2,1,0:T(8,128)S(1)}, f32[16,96]{1,0:T(8,128)S(1)}, f32[16,768]{1,0:T(8,128)S(1)}, f32[16...) custom-call(f32[16,96,768]{2,1,0:T(8,128)} %w_hbm.1, f32[16,8,96,768]{3,2,1,0:T(8,128)} %bitcast.1, ...), custom_call_target="tpu_custom_call" | custom-call | tf_op jit(solution)/shard_map/adafactor_step/pallas_call | solution.py:429
  175.3 2.3 %write_out.1 = (f32[16,96,768]{2,1,0:T(8,128)}, f32[16,96]{1,0:T(8,128)}, f32[16,768]{1,0:T(8,128)}, f32[16,96]{1,0:T(8,128)}, f32[16,96]{1,0:T(8,128)}) custom-call(f32[]{:T(128)S(6)} %copy.13.lr_ref, f32[16,96,768]{2,1,0:T(8,128)S(1)} %get-tuple-element.12.w, f32[16,96,768]{2,1,0:T(8,128)S(1)} %get-tuple-element.13.d, f32[16,96]{1,0:T(8,128)S(1)} %get-tuple-element.14.r, ...), custom_call_target="tpu_custom_call" | custom-call | tf_op jit(solution)/shard_map/write_out/pallas_call | solution.py:407

commit v7 on v6

--- a/solution.py
+++ b/solution.py
@@ -29,7 +29,7 @@
                 cl_send, cl_recv, tl_send, tl_recv, small_sem, h_send, h_recv, k_send, k_recv):
     layers, _, rows, cols = own.shape
     half = rows // 2
-    last, ds = layers - 1, c_last.shape[0]
+    last, ds = layers - 1, c_last.shape[1]
     late = layers - DIRECT
     zs = r_all.shape[1]
     chips = ds // 2
@@ -228,25 +228,26 @@
         q = g * g + EPS_FLOOR
         col = jnp.sum(q, axis=0, keepdims=True)
 
-        @pl.when(l < last)
+        @pl.when(l < late)
         def _():
             c_mine[l, 0] = col[:, 0:cols // 2]
             c_mine[l, 1] = col[:, cols // 2:cols]
 
-        @pl.when(l == last)
-        def _():
-            c_last[d] = col
+        @pl.when(l >= late)
+        def _():
+            c_last[l - late, d] = col
 
         p = jnp.concatenate([fold(q), jnp.zeros((LANES - rows, LANES), jnp.float32)], axis=0)
         r_all[l, z] = jnp.sum(jnp.transpose(p), axis=0, keepdims=True)
 
-        @pl.when(l < last)
+        @pl.when(l < late)
         def _():
             pair_columns(l).start()
 
-        @pl.when(l == last)
-        def _():
-            spread(c_last.at[d], cl_send, cl_recv, d_peers)
+        @pl.when(l >= late)
+        def _():
+            e = l - late
+            spread(c_last.at[e, d], cl_send.at[e], cl_recv.at[e], d_peers)
 
         spread(r_all.at[l, z], ring(r_send, l), ring(r_recv, l), z_peers)
 
@@ -268,15 +269,16 @@
         full_columns(l).start()
 
     def stage_moments(l):
-        @pl.when(l < last)
+        @pl.when(l < late)
         def _():
             full_columns(l).wait()
 
-        @pl.when(l == last)
-        def _():
-            drain(c_last.at[0:ds - 1], cl_recv)
-            drain(c_last.at[0:ds - 1], cl_send)
-            col = total(c_last)
+        @pl.when(l >= late)
+        def _():
+            e = l - late
+            drain(c_last.at[e, 0:ds - 1], cl_recv.at[e])
+            drain(c_last.at[e, 0:ds - 1], cl_send.at[e])
+            col = total(c_last.at[e])
             c_full[l, 0] = col[:, 0:cols // 2]
             c_full[l, 1] = col[:, cols // 2:cols]
 
@@ -301,17 +303,16 @@
         row = jnp.where(lane == 1, jnp.sum(w_sq[pl.ds(l, 1)], axis=1, keepdims=True), row)
         row = jnp.where(lane == 2, jnp.sum(r_new, axis=1, keepdims=True), row)
 
-        @pl.when(l < late)
+        @pl.when(l < last)
         def _():
             s_all[l, 2 * z + core] = row
             spread(s_all.at[l, 2 * z + core], ring(s_send, l), ring(s_recv, l), column_peers)
 
-        @pl.when(l >= late)
-        def _():
-            e = l - late
+        @pl.when(l == last)
+        def _():
             me = ds * z + d
-            t_last[e, me] = row
-            spread(t_last.at[e, me], tl_send.at[e], tl_recv.at[e], others)
+            t_last[me] = row
+            spread(t_last.at[me], tl_send, tl_recv, others)
 
     def stage_gather(l):
         drain(s_all.at[l, 0:2 * zs - 1], ring(s_recv, l))
@@ -324,10 +325,10 @@
         drain(t_all.at[l, 0:chips - 1], ring(t_send, l))
         apply(l, total(t_all.at[l]))
 
-    def stage_final(e):
-        drain(t_last.at[e, 0:ds * zs - 1], tl_recv.at[e])
-        drain(t_last.at[e, 0:ds * zs - 1], tl_send.at[e])
-        apply(e + late, total(t_last.at[e]))
+    def stage_final():
+        drain(t_last.at[0:ds * zs - 1], tl_recv)
+        drain(t_last.at[0:ds * zs - 1], tl_send)
+        apply(last, total(t_last))
 
     def apply(l, sums):
         count = rows_total * cols_total
@@ -366,20 +367,19 @@
         at(i, 1, stage_forward)
         once(i, 1, norm_split)
         once(i, 2, norm_send)
-        at(i, 3, stage_columns, 0, last)
-        at(i, 4, stage_share, 0, last)
+        at(i, 3, stage_columns, 0, late)
+        at(i, 4, stage_share, 0, late)
         at(i, 5, stage_moments)
-        at(i, 7, stage_gather, 0, late)
-        at(i, 8, stage_update, 0, late)
+        at(i, 7, stage_gather, 0, last)
+        at(i, 8, stage_update, 0, last)
         at(i, 4, drain_bulk)
         once(i, 4, norm_stats)
         once(i, 6, norm_update)
         at(i, 2, stage_stats)
         return carry
 
-    lax.fori_loop(0, late + 8, body, 0)
-    for e in range(DIRECT):
-        stage_final(e)
+    lax.fori_loop(0, last + 8, body, 0)
+    stage_final()
     drain(h_all.at[0:chips - 1], h_send.at[1])
     drain(k_all.at[0:ds - 1], k_send)
 
@@ -445,16 +445,16 @@
                 pltpu.VMEM((layers, 1, cols // 2), f32),
                 pltpu.VMEM((layers, ds // 2, 1, cols // 2), f32),
                 pltpu.VMEM((layers, 2, 1, cols // 2), f32),
-                pltpu.VMEM((ds, 1, cols), f32),
+                pltpu.VMEM((DIRECT, ds, 1, cols), f32),
                 pltpu.VMEM((layers, 2 * zs, 1, LANES), f32),
                 pltpu.VMEM((layers, ds // 2, 1, LANES), f32),
-                pltpu.VMEM((DIRECT, ds * zs, 1, LANES), f32),
+                pltpu.VMEM((ds * zs, 1, LANES), f32),
                 pltpu.VMEM((ds // 2, 2, layers, LANES), f32),
                 pltpu.VMEM((ds // 2, layers, LANES), f32),
                 pltpu.VMEM((ds // 2, layers, LANES), f32),
                 pltpu.VMEM((ds, 1, 2 * LANES), f32),
                 *[dma((n,)) for n in (3, 2, 3, 3, 4, 4, 4, 4, 4, 3, 6, 2, 2, 2, 4, 2, 4, 3, 6, 2, 4, 2)],
-                dma, dma, dma((DIRECT,)), dma((DIRECT,)), dma((5,)), dma((2,)), dma((2,)), dma, dma,
+                dma((DIRECT,)), dma((DIRECT,)), dma, dma, dma((5,)), dma((2,)), dma((2,)), dma, dma,
             ],
             compiler_params=pltpu.CompilerParams(collective_id=0, has_side_effects=True, vmem_limit_bytes=50 * 1000 * 1000),
             name='adafactor_step',

time: 178 us -> 179 us (level)
  no operation moved by 1% of the time
where the time goes in v7:
time: 179 us; the launch traced here: 178 us
  Pallas kernels  177 us (99%)
    pallas_call x1, Pallas kernels, local_step(): pl.pallas_call(step_kernel, out_shape=[pltpu.VMEM(a.shape, f32) for a in...  175 us

profile of v7, /device:TPU:0, one launch (start us, length us, event | category | flops | bytes accessed | tf_op | source)
XLA Modules:
  0.0 178.4 jit_solution(16789705366114137718)
XLA Ops:
  1.3 174.9 %adafactor_step.1 = (f32[16,96,768]{2,1,0:T(8,128)S(1)}, f32[16,96,768]{2,1,0:T(8,128)S(1)}, f32[16,96]{1,0:T(8,128)S(1)}, f32[16,768]{1,0:T(8,128)S(1)}, f32[16...) custom-call(f32[16,96,768]{2,1,0:T(8,128)} %w_hbm.1, f32[16,8,96,768]{3,2,1,0:T(8,128)} %bitcast.1, ...), custom_call_target="tpu_custom_call" | custom-call | tf_op jit(solution)/shard_map/adafactor_step/pallas_call | solution.py:429
  176.2 2.3 %write_out.1 = (f32[16,96,768]{2,1,0:T(8,128)}, f32[16,96]{1,0:T(8,128)}, f32[16,768]{1,0:T(8,128)}, f32[16,96]{1,0:T(8,128)}, f32[16,96]{1,0:T(8,128)}) custom-call(f32[]{:T(128)S(6)} %copy.13.lr_ref, f32[16,96,768]{2,1,0:T(8,128)S(1)} %get-tuple-element.12.w, f32[16,96,768]{2,1,0:T(8,128)S(1)} %get-tuple-element.13.d, f32[16,96]{1,0:T(8,128)S(1)} %get-tuple-element.14.r, ...), custom_call_target="tpu_custom_call" | custom-call | tf_op jit(solution)/shard_map/write_out/pallas_call | solution.py:407

commit v8 on v7

--- a/solution.py
+++ b/solution.py
@@ -19,17 +19,30 @@
 DIRECT = 2
 
 
+def column(row, rows):
+    return jnp.transpose(jnp.broadcast_to(row, (LANES, LANES)))[0:rows]
+
+
+def factors(sums, r_row, rows, zs, rows_total, cols_total):
+    count = rows_total * cols_total
+    r_mean = sums[:, 2:3] / (rows_total * zs)
+    u_rms = jnp.sqrt(sums[:, 0:1] / count * r_mean)
+    clip = jnp.maximum(1.0, u_rms / CLIP_LIMIT)
+    scale = jnp.maximum(SCALE_FLOOR, jnp.sqrt(sums[:, 1:2] / count))
+    return scale, clip, column(lax.rsqrt(r_row / r_mean), rows)
+
+
 def step_kernel(w_hbm, g_hbm, r_hbm, c_hbm, n_hbm, ng_hbm, v_hbm,
-                w_buf, d_buf, r_buf, c_buf, n_buf, dn_buf, v_buf,
-                own, peer, in1x, in1y, in2, ng_buf, r_pad, w_sq,
+                w_buf, d_buf, r_buf, c_buf, n_buf, dn_buf, v_buf, r_pad, sums_out,
+                own, peer, in1x, in1y, in2, ng_buf, w_sq,
                 r_all, c_mine, c_pair, c_all, c_full, c_last, s_all, t_all, t_last, h_out, h_pair, h_all, k_all,
-                load_sem, stage_sem, first_recv, pair_send, pair_recv, one_send, one_recv, two_send, two_recv,
+                load_sem, pair_send, pair_recv, one_send, one_recv, two_send, two_recv,
                 r_send, r_recv, cp_send, cp_recv, c_send, c_recv, cf_send, cf_recv,
                 s_send, s_recv, t_send, t_recv, w_sem,
-                cl_send, cl_recv, tl_send, tl_recv, small_sem, h_send, h_recv, k_send, k_recv):
+                cl_send, cl_recv, tl_send, tl_recv):
     layers, _, rows, cols = own.shape
     half = rows // 2
-    last, ds = layers - 1, c_last.shape[1]
+    ds = c_last.shape[1]
     late = layers - DIRECT
     zs = r_all.shape[1]
     chips = ds // 2
@@ -96,9 +109,6 @@
             parts = [a + b for a, b in zip(parts[::2], parts[1::2])]
         return parts[0]
 
-    def column(row):
-        return jnp.transpose(jnp.broadcast_to(row, (LANES, LANES)))[0:rows]
-
     def fold(values):
         acc = values[:, 0:LANES]
         for t in range(1, cols // LANES):
@@ -110,10 +120,8 @@
     for i, group in enumerate(groups):
         for k, row in group:
             part = pl.ds(row, half)
-            pltpu.make_async_copy(from_hbm(0, k).at[part], own.at[layers - 1, i, pl.ds((k - i) * half, half)], stage_sem.at[i]).start()
+            pltpu.make_async_copy(from_hbm(0, k).at[part], own.at[layers - 1, i, pl.ds((k - i) * half, half)], w_sem.at[i]).start()
     load_own(0)
-    for i, (src, dst) in enumerate(small):
-        pltpu.make_async_copy(src, dst, small_sem.at[i]).start()
 
     barrier = pltpu.get_barrier_semaphore()
     known = d_peers + column_peers[1:]
@@ -121,42 +129,45 @@
         pl.semaphore_signal(barrier, inc=1, device_id=where, device_id_type=MESH)
     pl.semaphore_wait(barrier, len(known))
     for i, group in enumerate(groups):
-        drain(own.at[layers - 1, i], stage_sem.at[i])
+        drain(own.at[layers - 1, i], w_sem.at[i])
         for k, row in group:
             part = pl.ds(row, half)
             remote(own.at[layers - 1, i, pl.ds((k - i) * half, half)], peer.at[0, k, part],
-                   pair_send.at[0], first_recv.at[i], {'dp': dc}).start()
+                   pair_send.at[0], two_recv.at[i + 1], {'dp': dc}).start()
     for k, row in ((0, half), (2, 0), (3, 0), (3, half)):
-        pair_copy(0, k, row, from_hbm(0, k), first_recv.at[2]).start()
+        pair_copy(0, k, row, from_hbm(0, k), two_recv.at[3]).start()
     for l in range(1, AHEAD):
         send_pair(l)
         load_own(l)
 
     def norm_split():
-        for i, (src, dst) in enumerate(small):
-            pltpu.make_async_copy(src, dst, small_sem.at[i]).wait()
+        for src, dst in small:
+            copy = pltpu.make_async_copy(src, dst, w_sem.at[1])
+            copy.start()
+            copy.wait()
         r_pad[...] = jnp.zeros_like(r_pad)
         r_pad[:, 0:rows] = r_buf[...]
         h_out[...] = jnp.zeros_like(h_out)
         k_all[...] = jnp.zeros_like(k_all)
         for k in range(ds):
             h_out[k // 2, k % 2, :, 0:rows] = ng_buf[:, k * rows:(k + 1) * rows]
-        remote(h_out.at[:, 1 - core], h_pair, h_send.at[0], h_recv.at[0], {'dp': dc}).start()
+        remote(h_out.at[:, 1 - core], h_pair, cl_send.at[0], cl_recv.at[0], {'dp': dc}).start()
 
     def norm_send():
-        remote(h_out.at[:, 1 - core], h_pair, h_send.at[0], h_recv.at[0], {'dp': dc}).wait()
+        remote(h_out.at[:, 1 - core], h_pair, cl_send.at[0], cl_recv.at[0], {'dp': dc}).wait()
         for k in range(chips):
             h_pair[k] = h_pair[k] + h_out[k, core]
         h_all[chip] = h_pair[chip]
         for e in (dx, dy, dxy):
-            remote(h_pair.at[lax.div(e, 2)], h_all.at[chip], h_send.at[1], h_recv.at[1], {'dp': e}).start()
+            remote(h_pair.at[lax.div(e, 2)], h_all.at[chip], cl_send.at[1], cl_recv.at[1], {'dp': e}).start()
 
     def layer_sums(values):
         padded = jnp.concatenate([values, jnp.zeros((layers, LANES - rows), jnp.float32)], axis=1)
         return jnp.sum(jnp.transpose(padded), axis=0, keepdims=True)
 
     def norm_stats():
-        drain(h_all.at[0:chips - 1], h_recv.at[1])
+        drain(h_all.at[0:chips - 1], cl_recv.at[1])
+        drain(h_all.at[0:chips - 1], cl_send.at[1])
         h = total(h_all)[:, 0:rows]
         v_new = DECAY * v_buf[...] + (1.0 - DECAY) * (h * h + EPS_FLOOR)
         v_buf[...] = v_new
@@ -164,10 +175,11 @@
         nv = n_buf[...]
         k_all[d, :, 0:layers] = layer_sums(zv * zv)
         k_all[d, :, LANES:LANES + layers] = layer_sums(nv * nv)
-        spread(k_all.at[d], k_send, k_recv, d_peers)
+        spread(k_all.at[d], tl_send.at[0], tl_recv.at[0], d_peers)
 
     def norm_update():
-        drain(k_all.at[0:ds - 1], k_recv)
+        drain(k_all.at[0:ds - 1], tl_recv.at[0])
+        drain(k_all.at[0:ds - 1], tl_send.at[0])
         acc = total(k_all)
         z_sq, n_sq = acc[:, 0:layers], acc[:, LANES:LANES + layers]
         clip = jnp.maximum(1.0, jnp.sqrt(z_sq / rows_total) / CLIP_LIMIT)
@@ -184,13 +196,13 @@
 
     def stage_first():
         drain(peer.at[0], load_sem.at[0])
-        drain(in1x.at[0], first_recv.at[0])
+        drain(in1x.at[0], two_recv.at[1])
         combine(0, slice(0, 2), first)
         x1(0).start()
-        drain(in1y.at[0], first_recv.at[1])
+        drain(in1y.at[0], two_recv.at[2])
         combine(0, slice(1, 3), second)
         y1(0).start()
-        drain(peer.at[0, 0:2], first_recv.at[2])
+        drain(peer.at[0, 0:2], two_recv.at[3])
         combine(0, 0, second)
         combine(0, 2, first)
         d_buf[0] = d_buf[0] + peer[0, 3]
@@ -257,8 +269,14 @@
     def full_columns(l):
         return remote(c_full.at[l, core], c_full.at[l, core], ring(cf_send, l), ring(cf_recv, l), {'dp': dc})
 
+    def drain_rows(l):
+        if zs > 1:
+            drain(r_all.at[l, 0:zs - 1], ring(r_recv, l))
+            drain(r_all.at[l, 0:zs - 1], ring(r_send, l))
+
     def stage_columns(l):
         pair_columns(l).wait()
+        drain_rows(l)
         c_all[l, chip] = c_mine[l, core] + c_pair[l]
         spread(c_all.at[l, chip], ring(c_send, l), ring(c_recv, l), plane_peers)
 
@@ -278,20 +296,18 @@
             e = l - late
             drain(c_last.at[e, 0:ds - 1], cl_recv.at[e])
             drain(c_last.at[e, 0:ds - 1], cl_send.at[e])
+            drain_rows(l)
             col = total(c_last.at[e])
             c_full[l, 0] = col[:, 0:cols // 2]
             c_full[l, 1] = col[:, cols // 2:cols]
 
-        if zs > 1:
-            drain(r_all.at[l, 0:zs - 1], ring(r_recv, l))
-            drain(r_all.at[l, 0:zs - 1], ring(r_send, l))
         col = jnp.concatenate([c_full[l, 0], c_full[l, 1]], axis=1)
         r_new = DECAY * r_pad[pl.ds(l, 1)] + (1.0 - DECAY) * (total(r_all.at[l]) / cols_total)
         c_new = DECAY * c_buf[pl.ds(l, 1)] + (1.0 - DECAY) * (col / rows_total)
         r_pad[pl.ds(l, 1)] = r_new
         r_buf[pl.ds(l, 1)] = r_new[:, 0:rows]
         c_buf[pl.ds(l, 1)] = c_new
-        a = column(lax.rsqrt(r_new))
+        a = column(lax.rsqrt(r_new), rows)
         b = lax.rsqrt(c_new)
         acc = jnp.zeros((1, LANES), jnp.float32)
         for t in range(cols // LANES):
@@ -303,16 +319,17 @@
         row = jnp.where(lane == 1, jnp.sum(w_sq[pl.ds(l, 1)], axis=1, keepdims=True), row)
         row = jnp.where(lane == 2, jnp.sum(r_new, axis=1, keepdims=True), row)
 
-        @pl.when(l < last)
+        @pl.when(l < late)
         def _():
             s_all[l, 2 * z + core] = row
             spread(s_all.at[l, 2 * z + core], ring(s_send, l), ring(s_recv, l), column_peers)
 
-        @pl.when(l == last)
-        def _():
+        @pl.when(l >= late)
+        def _():
+            e = l - late
             me = ds * z + d
-            t_last[me] = row
-            spread(t_last.at[me], tl_send, tl_recv, others)
+            t_last[e, me] = row
+            spread(t_last.at[e, me], tl_send.at[e], tl_recv.at[e], others)
 
     def stage_gather(l):
         drain(s_all.at[l, 0:2 * zs - 1], ring(s_recv, l))
@@ -323,27 +340,21 @@
     def stage_update(l):
         drain(t_all.at[l, 0:chips - 1], ring(t_recv, l))
         drain(t_all.at[l, 0:chips - 1], ring(t_send, l))
-        apply(l, total(t_all.at[l]))
-
-    def stage_final():
-        drain(t_last.at[0:ds * zs - 1], tl_recv)
-        drain(t_last.at[0:ds * zs - 1], tl_send)
-        apply(last, total(t_last))
-
-    def apply(l, sums):
-        count = rows_total * cols_total
-        r_mean = sums[:, 2:3] / (rows_total * zs)
-        u_rms = jnp.sqrt(sums[:, 0:1] / count * r_mean)
-        clip = jnp.maximum(1.0, u_rms / CLIP_LIMIT)
-        scale = jnp.maximum(SCALE_FLOOR, jnp.sqrt(sums[:, 1:2] / count))
-        a = column(lax.rsqrt(r_pad[pl.ds(l, 1)] / r_mean))
-        b = lax.rsqrt(c_buf[pl.ds(l, 1)])
+        scale, clip, a = factors(total(t_all.at[l]), r_pad[pl.ds(l, 1)], rows, zs, rows_total, cols_total)
+        b = lax.rsqrt(c_buf[pl.ds(l, 1)]) / clip
         for t in range(cols // LANES):
             sl = slice(t * LANES, (t + 1) * LANES)
-            d_buf[l, :, sl] = d_buf[l, :, sl] * a * (b[:, sl] / clip) * scale
-
-    def drain_bulk(l):
+            d_buf[l, :, sl] = d_buf[l, :, sl] * a * b[:, sl] * scale
+
+    def stage_final(e):
+        drain(t_last.at[e, 0:ds * zs - 1], tl_recv.at[e])
+        drain(t_last.at[e, 0:ds * zs - 1], tl_send.at[e])
+        sums_out[e] = total(t_last.at[e])
+
+    def drain_one(l):
         drain(in1x.at[0:2], ring(one_send, l))
+
+    def drain_two(l):
         drain(in2.at[l], ring(two_send, l))
 
     def at(i, lag, stage, begin=0, end=layers):
@@ -370,30 +381,37 @@
         at(i, 3, stage_columns, 0, late)
         at(i, 4, stage_share, 0, late)
         at(i, 5, stage_moments)
-        at(i, 7, stage_gather, 0, last)
-        at(i, 8, stage_update, 0, last)
-        at(i, 4, drain_bulk)
+        at(i, 7, stage_gather, 0, late)
+        at(i, 8, stage_update, 0, late)
+        at(i, 2, drain_one)
+        at(i, 3, drain_two)
         once(i, 4, norm_stats)
         once(i, 6, norm_update)
         at(i, 2, stage_stats)
         return carry
 
-    lax.fori_loop(0, last + 8, body, 0)
-    stage_final()
-    drain(h_all.at[0:chips - 1], h_send.at[1])
-    drain(k_all.at[0:ds - 1], k_send)
-
-
-def write_kernel(lr_ref, w, d, r, c, n, dn, v, wo, ro, co, no, vo, w_new, n_new, sem):
-    layers = w.shape[0]
-    rate = lr_ref[...]
+    lax.fori_loop(0, late + 8, body, 0)
+    for e in range(DIRECT):
+        stage_final(e)
+
+
+def write_kernel(ds, zs, rate_ref, w, d, r, c, n, dn, v, r_pad, sums, wo, ro, co, no, vo, w_new, n_new, sem):
+    layers, rows, cols = w.shape
+    late = layers - DIRECT
+    rate = rate_ref[...]
     pairs = ((r, ro), (c, co), (v, vo), (n_new, no))
     for i in range(3):
         pltpu.make_async_copy(*pairs[i], sem.at[i]).start()
     n_new[...] = n[...] - rate * dn[...]
     for l in range(layers + 1):
-        if l < layers:
+        if l < late:
             w_new[l] = w[l] - rate * d[l]
+        elif l < layers:
+            scale, clip, a = factors(sums[l - late], r_pad[l:l + 1], rows, zs, rows * ds, cols * zs)
+            b = lax.rsqrt(c[l:l + 1]) / clip
+            for t in range(cols // LANES):
+                sl = slice(t * LANES, (t + 1) * LANES)
+                w_new[l, :, sl] = w[l, :, sl] - rate * (d[l, :, sl] * a * b[:, sl] * scale)
         if l == 1:
             pltpu.make_async_copy(*pairs[3], sem.at[3]).start()
         if l >= 1:
@@ -403,16 +421,16 @@
     pltpu.make_async_copy(w_new, wo, sem.at[4]).wait()
 
 
-def write_out(rate, w, d, r, c, n, dn, v):
+def write_out(ds, zs, rate, w, d, r, c, n, dn, v, r_pad, sums):
     return pl.pallas_call(
-        write_kernel,
+        functools.partial(write_kernel, ds, zs),
         out_shape=[jax.ShapeDtypeStruct(a.shape, a.dtype) for a in (w, r, c, n, v)],
-        in_specs=[pl.BlockSpec(memory_space=pltpu.MemorySpace.SMEM)] + [pl.BlockSpec(memory_space=pltpu.MemorySpace.VMEM)] * 7,
+        in_specs=[pl.BlockSpec(memory_space=pltpu.MemorySpace.SMEM)] + [pl.BlockSpec(memory_space=pltpu.MemorySpace.VMEM)] * 9,
         out_specs=[pl.BlockSpec(memory_space=pltpu.MemorySpace.HBM)] * 5,
         scratch_shapes=[pltpu.VMEM(w.shape, w.dtype), pltpu.VMEM(n.shape, n.dtype), pltpu.SemaphoreType.DMA((5,))],
         compiler_params=pltpu.CompilerParams(vmem_limit_bytes=8 << 20),
         name='write_out',
-    )(rate, w, d, r, c, n, dn, v)
+    )(rate, w, d, r, c, n, dn, v, r_pad, sums)
 
 
 def solution(mesh):
@@ -428,9 +446,10 @@
         dma = pltpu.SemaphoreType.DMA
         outs = pl.pallas_call(
             step_kernel,
-            out_shape=[pltpu.VMEM(a.shape, f32) for a in (weight, weight, row_stat, col_stat, norm_scale, norm_scale, norm_stat)],
+            out_shape=[pltpu.VMEM(a.shape, f32) for a in (weight, weight, row_stat, col_stat, norm_scale, norm_scale, norm_stat)]
+            + [pltpu.VMEM((layers, LANES), f32), pltpu.VMEM((DIRECT, 1, LANES), f32)],
             in_specs=[any_spec] * 7,
-            out_specs=[pl.BlockSpec(memory_space=pltpu.MemorySpace.VMEM)] * 7,
+            out_specs=[pl.BlockSpec(memory_space=pltpu.MemorySpace.VMEM)] * 9,
             scratch_shapes=[
                 pltpu.VMEM((layers, 3, rows, cols), f32),
                 pltpu.VMEM((layers, 4, rows, cols), f32),
@@ -438,7 +457,6 @@
                 pltpu.VMEM((layers, 2, half, cols), f32),
                 pltpu.VMEM((layers, 2, half, cols), f32),
                 pltpu.VMEM(norm_grads.shape, f32),
-                pltpu.VMEM((layers, LANES), f32),
                 pltpu.VMEM((layers, LANES), f32),
                 pltpu.VMEM((layers, zs, 1, LANES), f32),
                 pltpu.VMEM((layers, 2, 1, cols // 2), f32),
@@ -448,18 +466,18 @@
                 pltpu.VMEM((DIRECT, ds, 1, cols), f32),
                 pltpu.VMEM((layers, 2 * zs, 1, LANES), f32),
                 pltpu.VMEM((layers, ds // 2, 1, LANES), f32),
-                pltpu.VMEM((ds * zs, 1, LANES), f32),
+                pltpu.VMEM((DIRECT, ds * zs, 1, LANES), f32),
                 pltpu.VMEM((ds // 2, 2, layers, LANES), f32),
                 pltpu.VMEM((ds // 2, layers, LANES), f32),
                 pltpu.VMEM((ds // 2, layers, LANES), f32),
                 pltpu.VMEM((ds, 1, 2 * LANES), f32),
-                *[dma((n,)) for n in (3, 2, 3, 3, 4, 4, 4, 4, 4, 3, 6, 2, 2, 2, 4, 2, 4, 3, 6, 2, 4, 2)],
-                dma((DIRECT,)), dma((DIRECT,)), dma, dma, dma((5,)), dma((2,)), dma((2,)), dma, dma,
+                *[dma((n,)) for n in (3, 3, 4, 3, 3, 3, 4, 4, 4, 2, 2, 2, 4, 2, 4, 3, 6, 2, 4, 2)],
+                *[dma((DIRECT,))] * 4,
             ],
             compiler_params=pltpu.CompilerParams(collective_id=0, has_side_effects=True, vmem_limit_bytes=50 * 1000 * 1000),
             name='adafactor_step',
         )(weight, grads, row_stat, col_stat, norm_scale, norm_grads, norm_stat)
-        return write_out(learn_rate, *outs)
+        return write_out(ds, zs, learn_rate, *outs)
 
     mat_spec = P(None, 'dp', 'model')
     row_spec = P(None, 'dp')

time: 179 us -> 177 us (0.989)
  no operation moved by 1% of the time
where the time goes in v8:
time: 177 us
  Pallas kernels  176 us (99%)
    pallas_call x1, Pallas kernels, local_step(): pl.pallas_call(step_kernel, out_shape=[pltpu.VMEM(a.shape, f32) for a in...  173 us

profile of v8, /device:TPU:0, one launch (start us, length us, event | category | flops | bytes accessed | tf_op | source)
XLA Modules:
  0.0 176.8 jit_solution(3648891974903029122)
XLA Ops:
  1.3 173.2 %adafactor_step.1 = (f32[16,96,768]{2,1,0:T(8,128)S(1)}, f32[16,96,768]{2,1,0:T(8,128)S(1)}, f32[16,96]{1,0:T(8,128)S(1)}, f32[16,768]{1,0:T(8,128)S(1)}, f32[16...) custom-call(f32[16,96,768]{2,1,0:T(8,128)} %w_hbm.1, ...), custom_call_target="tpu_custom_call" | custom-call | tf_op jit(solution)/shard_map/adafactor_step/pallas_call | solution.py:447
  174.5 2.3 %write_out.1 = (f32[16,96,768]{2,1,0:T(8,128)}, f32[16,96]{1,0:T(8,128)}, f32[16,768]{1,0:T(8,128)}, f32[16,96]{1,0:T(8,128)}, f32[16,96]{1,0:T(8,128)}) custom-call(f32[]{:T(128)S(6)} %copy.13.rate_ref, f32[16,96,768]{2,1,0:T(8,128)S(1)} %get-tuple-element.14.w, f32[16,96,768]{2,1,0:T(8,128)S(1)} %get-tuple-element.15.d, f32[16,96]{1,0:T(8,128)S(1)} %get-tuple-element.16.r, ...), custom_call_target="tpu_custom_call" | custom-call | tf_op jit(solution)/shard_map/write_out/pallas_call | solution.py:425

commit v9 on v8

--- a/solution.py
+++ b/solution.py
@@ -17,6 +17,7 @@
 LANES = 128
 AHEAD = 2
 DIRECT = 2
+EARLY = 8
 
 
 def column(row, rows):
@@ -34,7 +35,7 @@
 
 def step_kernel(w_hbm, g_hbm, r_hbm, c_hbm, n_hbm, ng_hbm, v_hbm,
                 w_buf, d_buf, r_buf, c_buf, n_buf, dn_buf, v_buf, r_pad, sums_out,
-                own, peer, in1x, in1y, in2, ng_buf, w_sq,
+                own, peer, in1x, in1y, in2, early, ng_buf, w_sq,
                 r_all, c_mine, c_pair, c_all, c_full, c_last, s_all, t_all, t_last, h_out, h_pair, h_all, k_all,
                 load_sem, pair_send, pair_recv, one_send, one_recv, two_send, two_recv,
                 r_send, r_recv, cp_send, cp_recv, c_send, c_recv, cf_send, cf_recv,
@@ -122,12 +123,18 @@
             part = pl.ds(row, half)
             pltpu.make_async_copy(from_hbm(0, k).at[part], own.at[layers - 1, i, pl.ds((k - i) * half, half)], w_sem.at[i]).start()
     load_own(0)
+    small_sems = (r_send.at[0], r_send.at[1], r_send.at[2], r_send.at[3], cl_send.at[0])
+    for (src, dst), sem in zip(small, small_sems):
+        pltpu.make_async_copy(src, dst, sem).start()
 
     barrier = pltpu.get_barrier_semaphore()
     known = d_peers + column_peers[1:]
     for where in known:
         pl.semaphore_signal(barrier, inc=1, device_id=where, device_id_type=MESH)
     pl.semaphore_wait(barrier, len(known))
+    for i, (near, row) in enumerate(((dx, 0), (dy, half))):
+        for e in (near, near + dc - d):
+            remote(g_hbm.at[0, e, pl.ds(row, EARLY)], early.at[i, core], tl_send.at[1], tl_recv.at[1], {'dp': e}).start()
     for i, group in enumerate(groups):
         drain(own.at[layers - 1, i], w_sem.at[i])
         for k, row in group:
@@ -141,10 +148,8 @@
         load_own(l)
 
     def norm_split():
-        for src, dst in small:
-            copy = pltpu.make_async_copy(src, dst, w_sem.at[1])
-            copy.start()
-            copy.wait()
+        for (src, dst), sem in zip(small, small_sems):
+            pltpu.make_async_copy(src, dst, sem).wait()
         r_pad[...] = jnp.zeros_like(r_pad)
         r_pad[:, 0:rows] = r_buf[...]
         h_out[...] = jnp.zeros_like(h_out)
@@ -198,10 +203,14 @@
         drain(peer.at[0], load_sem.at[0])
         drain(in1x.at[0], two_recv.at[1])
         combine(0, slice(0, 2), first)
-        x1(0).start()
+        for k, row in ((0, EARLY), (1, 0)):
+            part = pl.ds(row, half - row)
+            remote(own.at[0, k, part], in1x.at[0, k, part], one_send.at[0], one_recv.at[0], {'dp': dx}).start()
         drain(in1y.at[0], two_recv.at[2])
         combine(0, slice(1, 3), second)
-        y1(0).start()
+        for k, row in ((0, 0), (1, EARLY)):
+            remote(own.at[0, k + 1, pl.ds(half + row, half - row)], in1y.at[0, k, pl.ds(row, half - row)],
+                   one_send.at[0], one_recv.at[0], {'dp': dy}).start()
         drain(peer.at[0, 0:2], two_recv.at[3])
         combine(0, 0, second)
         combine(0, 2, first)
@@ -229,6 +238,23 @@
         d_buf[l, 0:half] = d_buf[l, 0:half] + in1x[l, 0]
         x2(l).start()
         d_buf[l, half:rows] = d_buf[l, half:rows] + in1y[l, 1]
+
+    first_part = w_buf.at[0:half // 4 - EARLY // 8, 0:16]
+
+    def forward_first():
+        drain(first_part, one_recv.at[0])
+        own[0, 2, first] = own[0, 2, first] + in1x[0, 1]
+        own[0, 0, second] = own[0, 0, second] + in1y[0, 0]
+        y2(0).start()
+        x2(0).start()
+        pltpu.make_async_copy(w_hbm.at[0], w_buf.at[0], w_sem.at[0]).start()
+        drain(early, tl_recv.at[1])
+        drain(early, tl_send.at[1])
+        rest = slice(EARLY, half)
+        d_buf[0, 0:EARLY] = d_buf[0, 0:EARLY] + (early[0, 0] + early[0, 1])
+        d_buf[0, rest] = d_buf[0, rest] + in1x[0, 0, rest]
+        d_buf[0, half:half + EARLY] = d_buf[0, half:half + EARLY] + (early[1, 0] + early[1, 1])
+        d_buf[0, half + EARLY:rows] = d_buf[0, half + EARLY:rows] + in1y[0, 1, rest]
 
     def stage_stats(l):
         drain(w_buf.at[l], ring(w_sem, l))
@@ -375,7 +401,8 @@
         at(i, -AHEAD, prefetch)
         at(i, 0, stage_combine, 1)
         once(i, 0, stage_first)
-        at(i, 1, stage_forward)
+        at(i, 1, stage_forward, 1)
+        once(i, 1, forward_first)
         once(i, 1, norm_split)
         once(i, 2, norm_send)
         at(i, 3, stage_columns, 0, late)
@@ -383,7 +410,8 @@
         at(i, 5, stage_moments)
         at(i, 7, stage_gather, 0, late)
         at(i, 8, stage_update, 0, late)
-        at(i, 2, drain_one)
+        at(i, 2, drain_one, 1)
+        once(i, 2, lambda: drain(first_part, one_send.at[0]))
         at(i, 3, drain_two)
         once(i, 4, norm_stats)
         once(i, 6, norm_update)
@@ -456,6 +484,7 @@
                 pltpu.VMEM((layers, 2, half, cols), f32),
                 pltpu.VMEM((layers, 2, half, cols), f32),
                 pltpu.VMEM((layers, 2, half, cols), f32),
+                pltpu.VMEM((2, 2, EARLY, cols), f32),
                 pltpu.VMEM(norm_grads.shape, f32),
                 pltpu.VMEM((layers, LANES), f32),
                 pltpu.VMEM((layers, zs, 1, LANES), f32),

time: 177 us -> 176 us (level)
  no operation moved by 1% of the time
where the time goes in v9:
time: 176 us
  Pallas kernels  175 us (99%)
    pallas_call x1, Pallas kernels, local_step(): pl.pallas_call(step_kernel, out_shape=[pltpu.VMEM(a.shape, f32) for a in...  173 us

profile of v9, /device:TPU:0, one launch (start us, length us, event | category | flops | bytes accessed | tf_op | source)
XLA Modules:
  0.0 176.3 jit_solution(6771687854355601427)
XLA Ops:
  1.3 172.7 %adafactor_step.1 = (f32[16,96,768]{2,1,0:T(8,128)S(1)}, f32[16,96,768]{2,1,0:T(8,128)S(1)}, f32[16,96]{1,0:T(8,128)S(1)}, f32[16,768]{1,0:T(8,128)S(1)}, f32[16...) custom-call(f32[16,96,768]{2,1,0:T(8,128)} %w_hbm.1, ...), custom_call_target="tpu_custom_call" | custom-call | tf_op jit(solution)/shard_map/adafactor_step/pallas_call | solution.py:475
  174.0 2.3 %write_out.1 = (f32[16,96,768]{2,1,0:T(8,128)}, f32[16,96]{1,0:T(8,128)}, f32[16,768]{1,0:T(8,128)}, f32[16,96]{1,0:T(8,128)}, f32[16,96]{1,0:T(8,128)}) custom-call(f32[]{:T(128)S(6)} %copy.13.rate_ref, f32[16,96,768]{2,1,0:T(8,128)S(1)} %get-tuple-element.14.w, f32[16,96,768]{2,1,0:T(8,128)S(1)} %get-tuple-element.15.d, f32[16,96]{1,0:T(8,128)S(1)} %get-tuple-element.16.r, ...), custom_call_target="tpu_custom_call" | custom-call | tf_op jit(solution)/shard_map/write_out/pallas_call | solution.py:453

commit v10 on v9

--- a/solution.py
+++ b/solution.py
@@ -24,26 +24,26 @@
     return jnp.transpose(jnp.broadcast_to(row, (LANES, LANES)))[0:rows]
 
 
-def factors(sums, r_row, rows, zs, rows_total, cols_total):
+def factors(sums, r_row, rate, rows, zs, rows_total, cols_total):
     count = rows_total * cols_total
     r_mean = sums[:, 2:3] / (rows_total * zs)
     u_rms = jnp.sqrt(sums[:, 0:1] / count * r_mean)
     clip = jnp.maximum(1.0, u_rms / CLIP_LIMIT)
-    scale = jnp.maximum(SCALE_FLOOR, jnp.sqrt(sums[:, 1:2] / count))
+    scale = rate * jnp.maximum(SCALE_FLOOR, jnp.sqrt(sums[:, 1:2] / count))
     return scale, clip, column(lax.rsqrt(r_row / r_mean), rows)
 
 
-def step_kernel(w_hbm, g_hbm, r_hbm, c_hbm, n_hbm, ng_hbm, v_hbm,
-                w_buf, d_buf, r_buf, c_buf, n_buf, dn_buf, v_buf, r_pad, sums_out,
+def step_kernel(w_hbm, g_hbm, r_hbm, c_hbm, n_hbm, ng_hbm, v_hbm, rate_ref,
+                w_buf, d_buf, r_buf, c_buf, n_buf, v_buf, r_pad, sums_out,
                 own, peer, in1x, in1y, in2, early, ng_buf, w_sq,
-                r_all, c_mine, c_pair, c_all, c_full, c_last, s_all, t_all, t_last, h_out, h_pair, h_all, k_all,
+                r_all, c_mine, c_pair, c_all, c_full, c_last, s_all, t_all, t_last, held, h_out, h_all, k_all,
                 load_sem, pair_send, pair_recv, one_send, one_recv, two_send, two_recv,
                 r_send, r_recv, cp_send, cp_recv, c_send, c_recv, cf_send, cf_recv,
                 s_send, s_recv, t_send, t_recv, w_sem,
                 cl_send, cl_recv, tl_send, tl_recv):
     layers, _, rows, cols = own.shape
     half = rows // 2
-    ds = c_last.shape[1]
+    last, ds = layers - 1, c_last.shape[0]
     late = layers - DIRECT
     zs = r_all.shape[1]
     chips = ds // 2
@@ -148,31 +148,27 @@
         load_own(l)
 
     def norm_split():
-        for (src, dst), sem in zip(small, small_sems):
-            pltpu.make_async_copy(src, dst, sem).wait()
+        for i in (0, 1, 2, 4):
+            pltpu.make_async_copy(*small[i], small_sems[i]).wait()
         r_pad[...] = jnp.zeros_like(r_pad)
         r_pad[:, 0:rows] = r_buf[...]
-        h_out[...] = jnp.zeros_like(h_out)
         k_all[...] = jnp.zeros_like(k_all)
-        for k in range(ds):
-            h_out[k // 2, k % 2, :, 0:rows] = ng_buf[:, k * rows:(k + 1) * rows]
-        remote(h_out.at[:, 1 - core], h_pair, cl_send.at[0], cl_recv.at[0], {'dp': dc}).start()
-
-    def norm_send():
-        remote(h_out.at[:, 1 - core], h_pair, cl_send.at[0], cl_recv.at[0], {'dp': dc}).wait()
-        for k in range(chips):
-            h_pair[k] = h_pair[k] + h_out[k, core]
-        h_all[chip] = h_pair[chip]
-        for e in (dx, dy, dxy):
-            remote(h_pair.at[lax.div(e, 2)], h_all.at[chip], cl_send.at[1], cl_recv.at[1], {'dp': e}).start()
+
+    h_out[...] = jnp.zeros_like(h_out)
+    pltpu.make_async_copy(*small[3], small_sems[3]).wait()
+    for k in range(ds):
+        h_out[k, :, 0:rows] = ng_buf[:, k * rows:(k + 1) * rows]
+    h_all[d] = h_out[d]
+    for where in d_peers:
+        remote(h_out.at[where['dp']], h_all.at[d], cl_send.at[1], cl_recv.at[1], where).start()
 
     def layer_sums(values):
         padded = jnp.concatenate([values, jnp.zeros((layers, LANES - rows), jnp.float32)], axis=1)
         return jnp.sum(jnp.transpose(padded), axis=0, keepdims=True)
 
     def norm_stats():
-        drain(h_all.at[0:chips - 1], cl_recv.at[1])
-        drain(h_all.at[0:chips - 1], cl_send.at[1])
+        drain(h_all.at[0:ds - 1], cl_recv.at[1])
+        drain(h_all.at[0:ds - 1], cl_send.at[1])
         h = total(h_all)[:, 0:rows]
         v_new = DECAY * v_buf[...] + (1.0 - DECAY) * (h * h + EPS_FLOOR)
         v_buf[...] = v_new
@@ -188,11 +184,11 @@
         acc = total(k_all)
         z_sq, n_sq = acc[:, 0:layers], acc[:, LANES:LANES + layers]
         clip = jnp.maximum(1.0, jnp.sqrt(z_sq / rows_total) / CLIP_LIMIT)
-        scale = jnp.maximum(SCALE_FLOOR, jnp.sqrt(n_sq / rows_total))
+        scale = rate_ref[...] * jnp.maximum(SCALE_FLOOR, jnp.sqrt(n_sq / rows_total))
         clip = jnp.transpose(jnp.broadcast_to(clip, (LANES, layers)))[:, 0:rows]
         scale = jnp.transpose(jnp.broadcast_to(scale, (LANES, layers)))[:, 0:rows]
         zv = total(h_all)[:, 0:rows] * lax.rsqrt(v_buf[...])
-        dn_buf[...] = scale * (zv / clip)
+        n_buf[...] = n_buf[...] - scale * (zv / clip)
 
     def combine(l, k, part):
         own[l, k, part] = own[l, k, part] + peer[l, k, part]
@@ -266,26 +262,25 @@
         q = g * g + EPS_FLOOR
         col = jnp.sum(q, axis=0, keepdims=True)
 
-        @pl.when(l < late)
+        @pl.when(l < last)
         def _():
             c_mine[l, 0] = col[:, 0:cols // 2]
             c_mine[l, 1] = col[:, cols // 2:cols]
 
-        @pl.when(l >= late)
-        def _():
-            c_last[l - late, d] = col
+        @pl.when(l == last)
+        def _():
+            c_last[d] = col
 
         p = jnp.concatenate([fold(q), jnp.zeros((LANES - rows, LANES), jnp.float32)], axis=0)
         r_all[l, z] = jnp.sum(jnp.transpose(p), axis=0, keepdims=True)
 
-        @pl.when(l < late)
+        @pl.when(l < last)
         def _():
             pair_columns(l).start()
 
-        @pl.when(l >= late)
-        def _():
-            e = l - late
-            spread(c_last.at[e, d], cl_send.at[e], cl_recv.at[e], d_peers)
+        @pl.when(l == last)
+        def _():
+            spread(c_last.at[d], cl_send.at[0], cl_recv.at[0], d_peers)
 
         spread(r_all.at[l, z], ring(r_send, l), ring(r_recv, l), z_peers)
 
@@ -313,17 +308,16 @@
         full_columns(l).start()
 
     def stage_moments(l):
-        @pl.when(l < late)
+        @pl.when(l < last)
         def _():
             full_columns(l).wait()
 
-        @pl.when(l >= late)
-        def _():
-            e = l - late
-            drain(c_last.at[e, 0:ds - 1], cl_recv.at[e])
-            drain(c_last.at[e, 0:ds - 1], cl_send.at[e])
+        @pl.when(l == last)
+        def _():
+            drain(c_last.at[0:ds - 1], cl_recv.at[0])
+            drain(c_last.at[0:ds - 1], cl_send.at[0])
             drain_rows(l)
-            col = total(c_last.at[e])
+            col = total(c_last)
             c_full[l, 0] = col[:, 0:cols // 2]
             c_full[l, 1] = col[:, cols // 2:cols]
 
@@ -341,6 +335,7 @@
             u = d_buf[l, :, sl] * a * b[:, sl]
             acc = acc + jnp.sum(u * u, axis=0, keepdims=True)
         lane = lax.broadcasted_iota(jnp.int32, (1, LANES), 1)
+        lane = lane - jnp.where(l == late, 3, 0)
         row = jnp.where(lane == 0, jnp.sum(acc, axis=1, keepdims=True), 0.0)
         row = jnp.where(lane == 1, jnp.sum(w_sq[pl.ds(l, 1)], axis=1, keepdims=True), row)
         row = jnp.where(lane == 2, jnp.sum(r_new, axis=1, keepdims=True), row)
@@ -350,12 +345,15 @@
             s_all[l, 2 * z + core] = row
             spread(s_all.at[l, 2 * z + core], ring(s_send, l), ring(s_recv, l), column_peers)
 
-        @pl.when(l >= late)
-        def _():
-            e = l - late
+        @pl.when(l == late)
+        def _():
+            held[...] = row
+
+        @pl.when(l == last)
+        def _():
             me = ds * z + d
-            t_last[e, me] = row
-            spread(t_last.at[e, me], tl_send.at[e], tl_recv.at[e], others)
+            t_last[me] = row + held[...]
+            spread(t_last.at[me], tl_send.at[0], tl_recv.at[0], others)
 
     def stage_gather(l):
         drain(s_all.at[l, 0:2 * zs - 1], ring(s_recv, l))
@@ -366,16 +364,16 @@
     def stage_update(l):
         drain(t_all.at[l, 0:chips - 1], ring(t_recv, l))
         drain(t_all.at[l, 0:chips - 1], ring(t_send, l))
-        scale, clip, a = factors(total(t_all.at[l]), r_pad[pl.ds(l, 1)], rows, zs, rows_total, cols_total)
+        scale, clip, a = factors(total(t_all.at[l]), r_pad[pl.ds(l, 1)], rate_ref[...], rows, zs, rows_total, cols_total)
         b = lax.rsqrt(c_buf[pl.ds(l, 1)]) / clip
         for t in range(cols // LANES):
             sl = slice(t * LANES, (t + 1) * LANES)
-            d_buf[l, :, sl] = d_buf[l, :, sl] * a * b[:, sl] * scale
-
-    def stage_final(e):
-        drain(t_last.at[e, 0:ds * zs - 1], tl_recv.at[e])
-        drain(t_last.at[e, 0:ds * zs - 1], tl_send.at[e])
-        sums_out[e] = total(t_last.at[e])
+            w_buf[l, :, sl] = w_buf[l, :, sl] - scale * (d_buf[l, :, sl] * a * b[:, sl])
+
+    def stage_final():
+        drain(t_last.at[0:ds * zs - 1], tl_recv.at[0])
+        sums_out[...] = total(t_last)
+        drain(t_last.at[0:ds * zs - 1], tl_send.at[0])
 
     def drain_one(l):
         drain(in1x.at[0:2], ring(one_send, l))
@@ -404,9 +402,8 @@
         at(i, 1, stage_forward, 1)
         once(i, 1, forward_first)
         once(i, 1, norm_split)
-        once(i, 2, norm_send)
-        at(i, 3, stage_columns, 0, late)
-        at(i, 4, stage_share, 0, late)
+        at(i, 3, stage_columns, 0, last)
+        at(i, 4, stage_share, 0, last)
         at(i, 5, stage_moments)
         at(i, 7, stage_gather, 0, late)
         at(i, 8, stage_update, 0, late)
@@ -419,46 +416,40 @@
         return carry
 
     lax.fori_loop(0, late + 8, body, 0)
-    for e in range(DIRECT):
-        stage_final(e)
-
-
-def write_kernel(ds, zs, rate_ref, w, d, r, c, n, dn, v, r_pad, sums, wo, ro, co, no, vo, w_new, n_new, sem):
+    stage_final()
+
+
+def write_kernel(ds, zs, rate_ref, w, d, r, c, n, v, r_pad, sums, wo, ro, co, no, vo, w_new, sem):
     layers, rows, cols = w.shape
     late = layers - DIRECT
-    rate = rate_ref[...]
-    pairs = ((r, ro), (c, co), (v, vo), (n_new, no))
-    for i in range(3):
-        pltpu.make_async_copy(*pairs[i], sem.at[i]).start()
-    n_new[...] = n[...] - rate * dn[...]
-    for l in range(layers + 1):
-        if l < late:
-            w_new[l] = w[l] - rate * d[l]
-        elif l < layers:
-            scale, clip, a = factors(sums[l - late], r_pad[l:l + 1], rows, zs, rows * ds, cols * zs)
-            b = lax.rsqrt(c[l:l + 1]) / clip
-            for t in range(cols // LANES):
-                sl = slice(t * LANES, (t + 1) * LANES)
-                w_new[l, :, sl] = w[l, :, sl] - rate * (d[l, :, sl] * a * b[:, sl] * scale)
-        if l == 1:
-            pltpu.make_async_copy(*pairs[3], sem.at[3]).start()
-        if l >= 1:
-            pltpu.make_async_copy(w_new.at[l - 1], wo.at[l - 1], sem.at[4]).start()
+    pairs = ((w.at[0:late], wo.at[0:late]), (r, ro), (c, co), (v, vo), (n, no))
+    for i, pair in enumerate(pairs):
+        pltpu.make_async_copy(*pair, sem.at[i]).start()
+    for e in range(DIRECT):
+        l = late + e
+        lane = 3 * (DIRECT - 1 - e)
+        scale, clip, a = factors(sums[:, lane:lane + 3], r_pad[l:l + 1], rate_ref[...], rows, zs, rows * ds, cols * zs)
+        b = lax.rsqrt(c[l:l + 1]) / clip
+        for t in range(cols // LANES):
+            sl = slice(t * LANES, (t + 1) * LANES)
+            w_new[e, :, sl] = w[l, :, sl] - scale * (d[l, :, sl] * a * b[:, sl])
+    for e in range(DIRECT):
+        pltpu.make_async_copy(w_new.at[e], wo.at[late + e], sem.at[5]).start()
     for i, pair in enumerate(pairs):
         pltpu.make_async_copy(*pair, sem.at[i]).wait()
-    pltpu.make_async_copy(w_new, wo, sem.at[4]).wait()
-
-
-def write_out(ds, zs, rate, w, d, r, c, n, dn, v, r_pad, sums):
+    pltpu.make_async_copy(w_new, wo.at[late:layers], sem.at[5]).wait()
+
+
+def write_out(ds, zs, rate, w, d, r, c, n, v, r_pad, sums):
     return pl.pallas_call(
         functools.partial(write_kernel, ds, zs),
         out_shape=[jax.ShapeDtypeStruct(a.shape, a.dtype) for a in (w, r, c, n, v)],
-        in_specs=[pl.BlockSpec(memory_space=pltpu.MemorySpace.SMEM)] + [pl.BlockSpec(memory_space=pltpu.MemorySpace.VMEM)] * 9,
+        in_specs=[pl.BlockSpec(memory_space=pltpu.MemorySpace.SMEM)] + [pl.BlockSpec(memory_space=pltpu.MemorySpace.VMEM)] * 8,
         out_specs=[pl.BlockSpec(memory_space=pltpu.MemorySpace.HBM)] * 5,
-        scratch_shapes=[pltpu.VMEM(w.shape, w.dtype), pltpu.VMEM(n.shape, n.dtype), pltpu.SemaphoreType.DMA((5,))],
-        compiler_params=pltpu.CompilerParams(vmem_limit_bytes=8 << 20),
+        scratch_shapes=[pltpu.VMEM((DIRECT,) + w.shape[1:], w.dtype), pltpu.SemaphoreType.DMA((6,))],
+        compiler_params=pltpu.CompilerParams(vmem_limit_bytes=4 << 20),
         name='write_out',
-    )(rate, w, d, r, c, n, dn, v, r_pad, sums)
+    )(rate, w, d, r, c, n, v, r_pad, sums)
 
 
 def solution(mesh):
@@ -474,10 +465,10 @@
         dma = pltpu.SemaphoreType.DMA
         outs = pl.pallas_call(
             step_kernel,
-            out_shape=[pltpu.VMEM(a.shape, f32) for a in (weight, weight, row_stat, col_stat, norm_scale, norm_scale, norm_stat)]
-            + [pltpu.VMEM((layers, LANES), f32), pltpu.VMEM((DIRECT, 1, LANES), f32)],
-            in_specs=[any_spec] * 7,
-            out_specs=[pl.BlockSpec(memory_space=pltpu.MemorySpace.VMEM)] * 9,
+            out_shape=[pltpu.VMEM(a.shape, f32) for a in (weight, weight, row_stat, col_stat, norm_scale, norm_stat)]
+            + [pltpu.VMEM((layers, LANES), f32), pltpu.VMEM((1, LANES), f32)],
+            in_specs=[any_spec] * 7 + [pl.BlockSpec(memory_space=pltpu.MemorySpace.SMEM)],
+            out_specs=[pl.BlockSpec(memory_space=pltpu.MemorySpace.VMEM)] * 8,
             scratch_shapes=[
                 pltpu.VMEM((layers, 3, rows, cols), f32),
                 pltpu.VMEM((layers, 4, rows, cols), f32),
@@ -492,20 +483,20 @@
                 pltpu.VMEM((layers, 1, cols // 2), f32),
                 pltpu.VMEM((layers, ds // 2, 1, cols // 2), f32),
                 pltpu.VMEM((layers, 2, 1, cols // 2), f32),
-                pltpu.VMEM((DIRECT, ds, 1, cols), f32),
+                pltpu.VMEM((ds, 1, cols), f32),
                 pltpu.VMEM((layers, 2 * zs, 1, LANES), f32),
                 pltpu.VMEM((layers, ds // 2, 1, LANES), f32),
-                pltpu.VMEM((DIRECT, ds * zs, 1, LANES), f32),
-                pltpu.VMEM((ds // 2, 2, layers, LANES), f32),
-                pltpu.VMEM((ds // 2, layers, LANES), f32),
-                pltpu.VMEM((ds // 2, layers, LANES), f32),
+                pltpu.VMEM((ds * zs, 1, LANES), f32),
+                pltpu.VMEM((1, LANES), f32),
+                pltpu.VMEM((ds, layers, LANES), f32),
+                pltpu.VMEM((ds, layers, LANES), f32),
                 pltpu.VMEM((ds, 1, 2 * LANES), f32),
-                *[dma((n,)) for n in (3, 3, 4, 3, 3, 3, 4, 4, 4, 2, 2, 2, 4, 2, 4, 3, 6, 2, 4, 2)],
+                *[dma((n,)) for n in (3, 3, 5, 3, 3, 3, 4, 4, 4, 2, 2, 2, 4, 2, 4, 3, 6, 2, 4, 2)],
                 *[dma((DIRECT,))] * 4,
             ],
             compiler_params=pltpu.CompilerParams(collective_id=0, has_side_effects=True, vmem_limit_bytes=50 * 1000 * 1000),
             name='adafactor_step',
-        )(weight, grads, row_stat, col_stat, norm_scale, norm_grads, norm_stat)
+        )(weight, grads, row_stat, col_stat, norm_scale, norm_grads, norm_stat, learn_rate)
         return write_out(ds, zs, learn_rate, *outs)
 
     mat_spec = P(None, 'dp', 'model')

time: 176 us -> 179 us (1.017)
  Pallas kernels: 175 us -> 178 us
    pallas_call x1, Pallas kernels: 173 us -> 176 us  [local_step(): pl.pallas_call(step_kernel, out_shape=[pltpu.VMEM(a.shape, f32) for a in...]
where the time goes in v10:
time: 179 us
  Pallas kernels  178 us (99%)
    pallas_call x1, Pallas kernels, local_step(): pl.pallas_call(step_kernel, out_shape=[pltpu.VMEM(a.shape, f32) for a in...  176 us

profile of v10, /device:TPU:0, one launch (start us, length us, event | category | flops | bytes accessed | tf_op | source)
XLA Modules:
  0.0 179.1 jit_solution(281342471589423059)
XLA Ops:
  1.3 175.6 %adafactor_step.1 = (f32[16,96,768]{2,1,0:T(8,128)S(1)}, f32[16,96,768]{2,1,0:T(8,128)S(1)}, f32[16,96]{1,0:T(8,128)S(1)}, f32[16,768]{1,0:T(8,128)S(1)}, f32[16...) custom-call(f32[16,96,768]{2,1,0:T(8,128)} %w_hbm.1, ...), custom_call_target="tpu_custom_call" | custom-call | tf_op jit(solution)/shard_map/adafactor_step/pallas_call | solution.py:466
  176.9 2.2 %write_out.1 = (f32[16,96,768]{2,1,0:T(8,128)}, f32[16,96]{1,0:T(8,128)}, f32[16,768]{1,0:T(8,128)}, f32[16,96]{1,0:T(8,128)}, f32[16,96]{1,0:T(8,128)}) custom-call(f32[]{:T(128)S(6)} %copy.13.rate_ref, f32[16,96,768]{2,1,0:T(8,128)S(1)} %get-tuple-element.13.w, f32[16,96,768]{2,1,0:T(8,128)S(1)} %get-tuple-element.14.d, f32[16,96]{1,0:T(8,128)S(1)} %get-tuple-element.15.r, ...), custom_call_target="tpu_custom_call" | custom-call | tf_op jit(solution)/shard_map/write_out/pallas_call | solution.py:444

commit v11 on v10

--- a/solution.py
+++ b/solution.py
@@ -36,7 +36,7 @@
 def step_kernel(w_hbm, g_hbm, r_hbm, c_hbm, n_hbm, ng_hbm, v_hbm, rate_ref,
                 w_buf, d_buf, r_buf, c_buf, n_buf, v_buf, r_pad, sums_out,
                 own, peer, in1x, in1y, in2, early, ng_buf, w_sq,
-                r_all, c_mine, c_pair, c_all, c_full, c_last, s_all, t_all, t_last, held, h_out, h_all, k_all,
+                r_all, c_mine, c_pair, c_all, c_full, c_last, s_all, t_all, t_last, held, h_out, h_pair, h_all, k_all,
                 load_sem, pair_send, pair_recv, one_send, one_recv, two_send, two_recv,
                 r_send, r_recv, cp_send, cp_recv, c_send, c_recv, cf_send, cf_recv,
                 s_send, s_recv, t_send, t_recv, w_sem,
@@ -148,27 +148,31 @@
         load_own(l)
 
     def norm_split():
-        for i in (0, 1, 2, 4):
-            pltpu.make_async_copy(*small[i], small_sems[i]).wait()
+        for (src, dst), sem in zip(small, small_sems):
+            pltpu.make_async_copy(src, dst, sem).wait()
         r_pad[...] = jnp.zeros_like(r_pad)
         r_pad[:, 0:rows] = r_buf[...]
+        h_out[...] = jnp.zeros_like(h_out)
         k_all[...] = jnp.zeros_like(k_all)
-
-    h_out[...] = jnp.zeros_like(h_out)
-    pltpu.make_async_copy(*small[3], small_sems[3]).wait()
-    for k in range(ds):
-        h_out[k, :, 0:rows] = ng_buf[:, k * rows:(k + 1) * rows]
-    h_all[d] = h_out[d]
-    for where in d_peers:
-        remote(h_out.at[where['dp']], h_all.at[d], cl_send.at[1], cl_recv.at[1], where).start()
+        for k in range(ds):
+            h_out[k // 2, k % 2, :, 0:rows] = ng_buf[:, k * rows:(k + 1) * rows]
+        remote(h_out.at[:, 1 - core], h_pair, cl_send.at[0], cl_recv.at[0], {'dp': dc}).start()
+
+    def norm_send():
+        remote(h_out.at[:, 1 - core], h_pair, cl_send.at[0], cl_recv.at[0], {'dp': dc}).wait()
+        for k in range(chips):
+            h_pair[k] = h_pair[k] + h_out[k, core]
+        h_all[chip] = h_pair[chip]
+        for e in (dx, dy, dxy):
+            remote(h_pair.at[lax.div(e, 2)], h_all.at[chip], cl_send.at[1], cl_recv.at[1], {'dp': e}).start()
 
     def layer_sums(values):
         padded = jnp.concatenate([values, jnp.zeros((layers, LANES - rows), jnp.float32)], axis=1)
         return jnp.sum(jnp.transpose(padded), axis=0, keepdims=True)
 
     def norm_stats():
-        drain(h_all.at[0:ds - 1], cl_recv.at[1])
-        drain(h_all.at[0:ds - 1], cl_send.at[1])
+        drain(h_all.at[0:chips - 1], cl_recv.at[1])
+        drain(h_all.at[0:chips - 1], cl_send.at[1])
         h = total(h_all)[:, 0:rows]
         v_new = DECAY * v_buf[...] + (1.0 - DECAY) * (h * h + EPS_FLOOR)
         v_buf[...] = v_new
@@ -402,6 +406,7 @@
         at(i, 1, stage_forward, 1)
         once(i, 1, forward_first)
         once(i, 1, norm_split)
+        once(i, 2, norm_send)
         at(i, 3, stage_columns, 0, last)
         at(i, 4, stage_share, 0, last)
         at(i, 5, stage_moments)
@@ -488,8 +493,9 @@
                 pltpu.VMEM((layers, ds // 2, 1, LANES), f32),
                 pltpu.VMEM((ds * zs, 1, LANES), f32),
                 pltpu.VMEM((1, LANES), f32),
-                pltpu.VMEM((ds, layers, LANES), f32),
-                pltpu.VMEM((ds, layers, LANES), f32),
+                pltpu.VMEM((ds // 2, 2, layers, LANES), f32),
+                pltpu.VMEM((ds // 2, layers, LANES), f32),
+                pltpu.VMEM((ds // 2, layers, LANES), f32),
                 pltpu.VMEM((ds, 1, 2 * LANES), f32),
                 *[dma((n,)) for n in (3, 3, 5, 3, 3, 3, 4, 4, 4, 2, 2, 2, 4, 2, 4, 3, 6, 2, 4, 2)],
                 *[dma((DIRECT,))] * 4,

time: 179 us -> 180 us (level)
  no operation moved by 1% of the time
where the time goes in v11:
time: 180 us
  Pallas kernels  178 us (99%)
    pallas_call x1, Pallas kernels, local_step(): pl.pallas_call(step_kernel, out_shape=[pltpu.VMEM(a.shape, f32) for a in...  176 us

profile of v11, /device:TPU:0, one launch (start us, length us, event | category | flops | bytes accessed | tf_op | source)
XLA Modules:
  0.0 179.5 jit_solution(10732159951755236836)
XLA Ops:
  1.3 176.0 %adafactor_step.1 = (f32[16,96,768]{2,1,0:T(8,128)S(1)}, f32[16,96,768]{2,1,0:T(8,128)S(1)}, f32[16,96]{1,0:T(8,128)S(1)}, f32[16,768]{1,0:T(8,128)S(1)}, f32[16...) custom-call(f32[16,96,768]{2,1,0:T(8,128)} %w_hbm.1, ...), custom_call_target="tpu_custom_call" | custom-call | tf_op jit(solution)/shard_map/adafactor_step/pallas_call | solution.py:471
  177.3 2.2 %write_out.1 = (f32[16,96,768]{2,1,0:T(8,128)}, f32[16,96]{1,0:T(8,128)}, f32[16,768]{1,0:T(8,128)}, f32[16,96]{1,0:T(8,128)}, f32[16,96]{1,0:T(8,128)}) custom-call(f32[]{:T(128)S(6)} %copy.13.rate_ref, f32[16,96,768]{2,1,0:T(8,128)S(1)} %get-tuple-element.13.w, f32[16,96,768]{2,1,0:T(8,128)S(1)} %get-tuple-element.14.d, f32[16,96]{1,0:T(8,128)S(1)} %get-tuple-element.15.r, ...), custom_call_target="tpu_custom_call" | custom-call | tf_op jit(solution)/shard_map/write_out/pallas_call | solution.py:449

commit v12 on v10

--- a/solution.py
+++ b/solution.py
@@ -297,7 +297,6 @@
 
     def stage_columns(l):
         pair_columns(l).wait()
-        drain_rows(l)
         c_all[l, chip] = c_mine[l, core] + c_pair[l]
         spread(c_all.at[l, chip], ring(c_send, l), ring(c_recv, l), plane_peers)
 
@@ -306,6 +305,7 @@
         drain(c_all.at[l, 0:chips - 1], ring(c_send, l))
         c_full[l, core] = total(c_all.at[l])
         full_columns(l).start()
+        drain_rows(l)
 
     def stage_moments(l):
         @pl.when(l < last)
@@ -491,7 +491,7 @@
                 pltpu.VMEM((ds, layers, LANES), f32),
                 pltpu.VMEM((ds, layers, LANES), f32),
                 pltpu.VMEM((ds, 1, 2 * LANES), f32),
-                *[dma((n,)) for n in (3, 3, 5, 3, 3, 3, 4, 4, 4, 2, 2, 2, 4, 2, 4, 3, 6, 2, 4, 2)],
+                *[dma((n,)) for n in (3, 3, 5, 3, 3, 3, 4, 4, 5, 2, 2, 2, 4, 2, 4, 3, 6, 2, 4, 2)],
                 *[dma((DIRECT,))] * 4,
             ],
             compiler_params=pltpu.CompilerParams(collective_id=0, has_side_effects=True, vmem_limit_bytes=50 * 1000 * 1000),

time: 179 us -> 177 us (0.989)
  Pallas kernels: 178 us -> 175 us
    pallas_call x1, Pallas kernels: 176 us -> 173 us  [local_step(): pl.pallas_call(step_kernel, out_shape=[pltpu.VMEM(a.shape, f32) for a in...]
where the time goes in v12:
time: 177 us
  Pallas kernels  175 us (99%)
    pallas_call x1, Pallas kernels, local_step(): pl.pallas_call(step_kernel, out_shape=[pltpu.VMEM(a.shape, f32) for a in...  173 us

profile of v12, /device:TPU:0, one launch (start us, length us, event | category | flops | bytes accessed | tf_op | source)
XLA Modules:
  0.0 176.6 jit_solution(1870833959739768858)
XLA Ops:
  1.3 173.1 %adafactor_step.1 = (f32[16,96,768]{2,1,0:T(8,128)S(1)}, f32[16,96,768]{2,1,0:T(8,128)S(1)}, f32[16,96]{1,0:T(8,128)S(1)}, f32[16,768]{1,0:T(8,128)S(1)}, f32[16...) custom-call(f32[16,96,768]{2,1,0:T(8,128)} %w_hbm.1, ...), custom_call_target="tpu_custom_call" | custom-call | tf_op jit(solution)/shard_map/adafactor_step/pallas_call | solution.py:466
  174.4 2.2 %write_out.1 = (f32[16,96,768]{2,1,0:T(8,128)}, f32[16,96]{1,0:T(8,128)}, f32[16,768]{1,0:T(8,128)}, f32[16,96]{1,0:T(8,128)}, f32[16,96]{1,0:T(8,128)}) custom-call(f32[]{:T(128)S(6)} %copy.13.rate_ref, f32[16,96,768]{2,1,0:T(8,128)S(1)} %get-tuple-element.13.w, f32[16,96,768]{2,1,0:T(8,128)S(1)} %get-tuple-element.14.d, f32[16,96]{1,0:T(8,128)S(1)} %get-tuple-element.15.r, ...), custom_call_target="tpu_custom_call" | custom-call | tf_op jit(solution)/shard_map/write_out/pallas_call | solution.py:444

commit v13 on v12

--- a/solution.py
+++ b/solution.py
@@ -16,7 +16,7 @@
 MESH = pl.DeviceIdType.MESH
 LANES = 128
 AHEAD = 2
-DIRECT = 2
+DIRECT = 3
 EARLY = 8
 
 
@@ -335,7 +335,7 @@
             u = d_buf[l, :, sl] * a * b[:, sl]
             acc = acc + jnp.sum(u * u, axis=0, keepdims=True)
         lane = lax.broadcasted_iota(jnp.int32, (1, LANES), 1)
-        lane = lane - jnp.where(l == late, 3, 0)
+        lane = lane - jnp.where(l >= late, 3 * (last - l), 0)
         row = jnp.where(lane == 0, jnp.sum(acc, axis=1, keepdims=True), 0.0)
         row = jnp.where(lane == 1, jnp.sum(w_sq[pl.ds(l, 1)], axis=1, keepdims=True), row)
         row = jnp.where(lane == 2, jnp.sum(r_new, axis=1, keepdims=True), row)
@@ -348,6 +348,10 @@
         @pl.when(l == late)
         def _():
             held[...] = row
+
+        @pl.when((l > late) & (l < last))
+        def _():
+            held[...] = held[...] + row
 
         @pl.when(l == last)
         def _():
@@ -492,7 +496,7 @@
                 pltpu.VMEM((ds, layers, LANES), f32),
                 pltpu.VMEM((ds, 1, 2 * LANES), f32),
                 *[dma((n,)) for n in (3, 3, 5, 3, 3, 3, 4, 4, 5, 2, 2, 2, 4, 2, 4, 3, 6, 2, 4, 2)],
-                *[dma((DIRECT,))] * 4,
+                *[dma((2,))] * 4,
             ],
             compiler_params=pltpu.CompilerParams(collective_id=0, has_side_effects=True, vmem_limit_bytes=50 * 1000 * 1000),
             name='adafactor_step',

time: 177 us -> 177 us (level)
  no operation moved by 1% of the time
where the time goes in v13:
time: 177 us
  Pallas kernels  175 us (99%)
    pallas_call x1, Pallas kernels, local_step(): pl.pallas_call(step_kernel, out_shape=[pltpu.VMEM(a.shape, f32) for a in...  173 us

profile of v13, /device:TPU:0, one launch (start us, length us, event | category | flops | bytes accessed | tf_op | source)
XLA Modules:
  0.0 176.6 jit_solution(961437400745294453)
XLA Ops:
  1.3 173.1 %adafactor_step.1 = (f32[16,96,768]{2,1,0:T(8,128)S(1)}, f32[16,96,768]{2,1,0:T(8,128)S(1)}, f32[16,96]{1,0:T(8,128)S(1)}, f32[16,768]{1,0:T(8,128)S(1)}, f32[16...) custom-call(f32[16,96,768]{2,1,0:T(8,128)} %w_hbm.1, ...), custom_call_target="tpu_custom_call" | custom-call | tf_op jit(solution)/shard_map/adafactor_step/pallas_call | solution.py:470
  174.4 2.2 %write_out.1 = (f32[16,96,768]{2,1,0:T(8,128)}, f32[16,96]{1,0:T(8,128)}, f32[16,768]{1,0:T(8,128)}, f32[16,96]{1,0:T(8,128)}, f32[16,96]{1,0:T(8,128)}) custom-call(f32[]{:T(128)S(6)} %copy.13.rate_ref, f32[16,96,768]{2,1,0:T(8,128)S(1)} %get-tuple-element.13.w, f32[16,96,768]{2,1,0:T(8,128)S(1)} %get-tuple-element.14.d, f32[16,96]{1,0:T(8,128)S(1)} %get-tuple-element.15.r, ...), custom_call_target="tpu_custom_call" | custom-call | tf_op jit(solution)/shard_map/write_out/pallas_call | solution.py:448

commit v14 on v13

--- a/solution.py
+++ b/solution.py
@@ -43,7 +43,8 @@
                 cl_send, cl_recv, tl_send, tl_recv):
     layers, _, rows, cols = own.shape
     half = rows // 2
-    last, ds = layers - 1, c_last.shape[0]
+    last, ds = layers - 1, c_last.shape[1]
+    near_end = layers - c_last.shape[0]
     late = layers - DIRECT
     zs = r_all.shape[1]
     chips = ds // 2
@@ -262,25 +263,26 @@
         q = g * g + EPS_FLOOR
         col = jnp.sum(q, axis=0, keepdims=True)
 
-        @pl.when(l < last)
+        @pl.when(l < near_end)
         def _():
             c_mine[l, 0] = col[:, 0:cols // 2]
             c_mine[l, 1] = col[:, cols // 2:cols]
 
-        @pl.when(l == last)
-        def _():
-            c_last[d] = col
+        @pl.when(l >= near_end)
+        def _():
+            c_last[l - near_end, d] = col
 
         p = jnp.concatenate([fold(q), jnp.zeros((LANES - rows, LANES), jnp.float32)], axis=0)
         r_all[l, z] = jnp.sum(jnp.transpose(p), axis=0, keepdims=True)
 
-        @pl.when(l < last)
+        @pl.when(l < near_end)
         def _():
             pair_columns(l).start()
 
-        @pl.when(l == last)
-        def _():
-            spread(c_last.at[d], cl_send.at[0], cl_recv.at[0], d_peers)
+        @pl.when(l >= near_end)
+        def _():
+            e = l - near_end
+            spread(c_last.at[e, d], cl_send.at[e], cl_recv.at[e], d_peers)
 
         spread(r_all.at[l, z], ring(r_send, l), ring(r_recv, l), z_peers)
 
@@ -308,16 +310,17 @@
         drain_rows(l)
 
     def stage_moments(l):
-        @pl.when(l < last)
+        @pl.when(l < near_end)
         def _():
             full_columns(l).wait()
 
-        @pl.when(l == last)
-        def _():
-            drain(c_last.at[0:ds - 1], cl_recv.at[0])
-            drain(c_last.at[0:ds - 1], cl_send.at[0])
+        @pl.when(l >= near_end)
+        def _():
+            e = l - near_end
+            drain(c_last.at[e, 0:ds - 1], cl_recv.at[e])
+            drain(c_last.at[e, 0:ds - 1], cl_send.at[e])
             drain_rows(l)
-            col = total(c_last)
+            col = total(c_last.at[e])
             c_full[l, 0] = col[:, 0:cols // 2]
             c_full[l, 1] = col[:, cols // 2:cols]
 
@@ -406,8 +409,8 @@
         at(i, 1, stage_forward, 1)
         once(i, 1, forward_first)
         once(i, 1, norm_split)
-        at(i, 3, stage_columns, 0, last)
-        at(i, 4, stage_share, 0, last)
+        at(i, 3, stage_columns, 0, near_end)
+        at(i, 4, stage_share, 0, near_end)
         at(i, 5, stage_moments)
         at(i, 7, stage_gather, 0, late)
         at(i, 8, stage_update, 0, late)
@@ -487,7 +490,7 @@
                 pltpu.VMEM((layers, 1, cols // 2), f32),
                 pltpu.VMEM((layers, ds // 2, 1, cols // 2), f32),
                 pltpu.VMEM((layers, 2, 1, cols // 2), f32),
-                pltpu.VMEM((ds, 1, cols), f32),
+                pltpu.VMEM((2, ds, 1, cols), f32),
                 pltpu.VMEM((layers, 2 * zs, 1, LANES), f32),
                 pltpu.VMEM((layers, ds // 2, 1, LANES), f32),
                 pltpu.VMEM((ds * zs, 1, LANES), f32),

time: 177 us -> 176 us (level)
  no operation moved by 1% of the time
where the time goes in v14:
time: 176 us
  Pallas kernels  175 us (99%)
    pallas_call x1, Pallas kernels, local_step(): pl.pallas_call(step_kernel, out_shape=[pltpu.VMEM(a.shape, f32) for a in...  173 us

profile of v14, /device:TPU:0, one launch (start us, length us, event | category | flops | bytes accessed | tf_op | source)
XLA Modules:
  0.0 176.1 jit_solution(18385459463389750791)
XLA Ops:
  1.3 172.6 %adafactor_step.1 = (f32[16,96,768]{2,1,0:T(8,128)S(1)}, f32[16,96,768]{2,1,0:T(8,128)S(1)}, f32[16,96]{1,0:T(8,128)S(1)}, f32[16,768]{1,0:T(8,128)S(1)}, f32[16...) custom-call(f32[16,96,768]{2,1,0:T(8,128)} %w_hbm.1, ...), custom_call_target="tpu_custom_call" | custom-call | tf_op jit(solution)/shard_map/adafactor_step/pallas_call | solution.py:473
  173.8 2.2 %write_out.1 = (f32[16,96,768]{2,1,0:T(8,128)}, f32[16,96]{1,0:T(8,128)}, f32[16,768]{1,0:T(8,128)}, f32[16,96]{1,0:T(8,128)}, f32[16,96]{1,0:T(8,128)}) custom-call(f32[]{:T(128)S(6)} %copy.13.rate_ref, f32[16,96,768]{2,1,0:T(8,128)S(1)} %get-tuple-element.13.w, f32[16,96,768]{2,1,0:T(8,128)S(1)} %get-tuple-element.14.d, f32[16,96]{1,0:T(8,128)S(1)} %get-tuple-element.15.r, ...), custom_call_target="tpu_custom_call" | custom-call | tf_op jit(solution)/shard_map/write_out/pallas_call | solution.py:451

commit v15 on v14

--- a/solution.py
+++ b/solution.py
@@ -61,7 +61,12 @@
     d_peers = [{'dp': e} for e in (dc, dx, dx + dc - d, dy, dy + dc - d, dxy, dxy + dc - d)]
     column_peers = [{'dp': dc}] + [{'model': p['model'], 'dp': e} for p in z_peers for e in (d, dc)]
     plane_peers = [{'dp': e} for e in (dx, dy, dxy)]
-    others = [{'model': p['model'], **q} for q in d_peers[::-1] for p in z_peers] + d_peers[::-1] + z_peers
+    me = ds * z + d
+
+    def everyone_else():
+        for j in range(ds * zs - 1):
+            e = j + jnp.where(me <= j, 1, 0)
+            yield {'model': lax.div(e, ds), 'dp': lax.rem(e, ds)}
 
     def ring(sem, l):
         return sem.at[lax.rem(l, sem.shape[0])]
@@ -358,9 +363,8 @@
 
         @pl.when(l == last)
         def _():
-            me = ds * z + d
             t_last[me] = row + held[...]
-            spread(t_last.at[me], tl_send.at[0], tl_recv.at[0], others)
+            spread(t_last.at[me], tl_send.at[0], tl_recv.at[0], everyone_else())
 
     def stage_gather(l):
         drain(s_all.at[l, 0:2 * zs - 1], ring(s_recv, l))

time: 176 us -> 176 us (level)
  no operation moved by 1% of the time
where the time goes in v15:
time: 176 us
  Pallas kernels  175 us (99%)
    pallas_call x1, Pallas kernels, local_step(): pl.pallas_call(step_kernel, out_shape=[pltpu.VMEM(a.shape, f32) for a in...  173 us

profile of v15, /device:TPU:0, one launch (start us, length us, event | category | flops | bytes accessed | tf_op | source)
XLA Modules:
  0.0 176.0 jit_solution(9515008760420164559)
XLA Ops:
  1.3 172.5 %adafactor_step.1 = (f32[16,96,768]{2,1,0:T(8,128)S(1)}, f32[16,96,768]{2,1,0:T(8,128)S(1)}, f32[16,96]{1,0:T(8,128)S(1)}, f32[16,768]{1,0:T(8,128)S(1)}, f32[16...) custom-call(f32[16,96,768]{2,1,0:T(8,128)} %w_hbm.1, ...), custom_call_target="tpu_custom_call" | custom-call | tf_op jit(solution)/shard_map/adafactor_step/pallas_call | solution.py:477
  173.8 2.2 %write_out.1 = (f32[16,96,768]{2,1,0:T(8,128)}, f32[16,96]{1,0:T(8,128)}, f32[16,768]{1,0:T(8,128)}, f32[16,96]{1,0:T(8,128)}, f32[16,96]{1,0:T(8,128)}) custom-call(f32[]{:T(128)S(6)} %copy.13.rate_ref, f32[16,96,768]{2,1,0:T(8,128)S(1)} %get-tuple-element.13.w, f32[16,96,768]{2,1,0:T(8,128)S(1)} %get-tuple-element.14.d, f32[16,96]{1,0:T(8,128)S(1)} %get-tuple-element.15.r, ...), custom_call_target="tpu_custom_call" | custom-call | tf_op jit(solution)/shard_map/write_out/pallas_call | solution.py:455
